TPU v7x, 32 devices: a whole 2x2x4 slice. The times are simulated.
32 devices in a mesh: band: 8 (over z, y), grid: 4 (over x, core).
Axes of the slice: x: 2, y: 2, z: 4, core: 2. Of those that a mesh axis runs over, the one named last changes fastest.
Arguments:
- bands: float32 [8, 96, 96, 96], P('band', 'grid'), may hold values from -8 to 8
Outputs:
- exchange_term: float32 [8, 96, 96, 96], P('band', 'grid')
All inputs are finite; a program needn't handle non-finite values.
Results may differ from a plain program's by a relative error of at most 0.0003.
Values sent between devices are 32-bit elements; how exact they have to be, the bound alone decides.
No kernel may reach another device: no remote copies, remote signals or barrier semaphores. Data moves between devices by JAX's collectives and lax.ppermute only.
A program may use at most 64 MiB of HBM per device.

v0:
```python
import jax
import jax.numpy as jnp
import numpy as np
from jax import lax
from jax.sharding import PartitionSpec as P

CYCLE = 2


EXACT = lax.Precision.HIGHEST


def from_behind(shard, axis, by):
    length = lax.axis_size(axis)
    return lax.ppermute(shard, axis, [(i, (i + by) % length) for i in range(length)])


def hartley(length):
    indices = jnp.arange(length, dtype=jnp.int32)
    phases = indices[:, None] * indices[None, :] % length
    angles = phases.astype(jnp.float32) * (2.0 * np.pi / length)
    return jnp.cos(angles) + jnp.sin(angles)


def wavenumber_sq(indices, length):
    folded = jnp.minimum(indices, length - indices).astype(jnp.float32)
    return folded * (2.0 * np.pi / length) * (folded * (2.0 * np.pi / length))


def coulomb(wave_sq, extent):
    screen = 4.0 * np.pi / extent
    guarded = jnp.where(wave_sq > 0, wave_sq, 1.0)
    screened = 0.2 * 4.0 * np.pi / guarded * (1.0 - jnp.exp(-guarded / (4.0 * screen * screen)))
    return jnp.where(wave_sq > 0, screened, 0.0)


def solve(density):
    planes, height, breadth = (density.shape[1], density.shape[2], density.shape[3])
    parts_grid = lax.axis_size("grid")
    planes_all = planes * parts_grid
    share_y = height // parts_grid
    offset_y = lax.axis_index("grid") * share_y
    table_z = hartley(breadth)
    table_y = hartley(height)
    table_x = hartley(planes_all)
    wave_sq = (
        wavenumber_sq(jnp.arange(planes_all, dtype=jnp.int32), planes_all)[:, None, None]
        + wavenumber_sq(offset_y + jnp.arange(share_y, dtype=jnp.int32), height)[None, :, None]
        + wavenumber_sq(jnp.arange(breadth, dtype=jnp.int32), breadth)[None, None, :]
    )
    kernel = coulomb(wave_sq, planes_all)
    spectrum = jnp.einsum("pxyz,zw->pxyw", density, table_z, precision=EXACT)
    spectrum = jnp.einsum("pxyz,yw->pxwz", spectrum, table_y, precision=EXACT)
    screened = (
        jnp.einsum(
            "xa,pxyz->payz",
            table_x,
            lax.all_to_all(spectrum, "grid", split_axis=2, concat_axis=1, tiled=True),
            precision=EXACT,
        )
        * kernel[None]
    )
    restored = jnp.einsum("xa,pxyz->payz", table_x, screened, precision=EXACT)
    spectrum = lax.all_to_all(restored, "grid", split_axis=1, concat_axis=2, tiled=True)
    spectrum = jnp.einsum("pxyz,yw->pxwz", spectrum, table_y, precision=EXACT)
    spectrum = jnp.einsum("pxyz,zw->pxyw", spectrum, table_z, precision=EXACT)
    return spectrum * (1.0 / (planes_all * height * breadth))


def collect(terms, picker):
    return jnp.einsum("pxyz,pi->ixyz", terms, picker, precision=EXACT)


def cross_pairs(orbitals, visitors):
    number = orbitals.shape[0]
    guests = visitors.shape[0]
    density = (orbitals[:, None] * visitors[None, :]).reshape(
        (number * guests,) + orbitals.shape[1:]
    )
    potential = solve(density).reshape((number, guests) + orbitals.shape[1:])
    return (
        jnp.sum(potential * visitors[None], axis=1),
        jnp.sum(potential * orbitals[:, None], axis=0),
    )


def shards(bands):
    number = bands.shape[0]
    leading, trailing = np.triu_indices(number)
    columns_id = np.arange(number)[None, :]
    pick_first = jnp.asarray((leading[:, None] == columns_id).astype(np.float32))
    pick_second = jnp.asarray(
        ((trailing[:, None] == columns_id) & (leading != trailing)[:, None]).astype(np.float32)
    )
    potential = solve(bands[leading] * bands[trailing])
    summed = collect(potential * bands[trailing], pick_first) + collect(
        potential * bands[leading], pick_second
    )
    visitor = bands
    for offset in range(1, CYCLE + 1):
        visitor = from_behind(visitor, "band", 1)
        nearby, remote = cross_pairs(bands, visitor)
        summed = summed + nearby + from_behind(remote, "band", -offset)
    return -summed


def solution(mesh):
    return jax.shard_map(
        shards,
        mesh=mesh,
        in_specs=(P("band", "grid", None, None),),
        out_specs=P("band", "grid", None, None),
        check_vma=False,
    )
```

profile of v0, /device:TPU:0, one launch (start us, length us, event | category | flops | bytes accessed | tf_op | source)
XLA Modules:
  0.0 192.5 jit_solution(3368642876577580224)
XLA Ops:
  0.0 3.0 %collective-permute-start = (f32[1,24,96,96]{3,2,1,0:T(8,128)}, f32[1,24,96,96]{3,2,1,0:T(8,128)S(1)}, u32[]{:S(2)}, u32[]{:S(2)}) collective-permute-start(f32[1,24,96,96]{3,2,1,0:T(8,128)} %param.9), channel_id=1, source_target_pairs={{0,4},{4,8},{8,12},{12,16},{16,20},{20,24},{24,28},{28,0},{1,5},{5... | collective-permute-start | bytes 2654216 | tf_op jit(solution)/shard_map/ppermute | solution.py:15
  3.0 2.6 %fusion.23 = f32[24,96,96]{2,1,0:T(8,128)S(1)} fusion(f32[1,24,96,96]{3,2,1,0:T(8,128)} %param.9), kind=kOutput, calls=%fused_computation.43 | convolution fusion | flops 255117312 | bytes 1769472 | tf_op jit(solution)/shard_map/pxyz,zw->pxyw/dot_general | solution.py:52
  5.6 1.3 convolution_bitcast_fusion.11
  6.9 1.7 copy.59
  8.6 4.4 %all-to-all-start = ((f32[1,24,96,96]{3,1,0,2:T(8,128)}), f32[1,24,96,96]{3,1,0,2:T(8,128)}, u32[]{:S(2)}, u32[]{:S(2)}) async-start(f32[1,24,96,96]{3,1,0,2:T(8,128)} %copy.59), calls=%async_computation | async-start | bytes 2359296 | tf_op jit(solution)/shard_map/all_to_all | solution.py:58
  13.1 19.2 %collective-permute-done = f32[1,24,96,96]{3,2,1,0:T(8,128)S(1)} collective-permute-done((f32[1,24,96,96]{3,2,1,0:T(8,128)}, f32[1,24,96,96]{3,2,1,0:T(8,128)S(1)}, u32[]{:S(2)}, u32[]{:S(2)}) %collective-permute-start) | collective-permute-done | bytes 884768 | tf_op jit(solution)/shard_map/ppermute | solution.py:15
  32.2 0.0 collective-permute-start.2
  32.2 0.0 copy-done
  32.2 1.3 fusion.21
  33.5 0.0 copy-done.1
  33.5 1.3 convolution_bitcast_fusion.7
  34.9 1.7 copy.67
  36.6 0.0 all-to-all-done
  36.6 4.3 %all-to-all-start.2 = ((f32[1,24,96,96]{3,1,0,2:T(8,128)}), f32[1,24,96,96]{3,1,0,2:T(8,128)}, u32[]{:S(2)}, u32[]{:S(2)}) async-start(f32[1,24,96,96]{3,1,0,2:T(8,128)} %copy.67), calls=%async_computation.2 | async-start | bytes 2359296 | tf_op jit(solution)/shard_map/all_to_all | solution.py:58
  40.9 0.5 fusion.59
  41.5 20.6 %collective-permute-done.2 = f32[1,24,96,96]{3,2,1,0:T(8,128)S(1)} collective-permute-done((f32[1,24,96,96]{3,2,1,0:T(8,128)S(1)}, f32[1,24,96,96]{3,2,1,0:T(8,128)S(1)}, u32[]{:S(2)}, u32[]{:S(2)}) %collective-permute-start.2) | collective-permute-done | bytes 884768 | tf_op jit(solution)/shard_map/ppermute | solution.py:15
  62.0 1.3 fusion.15
  63.3 0.0 copy-done.3
  63.3 1.3 convolution_bitcast_fusion.3
  64.7 1.7 copy.75
  66.4 0.0 all-to-all-done.2
  66.4 3.7 %all-to-all-start.4 = ((f32[1,24,96,96]{3,1,0,2:T(8,128)}), f32[1,24,96,96]{3,1,0,2:T(8,128)S(1)}, u32[]{:S(2)}, u32[]{:S(2)}) async-start(f32[1,24,96,96]{3,1,0,2:T(8,128)} %copy.75), calls=%async_computation.4 | async-start | bytes 2359296 | tf_op jit(solution)/shard_map/all_to_all | solution.py:58
  70.1 0.0 copy-done.7
  70.1 0.1 broadcast_add_fusion
  70.2 1.5 copy.68
  71.7 0.1 copy.69
  71.8 2.6 %fusion.7 = f32[96,24,96]{0,2,1:T(8,128)S(1)} fusion(f32[96,24,96]{2,1,0:T(8,128)S(1)} %bitcast.192, f32[96]{0:T(128)S(1)} %fusion.56, f32[96,24]{0,1:T(8,128)S(1)} %broadcast_add_fusion), kind=kOutput, calls=%fused_computation.24 | convolution fusion | flops 257107968 | bytes 1779072 | tf_op jit(solution)/shard_map/xa,pxyz->payz/dot_general | solution.py:55
  74.4 1.3 convolution_bitcast_fusion.5
  75.7 1.4 copy.71
  77.1 8.7 %all-to-all-done.4 = f32[1,24,96,96]{3,1,0,2:T(8,128)S(1)} async-done(((f32[1,24,96,96]{3,1,0,2:T(8,128)}), f32[1,24,96,96]{3,1,0,2:T(8,128)S(1)}, u32[]{:S(2)}, u32[]{:S(2)}) %all-to-all-start.4) | async-done | bytes 884768 | tf_op jit(solution)/shard_map/all_to_all | solution.py:58
  85.7 3.5 %all-to-all-start.3 = ((f32[1,96,24,96]{3,2,0,1:T(8,128)}), f32[1,96,24,96]{3,2,0,1:T(8,128)S(1)}, u32[]{:S(2)}, u32[]{:S(2)}) async-start(f32[1,96,24,96]{3,2,0,1:T(8,128)} %copy.71), calls=%async_computation.3 | async-start | bytes 2359296 | tf_op jit(solution)/shard_map/all_to_all | solution.py:64
  89.3 1.5 copy.60
  90.8 1.1 copy.61
  91.9 0.2 copy.76
  92.1 0.1 copy.77
  92.2 2.6 %fusion.9 = f32[96,24,96]{0,2,1:T(8,128)S(1)} fusion(f32[96,24,96]{2,1,0:T(8,128)S(1)} %bitcast.193, f32[96]{0:T(128)S(1)} %fusion.56, f32[96,24]{0,1:T(8,128)S(1)} %broadcast_add_fusion), kind=kOutput, calls=%fused_computation.26 | convolution fusion | flops 257107968 | bytes 1779072 | tf_op jit(solution)/shard_map/xa,pxyz->payz/dot_general | solution.py:55
  94.8 1.3 convolution_bitcast_fusion.1
  96.1 1.4 copy.79
  97.5 7.6 %all-to-all-done.3 = f32[1,96,24,96]{3,2,0,1:T(8,128)S(1)} async-done(((f32[1,96,24,96]{3,2,0,1:T(8,128)}), f32[1,96,24,96]{3,2,0,1:T(8,128)S(1)}, u32[]{:S(2)}, u32[]{:S(2)}) %all-to-all-start.3) | async-done | bytes 884768 | tf_op jit(solution)/shard_map/all_to_all | solution.py:64
  105.1 4.5 %all-to-all-start.5 = ((f32[1,96,24,96]{3,2,0,1:T(8,128)}), f32[1,96,24,96]{3,2,0,1:T(8,128)}, u32[]{:S(2)}, u32[]{:S(2)}) async-start(f32[1,96,24,96]{3,2,0,1:T(8,128)} %copy.79), calls=%async_computation.5 | async-start | bytes 2359296 | tf_op jit(solution)/shard_map/all_to_all | solution.py:64
  109.6 0.0 copy-done.6
  109.6 2.6 %fusion.5 = f32[96,24,96]{0,2,1:T(8,128)S(1)} fusion(f32[96,24,96]{2,1,0:T(8,128)S(1)} %bitcast.191, f32[96]{0:T(128)S(1)} %fusion.56, f32[96,24]{0,1:T(8,128)S(1)} %broadcast_add_fusion), kind=kOutput, calls=%fused_computation.22 | convolution fusion | flops 257107968 | bytes 1779072 | tf_op jit(solution)/shard_map/xa,pxyz->payz/dot_general | solution.py:55
  112.2 1.3 convolution_bitcast_fusion.9
  113.5 1.4 copy.63
  114.9 0.1 copy.72
  115.0 1.3 convolution_bitcast_fusion.4
  116.4 8.9 %all-to-all-done.5 = f32[1,96,24,96]{3,2,0,1:T(8,128)} async-done(((f32[1,96,24,96]{3,2,0,1:T(8,128)}), f32[1,96,24,96]{3,2,0,1:T(8,128)}, u32[]{:S(2)}, u32[]{:S(2)}) %all-to-all-start.5) | async-done | bytes 884768 | tf_op jit(solution)/shard_map/all_to_all | solution.py:64
  125.3 4.3 %all-to-all-start.1 = ((f32[1,96,24,96]{3,2,0,1:T(8,128)}), f32[1,96,24,96]{3,2,0,1:T(8,128)}, u32[]{:S(2)}, u32[]{:S(2)}) async-start(f32[1,96,24,96]{3,2,0,1:T(8,128)} %copy.63), calls=%async_computation.1 | async-start | bytes 2359296 | tf_op jit(solution)/shard_map/all_to_all | solution.py:64
  129.5 1.4 copy.80
  131.0 1.3 convolution_bitcast_fusion
  132.3 1.3 fusion.2
  133.6 3.1 %bitcast_multiply_fusion = (f32[1,24,96,96]{3,2,1,0:T(8,128)}, f32[1,24,96,96]{3,2,1,0:T(8,128)}, f32[24,96,96]{2,1,0:T(8,128)}) fusion(f32[1,24,96,96]{3,2,1,0:T(8,128)S(1)} %copy-done, f32[1,24,96,96]{3,2,1,0:T(8,128)S(1)} %fusion.2, f32[24,96,96]{2,1,0:T(8,128)S(1)} %convolution_bitcast_fusion.4), kind=kOutput, calls=%fused_computation.34 | convolution fusion | flops 255559680 | bytes 5308416 | tf_op jit(solution)/shard_map/pxyz,zw->pxyw/dot_general | solution.py:66
  136.7 0.0 collective-permute-start.1
  136.7 0.0 collective-permute-start.3
  136.7 8.7 %all-to-all-done.1 = f32[1,96,24,96]{3,2,0,1:T(8,128)} async-done(((f32[1,96,24,96]{3,2,0,1:T(8,128)}), f32[1,96,24,96]{3,2,0,1:T(8,128)}, u32[]{:S(2)}, u32[]{:S(2)}) %all-to-all-start.1) | async-done | bytes 884768 | tf_op jit(solution)/shard_map/all_to_all | solution.py:64
  145.4 1.5 copy.64
  146.9 0.0 copy-start.2
  147.0 0.0 copy-start.4
  147.0 1.3 convolution_bitcast_fusion.8
  148.3 16.9 %collective-permute-done.1 = f32[1,24,96,96]{3,2,1,0:T(8,128)S(1)} collective-permute-done((f32[1,24,96,96]{3,2,1,0:T(8,128)}, f32[1,24,96,96]{3,2,1,0:T(8,128)S(1)}, u32[]{:S(2)}, u32[]{:S(2)}) %collective-permute-start.1) | collective-permute-done | bytes 884768 | tf_op jit(solution)/shard_map/ppermute | solution.py:15
  165.3 23.2 %collective-permute-done.3 = f32[1,24,96,96]{3,2,1,0:T(8,128)} collective-permute-done((f32[1,24,96,96]{3,2,1,0:T(8,128)}, f32[1,24,96,96]{3,2,1,0:T(8,128)}, u32[]{:S(2)}, u32[]{:S(2)}) %collective-permute-start.3) | collective-permute-done | bytes 884768 | tf_op jit(solution)/shard_map/ppermute | solution.py:15
  188.4 0.0 copy-done.5
  188.4 0.0 copy-done.2
  188.4 4.0 %fusion.19 = f32[1,24,96,96]{3,2,1,0:T(8,128)} fusion(f32[1,24,96,96]{3,2,1,0:T(8,128)} %collective-permute-done.3, f32[1,24,96,96]{3,2,1,0:T(8,128)S(1)} %collective-permute-done.1, f32[24,96,96]{2,1,0:T(8,128)S(1)} %copy-done.5, f32[1,24,96,96]{3,2,1,0:T(8,128)S(1)} %copy-done.2, f32[1,24,96,96]{3,2,1,0:T(8,128)S(1)} %fusion.2, ...), kind=kOutput, calls=%fused_computation.38 | convolution fusion | flops 256886784 | bytes 7962624 | tf_op jit(solution)/shard_map/pxyz,zw->pxyw/dot_general | solution.py:66
  (8 shorter events, 0.0 us)
Async XLA Ops:
  0.0 32.2 %collective-permute-start = (f32[1,24,96,96]{3,2,1,0:T(8,128)}, f32[1,24,96,96]{3,2,1,0:T(8,128)S(1)}, u32[]{:S(2)}, u32[]{:S(2)}) collective-permute-start(f32[1,24,96,96]{3,2,1,0:T(8,128)} %param.9), channel_id=1, source_target_pairs={{0,4},{4,8},{8,12},{12,16},{16,20},{20,24},{24,28},{28,0},{1,5},{5... | collective-permute-start | bytes 2654216 | tf_op jit(solution)/shard_map/ppermute | solution.py:15
  8.6 23.6 %copy-start = (f32[1,24,96,96]{3,2,1,0:T(8,128)S(1)}, f32[1,24,96,96]{3,2,1,0:T(8,128)}, u32[]{:S(2)}) copy-start(f32[1,24,96,96]{3,2,1,0:T(8,128)} %param.9) | copy-start | bytes 2654212
  8.6 28.0 %all-to-all-start = ((f32[1,24,96,96]{3,1,0,2:T(8,128)}), f32[1,24,96,96]{3,1,0,2:T(8,128)}, u32[]{:S(2)}, u32[]{:S(2)}) async-start(f32[1,24,96,96]{3,1,0,2:T(8,128)} %copy.59), calls=%async_computation | async-start | bytes 2359296 | tf_op jit(solution)/shard_map/all_to_all | solution.py:58
  32.2 1.3 copy-start.1
  32.2 29.8 %collective-permute-start.2 = (f32[1,24,96,96]{3,2,1,0:T(8,128)S(1)}, f32[1,24,96,96]{3,2,1,0:T(8,128)S(1)}, u32[]{:S(2)}, u32[]{:S(2)}) collective-permute-start(f32[1,24,96,96]{3,2,1,0:T(8,128)S(1)} %collective-permute-done), channel_id=1, source_target_pairs={{0,4},{4,8},{8,12},{12,16},{16,20},{20,24},{24,28},{28,0},{1,5},{5... | collective-permute-start | bytes 2654216 | tf_op jit(solution)/shard_map/ppermute | solution.py:15
  36.6 29.8 %all-to-all-start.2 = ((f32[1,24,96,96]{3,1,0,2:T(8,128)}), f32[1,24,96,96]{3,1,0,2:T(8,128)}, u32[]{:S(2)}, u32[]{:S(2)}) async-start(f32[1,24,96,96]{3,1,0,2:T(8,128)} %copy.67), calls=%async_computation.2 | async-start | bytes 2359296 | tf_op jit(solution)/shard_map/all_to_all | solution.py:58
  62.0 1.3 copy-start.3
  66.4 3.7 %copy-start.7 = (f32[24]{0:T(128)S(1)}, f32[24]{0:T(128)}, u32[]{:S(2)}) copy-start(f32[24]{0:T(128)} %fusion.59) | copy-start | bytes 292
  66.4 19.3 %all-to-all-start.4 = ((f32[1,24,96,96]{3,1,0,2:T(8,128)}), f32[1,24,96,96]{3,1,0,2:T(8,128)S(1)}, u32[]{:S(2)}, u32[]{:S(2)}) async-start(f32[1,24,96,96]{3,1,0,2:T(8,128)} %copy.75), calls=%async_computation.4 | async-start | bytes 2359296 | tf_op jit(solution)/shard_map/all_to_all | solution.py:58
  85.7 19.3 %all-to-all-start.3 = ((f32[1,96,24,96]{3,2,0,1:T(8,128)}), f32[1,96,24,96]{3,2,0,1:T(8,128)S(1)}, u32[]{:S(2)}, u32[]{:S(2)}) async-start(f32[1,96,24,96]{3,2,0,1:T(8,128)} %copy.71), calls=%async_computation.3 | async-start | bytes 2359296 | tf_op jit(solution)/shard_map/all_to_all | solution.py:64
  97.5 12.1 %copy-start.6 = (f32[1,4,24,24,96]{4,3,2,1,0:T(8,128)S(1)}, f32[1,4,24,24,96]{4,3,2,1,0:T(8,128)}, u32[]{:S(2)}) copy-start(f32[1,4,24,24,96]{4,3,2,1,0:T(8,128)} %copy.61) | copy-start | bytes 2654212
  105.1 20.2 %all-to-all-start.5 = ((f32[1,96,24,96]{3,2,0,1:T(8,128)}), f32[1,96,24,96]{3,2,0,1:T(8,128)}, u32[]{:S(2)}, u32[]{:S(2)}) async-start(f32[1,96,24,96]{3,2,0,1:T(8,128)} %copy.79), calls=%async_computation.5 | async-start | bytes 2359296 | tf_op jit(solution)/shard_map/all_to_all | solution.py:64
  125.3 20.2 %all-to-all-start.1 = ((f32[1,96,24,96]{3,2,0,1:T(8,128)}), f32[1,96,24,96]{3,2,0,1:T(8,128)}, u32[]{:S(2)}, u32[]{:S(2)}) async-start(f32[1,96,24,96]{3,2,0,1:T(8,128)} %copy.63), calls=%async_computation.1 | async-start | bytes 2359296 | tf_op jit(solution)/shard_map/all_to_all | solution.py:64
  136.7 28.5 %collective-permute-start.1 = (f32[1,24,96,96]{3,2,1,0:T(8,128)}, f32[1,24,96,96]{3,2,1,0:T(8,128)S(1)}, u32[]{:S(2)}, u32[]{:S(2)}) collective-permute-start(f32[1,24,96,96]{3,2,1,0:T(8,128)} %get-tuple-element.5), channel_id=1, source_target_pairs={{0,28},{4,0},{8,4},{12,8},{16,12},{20,16},{24,20},{28,24},{1,29},{... | collective-permute-start | bytes 2654216 | tf_op jit(solution)/shard_map/ppermute | solution.py:15
  136.7 51.7 %collective-permute-start.3 = (f32[1,24,96,96]{3,2,1,0:T(8,128)}, f32[1,24,96,96]{3,2,1,0:T(8,128)}, u32[]{:S(2)}, u32[]{:S(2)}) collective-permute-start(f32[1,24,96,96]{3,2,1,0:T(8,128)} %get-tuple-element.6), channel_id=1, source_target_pairs={{0,24},{4,28},{8,0},{12,4},{16,8},{20,12},{24,16},{28,20},{1,25},{... | collective-permute-start | bytes 2654216 | tf_op jit(solution)/shard_map/ppermute | solution.py:15
  145.4 43.0 %copy-start.5 = (f32[24,96,96]{2,1,0:T(8,128)S(1)}, f32[24,96,96]{2,1,0:T(8,128)}, u32[]{:S(2)}) copy-start(f32[24,96,96]{2,1,0:T(8,128)} %get-tuple-element.7) | copy-start | bytes 2654212
  146.9 41.5 %copy-start.2 = (f32[1,24,96,96]{3,2,1,0:T(8,128)S(1)}, f32[1,24,96,96]{3,2,1,0:T(8,128)}, u32[]{:S(2)}) copy-start(f32[1,24,96,96]{3,2,1,0:T(8,128)} %copy-done.1) | copy-start | bytes 2654212
  147.0 41.5 %copy-start.4 = (f32[1,24,96,96]{3,2,1,0:T(8,128)S(1)}, f32[1,24,96,96]{3,2,1,0:T(8,128)}, u32[]{:S(2)}) copy-start(f32[1,24,96,96]{3,2,1,0:T(8,128)} %copy-done.3) | copy-start | bytes 2654212
where the time goes:
time: 193 us; the launch traced here: 192 us
  waiting for transfers between devices  114 us (59%)
  matrix products  33.2 us (17%)
  starting transfers between devices  27.7 us (14%)
  local copies, waits for them, and re-layouts  16.9 us (9%)
    ppermute x4, waiting for transfers between devices, from_behind(): lax.ppermute(shard, axis, [(i, (i + by) % length) for i in range(length)])  79.9 us
    all_to_all x3, waiting for transfers between devices, solve(): lax.all_to_all(restored, 'grid', split_axis=1, concat_axis=2, tiled=True)  25.2 us
    all_to_all x3, starting transfers between devices, solve(): lax.all_to_all(spectrum, 'grid', split_axis=2, concat_axis=1, tiled=True)  12.4 us
    all_to_all x3, starting transfers between devices, solve(): lax.all_to_all(restored, 'grid', split_axis=1, concat_axis=2, tiled=True)  12.3 us
    all_to_all x3, waiting for transfers between devices, solve(): lax.all_to_all(spectrum, 'grid', split_axis=2, concat_axis=1, tiled=True)  8.68 us
    dot_general x3, matrix products, solve(): spectrum = jnp.einsum('pxyz,zw->pxyw', spectrum, table_z, precision=EXACT)  8.41 us
    dot_general x6, matrix products, solve(): spectrum = jnp.einsum('pxyz,yw->pxwz', spectrum, table_y, precision=EXACT)  8.06 us
    dot_general x3, matrix products, solve(): jnp.einsum('xa,pxyz->payz', table_x, lax.all_to_all(spectrum, 'grid', spl...  7.75 us
  transfers between devices with their start and end apart: 10, of which 8 were waited for; matrix products, arithmetic and copies ran while one was open for 24% of the time, Pallas kernels for 0%

commit v1 on v0

v1 whole, which is shorter than its diff:
```python
import functools

import jax
import jax.numpy as jnp
import numpy as np
from jax import lax
from jax.experimental import pallas as pl
from jax.experimental.pallas import tpu as pltpu
from jax.sharding import PartitionSpec as P


CYCLE = 2
LANES = 128
F32 = jnp.float32
BF16 = jnp.bfloat16


def cas(rows, columns, length):
    phases = (np.asarray(rows)[:, None] * np.asarray(columns)[None, :]) % length
    angles = 2.0 * np.pi * phases / length
    return np.cos(angles) + np.sin(angles)


def halves(table):
    high = np.asarray(table, np.float32).astype(jnp.bfloat16)
    low = (np.asarray(table, np.float64) - np.asarray(high, np.float64)).astype(np.float32)
    return high, low.astype(jnp.bfloat16)


def doubled(high, low):
    return np.concatenate(
        [np.concatenate([high, high], axis=1), np.concatenate([low, np.zeros_like(low)], axis=1)],
        axis=0,
    )


def wavenumber_sq(indices, length):
    folded = np.minimum(indices, length - indices).astype(np.float32)
    scaled = folded * np.float32(2.0 * np.pi / length)
    return scaled * scaled


class Plan:
    def __init__(self, planes, height, breadth, parts):
        self.planes, self.height, self.breadth, self.parts = planes, height, breadth, parts
        self.length = planes * parts
        self.share = height // parts
        third = breadth // 3
        assert third * 4 == LANES and self.share % 4 == 0 and planes % 8 == 0
        self.third = third
        self.extra = self.share // 4
        self.rows = 3 * self.extra
        assert self.extra <= 8
        self.block = self.rows * planes

    def table_z(self):
        high, low = halves(cas(np.arange(self.breadth), np.arange(self.breadth), self.breadth))
        out = np.zeros((2 * LANES, 2 * LANES), jnp.bfloat16)
        n = self.breadth
        out[:n, :n] = high
        out[:n, LANES : LANES + n] = low
        out[LANES : LANES + n, :n] = high
        return out

    def positions(self, part):
        rows, index = [], []
        for k in range(self.parts):
            base = self.share * (part ^ k)
            for t in range(3):
                for q in range(self.extra):
                    rows.append((k * 3 + t) * 8 + q)
                    index.append(base + t * self.extra + q)
            for q in range(self.extra):
                rows.append((self.parts * 3 + k) * 8 + q)
                index.append(base + 3 * self.extra + q)
        return np.array(rows), np.array(index)

    def table_y(self):
        m = self.parts * 32
        forward, backward = [], []
        for part in range(self.parts):
            rows, index = self.positions(part)
            full = np.zeros((m, self.height))
            full[rows] = cas(index, np.arange(self.height), self.height)
            high, low = halves(full)
            forward.append(doubled(high, low))
            backward.append(doubled(high.T, low.T))
        return np.stack(forward), np.stack(backward)

    def table_x(self):
        forward, backward = [], []
        for part in range(self.parts):
            order = np.concatenate(
                [np.arange(self.planes) + self.planes * (part ^ k) for k in range(self.parts)]
            )
            high, low = halves(cas(np.arange(self.length), order, self.length))
            forward.append(doubled(high, low))
            backward.append(doubled(high.T, low.T))
        return np.stack(forward), np.stack(backward)

    def waves(self):
        across = np.broadcast_to(
            wavenumber_sq(np.arange(self.length), self.length)[:, None], (self.length, LANES)
        )
        row = np.arange(self.rows)[:, None]
        lane = np.arange(LANES)[None, :]
        main = lane < self.breadth
        y = np.where(main, row, 3 * self.extra + row % self.extra)
        z = np.where(main, lane, self.third * (row // self.extra) + lane - self.breadth)
        within = np.zeros((self.parts, -(-self.rows // 8) * 8, LANES), np.float32)
        for part in range(self.parts):
            within[part, : self.rows] = wavenumber_sq(
                part * self.share + y, self.height
            ) + wavenumber_sq(z, self.breadth)
        return np.array(across), within


def split(value):
    high = value.astype(BF16)
    return high, (value - high.astype(F32)).astype(BF16)


def dot(a, b):
    return jnp.dot(a, b, preferred_element_type=F32)


def lanes(shape):
    return lax.broadcasted_iota(jnp.int32, shape, len(shape) - 1)


def along_rows(table, value):
    both = dot(table, jnp.concatenate(split(value), axis=0))
    half = both.shape[0] // 2
    return both[:half] + both[half:]


def along_lanes(value, table):
    both = dot(jnp.concatenate(split(value), axis=1), table)
    return both[:, :LANES] + both[:, LANES:]


def widen(value):
    rows, width = value.shape
    return jnp.concatenate([value, jnp.zeros((rows, LANES - width), value.dtype)], axis=1)


def pack(wide, plan):
    h = plan.height // 4
    tail = wide[3 * h :]
    parts = []
    for t in range(3):
        main = wide[t * h : (t + 1) * h]
        moved = pltpu.roll(tail, plan.breadth - plan.third * t, 1)
        parts.append(jnp.where(lanes(main.shape) < plan.breadth, main, moved))
    return jnp.concatenate(parts, axis=0)


def thirds(parts, plan):
    tail = None
    for t, part in enumerate(parts):
        moved = pltpu.roll(part, (plan.third * (t + 1)) % LANES, 1)
        tail = moved if tail is None else jnp.where(lanes(part.shape) < plan.third * t, tail, moved)
    return tail


def unpack(value, plan):
    h = plan.height // 4
    return jnp.concatenate(
        [value, thirds([value[t * h : (t + 1) * h] for t in range(3)], plan)], axis=0
    )


def clear(wide, plan):
    return jnp.where(lanes(wide.shape) < plan.breadth, wide, 0.0)


def store_spectrum(plan, density, tz, ty, outs, base, stride, plane):
    h, e = plan.height, plan.extra
    once = along_lanes(density, tz)
    for pair in range(CHUNK // 2):
        two = jnp.concatenate(
            [once[(2 * pair + i) * h : (2 * pair + i + 1) * h] for i in range(2)], axis=1
        )
        spectrum = along_rows(ty, two)
        for i in range(2):
            s = spectrum[:, i * LANES : (i + 1) * LANES]
            for k in range(plan.parts):
                tail = s[(3 * plan.parts + k) * 8 : (3 * plan.parts + k + 1) * 8]
                for t in range(3):
                    main = s[(k * 3 + t) * 8 : (k * 3 + t + 1) * 8]
                    moved = pltpu.roll(tail, plan.breadth - plan.third * t, 1)
                    packed = jnp.where(lanes(main.shape) < plan.breadth, main, moved)
                    first = base + t * e * stride + plane + 2 * pair + i
                    outs[k][pl.ds(first, e, stride=stride), :] = packed[:e]


def load_potential(plan, ins, base, stride, plane, tz, ty):
    e = plan.extra
    planes = []
    for pair in range(CHUNK // 2):
        two = []
        for i in range(2):
            rows, tails = [], []
            for k in range(plan.parts):
                parts = []
                for t in range(3):
                    first = base + t * e * stride + plane + 2 * pair + i
                    part = ins[k][pl.ds(first, e, stride=stride), :]
                    parts.append(jnp.concatenate([part, jnp.zeros((8 - e, LANES), F32)], axis=0))
                rows += parts
                tails.append(thirds(parts, plan))
            two.append(jnp.concatenate(rows + tails, axis=0))
        once = along_rows(ty, jnp.concatenate(two, axis=1))
        planes += [once[:, :LANES], once[:, LANES:]]
    return along_lanes(jnp.concatenate(planes, axis=0), tz)


CHUNK = 8


def forward_own_kernel(plan, scalars, own_ref, tz_ref, ty_ref, *outs):
    blocks, chunks = outs[: plan.parts], outs[plan.parts :]
    h = plan.height
    packed_rows = 3 * h // 4
    for c, chunk in enumerate(chunks):
        own = own_ref[c * CHUNK : (c + 1) * CHUNK].reshape(CHUNK * h, plan.breadth)
        wide = widen(own)
        for i in range(CHUNK):
            chunk[i * packed_rows : (i + 1) * packed_rows, :] = pack(
                wide[i * h : (i + 1) * h], plan
            )
        store_spectrum(plan, wide * wide, tz_ref[...], ty_ref[0], blocks, 0, plan.planes, c * CHUNK)


def load_packed(ref, plan):
    packed_rows = 3 * plan.height // 4
    return jnp.concatenate(
        [unpack(ref[i * packed_rows : (i + 1) * packed_rows, :], plan) for i in range(CHUNK)],
        axis=0,
    )


def load_own(ref, plan):
    return widen(ref[...].reshape(CHUNK * plan.height, plan.breadth))


def forward_pair_kernel(plan, scalars, own_ref, q_ref, r_ref, tz_ref, ty_ref, after_ref, *outs):
    even = scalars[1] == 1
    p = load_own(own_ref, plan)
    r = load_packed(r_ref, plan)
    tz, ty = tz_ref[...], ty_ref[0]
    store_spectrum(plan, p * r, tz, ty, outs, 0, CHUNK, 0)
    q = load_packed(q_ref, plan)
    mixed = clear(q * jnp.where(even, r, p), plan)
    store_spectrum(plan, mixed, tz, ty, outs, plan.rows * CHUNK, CHUNK, 0)


def screen_kernel(plan, scalars, across_ref, within_ref, after_ref, out_ref):
    cells = plan.length * plan.height * plan.breadth
    limit = 4.0 * np.pi / plan.length
    rate = 1.0 / (4.0 * limit * limit)
    for row in range(plan.rows):
        wave_sq = across_ref[...] + within_ref[0, row : row + 1, :]
        guarded = jnp.where(wave_sq > 0, wave_sq, 1.0)
        screened = (-0.2 * 4.0 * np.pi / cells) / guarded * (1.0 - jnp.exp(guarded * -rate))
        out_ref[row * plan.length : (row + 1) * plan.length, :] = jnp.where(
            wave_sq > 0, screened, 0.0
        )


def middle_kernel(plan, sizes_in, sizes_out, count, scalars, *refs):
    n = plan.parts
    ins = [refs[k * len(sizes_in) : (k + 1) * len(sizes_in)] for k in range(n)]
    refs = refs[n * len(sizes_in) :]
    screen_ref, tf_ref, tb_ref, after_ref, *refs = refs
    outs = [refs[k * len(sizes_out) : (k + 1) * len(sizes_out)] for k in range(n)]
    length = plan.length
    for pair in range(plan.rows // 2):
        for solve in range(count):
            columns = []
            for i in range(2):
                row = pair * 2 + i
                parts = []
                for k in range(n):
                    for ref, size in zip(ins[k], sizes_in):
                        first = (solve * plan.rows + row) * size
                        parts.append(ref[first : first + size, :])
                columns.append(jnp.concatenate(parts, axis=0))
            spectrum = along_rows(tf_ref[0], jnp.concatenate(columns, axis=1))
            screen = jnp.concatenate(
                [
                    screen_ref[(pair * 2 + i) * length : (pair * 2 + i + 1) * length, :]
                    for i in range(2)
                ],
                axis=1,
            )
            back = along_rows(tb_ref[0], spectrum * screen)
            for i in range(2):
                row = pair * 2 + i
                for k in range(n):
                    at = k * plan.planes
                    for ref, size in zip(outs[k], sizes_out):
                        first = (solve * plan.rows + row) * size
                        ref[first : first + size, :] = back[
                            at : at + size, i * LANES : (i + 1) * LANES
                        ]
                        at += size


def backward_pair_kernel(plan, scalars, *refs):
    n = plan.parts
    ins, refs = refs[:n], refs[n:]
    own_ref, q_ref, r_ref, tz_ref, ty_ref, _, total_ref, y_ref, z_ref = refs
    even = scalars[1] == 1
    h = plan.height
    tz, ty = tz_ref[...], ty_ref[0]
    visit = load_potential(plan, ins, 0, CHUNK, 0, tz, ty)
    mixed = load_potential(plan, ins, plan.rows * CHUNK, CHUNK, 0, tz, ty)
    p = load_own(own_ref, plan)
    r = load_packed(r_ref, plan)
    q = load_packed(q_ref, plan)
    other = mixed * q
    zero = jnp.zeros_like(other)
    total = visit * r + jnp.where(even, zero, other)
    total_ref[...] = total[:, : plan.breadth].reshape(CHUNK, h, plan.breadth)
    to_z = visit * p + jnp.where(even, other, zero)
    to_y = mixed * jnp.where(even, r, p)
    packed_rows = 3 * h // 4
    for i in range(CHUNK):
        rows = slice(i * packed_rows, (i + 1) * packed_rows)
        y_ref[rows, :] = pack(to_y[i * h : (i + 1) * h], plan)
        z_ref[rows, :] = pack(to_z[i * h : (i + 1) * h], plan)


def backward_own_kernel(plan, sizes, scalars, *refs):
    n, m = plan.parts, len(sizes)
    ins = [refs[k * m : (k + 1) * m] for k in range(n)]
    refs = refs[n * m :]
    chunks = plan.planes // CHUNK
    totals, refs = refs[:chunks], refs[chunks:]
    own_ref, tz_ref, ty_ref, _, out_ref = refs
    for c in range(chunks):
        at, piece = c * CHUNK, 0
        while at >= sizes[piece]:
            at -= sizes[piece]
            piece += 1
        value = load_potential(
            plan, [ins[k][piece] for k in range(n)], 0, sizes[piece], at, tz_ref[...], ty_ref[0]
        )
        value = value[:, : plan.breadth].reshape(CHUNK, plan.height, plan.breadth)
        here = slice(c * CHUNK, (c + 1) * CHUNK)
        out_ref[here] = totals[c][...] + value * own_ref[here]


def final_kernel(plan, scalars, own_ref, *refs):
    chunks = plan.planes // CHUNK
    ys, zs, out_ref = refs[:chunks], refs[chunks : 2 * chunks], refs[-1]
    packed_rows = 3 * plan.height // 4
    for c in range(chunks):
        for i in range(CHUNK):
            rows = slice(i * packed_rows, (i + 1) * packed_rows)
            returned = unpack(ys[c][rows, :] + zs[c][rows, :], plan)
            out_ref[c * CHUNK + i] = own_ref[c * CHUNK + i] + returned[:, : plan.breadth]


def call(kernel, scalars, operands, outs, selected=(), chunk=None, after=None):
    specs = []
    for operand in operands:
        if any(operand is s for s in selected):
            specs.append(pl.BlockSpec((1,) + operand.shape[1:], lambda i, s: (s[0], 0, 0)))
        elif chunk is not None and operand is chunk[0]:
            specs.append(
                pl.BlockSpec(
                    (CHUNK,) + operand.shape[1:], lambda i, s, c=chunk[1]: (c, 0, 0)
                )
            )
        else:
            zeros = (0,) * operand.ndim
            specs.append(pl.BlockSpec(operand.shape, lambda i, s, zeros=zeros: zeros))
    if after is not None:
        operands = (*operands, after)
        specs.append(pl.BlockSpec(memory_space=pl.ANY))
    out_specs = [pl.BlockSpec(o, lambda i, s, zeros=(0,) * len(o): zeros) for o in outs]
    return pl.pallas_call(
        kernel,
        grid_spec=pltpu.PrefetchScalarGridSpec(
            num_scalar_prefetch=1, grid=(1,), in_specs=specs, out_specs=out_specs
        ),
        out_shape=[jax.ShapeDtypeStruct(o, F32) for o in outs],
        compiler_params=pltpu.CompilerParams(vmem_limit_bytes=48 * 1024 * 1024),
    )(scalars, *operands)


def exchange(blocks, parts):
    return [blocks[0]] + [
        lax.ppermute(blocks[k], "grid", [(i, i ^ k) for i in range(parts)])
        for k in range(1, parts)
    ]


def exchange_term(bands):
    parts = lax.axis_size("grid")
    number = lax.axis_size("band")
    own = bands[0]
    plan = Plan(*own.shape, parts)
    part = lax.axis_index("grid")
    even = 1 - lax.axis_index("band") % 2
    scalars = jnp.stack([part, even]).astype(jnp.int32)
    swap = [(i, i ^ 1) for i in range(number)]
    behind = [(i, (i - CYCLE) % number) for i in range(number)]
    ahead = [(i, (i + CYCLE) % number) for i in range(number)]
    tz = jnp.asarray(plan.table_z())
    ty_forward, ty_backward = (jnp.asarray(t) for t in plan.table_y())
    tx_forward, tx_backward = (jnp.asarray(t) for t in plan.table_x())
    across, within = (jnp.asarray(t) for t in plan.waves())
    chunks = plan.planes // CHUNK
    whole = own.shape
    packed = (CHUNK * 3 * plan.height // 4, LANES)
    sizes = (CHUNK, plan.planes - CHUNK)

    *blocks, = call(
        functools.partial(forward_own_kernel, plan),
        scalars,
        (own, tz, ty_forward),
        [(plan.block, LANES)] * parts + [packed] * chunks,
        (ty_forward,),
    )
    blocks, mine = blocks[:parts], blocks[parts:]
    own_in = exchange(blocks, parts)
    q, r = [], []
    for chunk in mine:
        r.append(lax.ppermute(chunk, "band", behind))
        q.append(lax.ppermute(chunk, "band", swap))
    (screen,) = call(
        functools.partial(screen_kernel, plan),
        scalars,
        (across, within),
        [(plan.rows * plan.length, LANES)],
        (within,),
        after=blocks[0],
    )
    after = screen
    pair_in = []
    for c in range(chunks):
        out = call(
            functools.partial(forward_pair_kernel, plan),
            scalars,
            (own, q[c], r[c], tz, ty_forward),
            [(2 * plan.rows * CHUNK, LANES)] * parts,
            (ty_forward,),
            (own, c),
            after,
        )
        after = out[0]
        pair_in.append(exchange(out, parts))

    def middle(ins, sizes_in, sizes_out, count, after):
        out = call(
            functools.partial(middle_kernel, plan, sizes_in, sizes_out, count),
            scalars,
            (*[block for part in ins for block in part], screen, tx_forward, tx_backward),
            [(count * plan.rows * size, LANES) for size in sizes_out] * parts,
            (tx_forward, tx_backward),
            after=after,
        )
        return [out[i :: len(sizes_out)] for i in range(len(sizes_out))]

    own_mid = middle([[b] for b in own_in], (plan.planes,), sizes, 1, after)
    own_back = [exchange(own_mid[0], parts)]
    even_chunks = (CHUNK,) * chunks
    pair_mid = middle(
        [[pair_in[c][k] for c in range(chunks)] for k in range(parts)],
        even_chunks,
        even_chunks,
        2,
        own_mid[0][0],
    )
    pair_back = [exchange(blocks, parts) for blocks in pair_mid]
    own_back.append(exchange(own_mid[1], parts))
    after = pair_mid[0][0]
    totals, from_y, from_z = [], [], []
    for c in range(chunks):
        total, y, z = call(
            functools.partial(backward_pair_kernel, plan),
            scalars,
            (*pair_back[c], own, q[c], r[c], tz, ty_backward),
            [(CHUNK,) + whole[1:], packed, packed],
            (ty_backward,),
            (own, c),
            after,
        )
        after = total
        totals.append(total)
        from_z.append(lax.ppermute(z, "band", ahead))
        from_y.append(lax.ppermute(y, "band", swap))
    (total,) = call(
        functools.partial(backward_own_kernel, plan, sizes),
        scalars,
        (*[own_back[i][k] for k in range(parts) for i in range(2)], *totals, own, tz, ty_backward),
        [whole],
        (ty_backward,),
        after=after,
    )
    (result,) = call(
        functools.partial(final_kernel, plan), scalars, (total, *from_y, *from_z), [whole]
    )
    return result[None]


def solution(mesh):
    return jax.shard_map(
        exchange_term,
        mesh=mesh,
        in_specs=(P("band", "grid", None, None),),
        out_specs=P("band", "grid", None, None),
        check_vma=False,
    )
```

time: 193 us -> 118 us (0.61)
  waiting for transfers between devices: 114 us -> 56.9 us
  matrix products: 33.2 us -> 0 us
  Pallas kernels: 0 us -> 18.8 us
  local copies, waits for them, and re-layouts: 16.9 us -> 3.24 us
  starting transfers between devices: 27.7 us -> 38.8 us
    ppermute x4 -> x39, starting transfers between devices: 3 us -> 38.8 us  [the longest x27 20.4 us: exchange(): lax.ppermute(blocks[k], 'grid', [(i, i ^ k) for i in range(parts)])]
    all_to_all x6 -> x0, waiting for transfers between devices: 33.8 us -> none  [the longest x3 25.2 us: solve(): lax.all_to_all(restored, 'grid', split_axis=1, concat_axis=2, tiled=True)]
    dot_general x18 -> x0, matrix products: 33.2 us -> none  [the longest x3 8.41 us: solve(): spectrum = jnp.einsum('pxyz,zw->pxyw', spectrum, table_z, precision=EXACT)]
    all_to_all x6 -> x0, starting transfers between devices: 24.7 us -> none  [the longest x3 12.4 us: solve(): lax.all_to_all(spectrum, 'grid', split_axis=2, concat_axis=1, tiled=True)]
    ppermute x4 -> x39, waiting for transfers between devices: 79.9 us -> 56.9 us  [the longest x27 31.5 us: exchange(): lax.ppermute(blocks[k], 'grid', [(i, i ^ k) for i in range(parts)])]
    pallas_call x0 -> x12, Pallas kernels: none -> 18.8 us  [call(): pl.pallas_call(kernel, grid_spec=pltpu.PrefetchScalarGridSpec(num_scalar_...]
    transpose x6 -> x0, local copies, waits for them, and re-layouts: 9.34 us -> none  [the longest x3 5.14 us: solve(): spectrum = jnp.einsum('pxyz,yw->pxwz', spectrum, table_y, precision=EXACT)]
    all_to_all x9 -> x0, local copies, waits for them, and re-layouts: 7.54 us -> none  [the longest x6 4.51 us: solve(): lax.all_to_all(spectrum, 'grid', split_axis=2, concat_axis=1, tiled=True)]
  transfers between devices with their start and end apart: 10 -> 39, of which waited for: 8 -> 21; matrix products, arithmetic and copies ran while one was open for 24% -> 0% of each run, Pallas kernels for 0% -> 10%
where the time goes in v1:
time: 118 us
  waiting for transfers between devices  56.9 us (48%)
  starting transfers between devices  38.8 us (33%)
  Pallas kernels  18.8 us (16%)
  local copies, waits for them, and re-layouts  3.24 us (3%)
    ppermute x27, waiting for transfers between devices, exchange(): lax.ppermute(blocks[k], 'grid', [(i, i ^ k) for i in range(parts)])  31.5 us
    ppermute x27, starting transfers between devices, exchange(): lax.ppermute(blocks[k], 'grid', [(i, i ^ k) for i in range(parts)])  20.4 us
    pallas_call x12, Pallas kernels, call(): pl.pallas_call(kernel, grid_spec=pltpu.PrefetchScalarGridSpec(num_scalar_...  18.8 us
    ppermute x3, waiting for transfers between devices, exchange_term(): from_z.append(lax.ppermute(z, 'band', ahead))  15.1 us
    ppermute x3, waiting for transfers between devices, exchange_term(): r.append(lax.ppermute(chunk, 'band', behind))  8.31 us
    ppermute x3, starting transfers between devices, exchange_term(): r.append(lax.ppermute(chunk, 'band', behind))  6.03 us
    ppermute x3, starting transfers between devices, exchange_term(): from_z.append(lax.ppermute(z, 'band', ahead))  5.23 us
    ppermute x3, starting transfers between devices, exchange_term(): from_y.append(lax.ppermute(y, 'band', swap))  3.6 us
  transfers between devices with their start and end apart: 39, of which 21 were waited for; matrix products, arithmetic and copies ran while one was open for 0% of the time, Pallas kernels for 10%

profile of v1, /device:TPU:0, one launch (start us, length us, event | category | flops | bytes accessed | tf_op | source)
XLA Modules:
  0.0 118.0 jit_solution(6491761904483711298)
XLA Ops:
  0.1 1.3 %copy-done = f32[1,24,96,96]{3,2,1,0:T(8,128)S(1)} copy-done((f32[1,24,96,96]{3,2,1,0:T(8,128)S(1)}, f32[1,24,96,96]{3,2,1,0:T(8,128)}, u32[]{:S(2)}) %copy-start) | copy-done | bytes 884760
  1.4 0.9 copy-done.2
  2.3 1.0 copy-done.4
  3.3 1.9 %shard_map.82 = (f32[432,128]{1,0:T(8,128)S(1)}, f32[432,128]{1,0:T(8,128)S(1)}, f32[432,128]{1,0:T(8,128)S(1)}, f32[432,128]{1,0:T(8,128)S(1)}, f32[576,128]{1,...) custom-call(s32[2]{0:T(128)S(1)} %pad_add_fusion.scalars, f32[24,96,96]{2,1,0:T(8,128)S(1)} %bitcast.4, ...), custom_call_target="tpu_custom_call" | custom-call | tf_op jit(solution)/shard_map/pallas_call | solution.py:384
  5.2 5.1 %collective-permute-start.6 = (f32[576,128]{1,0:T(8,128)S(1)}, f32[576,128]{1,0:T(8,128)S(1)}, u32[]{:S(2)}, u32[]{:S(2)}) collective-permute-start(f32[576,128]{1,0:T(8,128)S(1)} %get-tuple-element.58), channel_id=1, source_target_pairs={{0,24},{4,28},{8,0},{12,4},{16,8},{20,12},{24,16},{28,20},{1,25},{... | collective-permute-start | bytes 884744 | tf_op jit(solution)/shard_map/ppermute | solution.py:432
  10.3 1.5 %collective-permute-start.5 = (f32[576,128]{1,0:T(8,128)S(1)}, f32[576,128]{1,0:T(8,128)S(1)}, u32[]{:S(2)}, u32[]{:S(2)}) collective-permute-start(f32[576,128]{1,0:T(8,128)S(1)} %get-tuple-element.58), channel_id=1, source_target_pairs={{0,4},{4,0},{8,12},{12,8},{16,20},{20,16},{24,28},{28,24},{1,5},{5... | collective-permute-start | bytes 884744 | tf_op jit(solution)/shard_map/ppermute | solution.py:433
  11.8 0.4 collective-permute-start.8
  12.3 0.5 collective-permute-start.7
  13.2 4.5 %collective-permute-done.6.r_ref.refs_6_ = f32[576,128]{1,0:T(8,128)S(1)} collective-permute-done((f32[576,128]{1,0:T(8,128)S(1)}, f32[576,128]{1,0:T(8,128)S(1)}, u32[]{:S(2)}, u32[]{:S(2)}) %collective-permute-start.6) | collective-permute-done | bytes 294944 | tf_op jit(solution)/shard_map/ppermute | solution.py:432
  17.7 1.5 %collective-permute-start.3 = (f32[576,128]{1,0:T(8,128)S(1)}, f32[576,128]{1,0:T(8,128)S(1)}, u32[]{:S(2)}, u32[]{:S(2)}) collective-permute-start(f32[576,128]{1,0:T(8,128)S(1)} %get-tuple-element.57), channel_id=1, source_target_pairs={{0,4},{4,0},{8,12},{12,8},{16,20},{20,16},{24,28},{28,24},{1,5},{5... | collective-permute-start | bytes 884744 | tf_op jit(solution)/shard_map/ppermute | solution.py:433
  19.2 1.0 collective-permute-done.5.q_ref.refs_5_
  20.2 3.8 %collective-permute-done.8.r_ref.refs_6_ = f32[576,128]{1,0:T(8,128)S(1)} collective-permute-done((f32[576,128]{1,0:T(8,128)S(1)}, f32[576,128]{1,0:T(8,128)S(1)}, u32[]{:S(2)}, u32[]{:S(2)}) %collective-permute-start.8) | collective-permute-done | bytes 294944 | tf_op jit(solution)/shard_map/ppermute | solution.py:432
  24.0 1.5 %collective-permute-start.1 = (f32[432,128]{1,0:T(8,128)S(1)}, f32[432,128]{1,0:T(8,128)S(1)}, u32[]{:S(2)}, u32[]{:S(2)}) collective-permute-start(f32[432,128]{1,0:T(8,128)S(1)} %get-tuple-element.55), channel_id=1, source_target_pairs={{0,2},{1,3},{2,0},{3,1},{4,6},{5,7},{6,4},{7,5},{8,10},{9,11},{10,... | collective-permute-start | bytes 663560 | tf_op jit(solution)/shard_map/ppermute | solution.py:396
  25.5 1.0 collective-permute-done.7.q_ref.refs_5_
  26.5 0.9 shard_map.83.after_ref.refs_4_.refs_12_
  27.4 1.5 %shard_map.84 = (f32[288,128]{1,0:T(8,128)S(1)}, f32[288,128]{1,0:T(8,128)S(1)}, f32[288,128]{1,0:T(8,128)S(1)}, f32[288,128]{1,0:T(8,128)S(1)}) custom-call(s32[2]{0:T(128)S(1)} %pad_add_fusion.scalars, f32[24,96,96]{2,1,0:T(8,128)S(1)} %bitcast.5, f32[576,128]{1,0:T(8,128)S(1)} %collective-permute-done.7.q_ref.refs_5_, ...), custom_call_target="tpu_custom_call" | custom-call | tf_op jit(solution)/shard_map/pallas_call | solution.py:384
  28.9 1.5 %shard_map.85 = (f32[288,128]{1,0:T(8,128)S(1)}, f32[288,128]{1,0:T(8,128)S(1)}, f32[288,128]{1,0:T(8,128)S(1)}, f32[288,128]{1,0:T(8,128)S(1)}) custom-call(s32[2]{0:T(128)S(1)} %pad_add_fusion.scalars, f32[24,96,96]{2,1,0:T(8,128)S(1)} %bitcast.6, f32[576,128]{1,0:T(8,128)S(1)} %collective-permute-done.5.q_ref.refs_5_, ...), custom_call_target="tpu_custom_call" | custom-call | tf_op jit(solution)/shard_map/pallas_call | solution.py:384
  30.5 1.7 %collective-permute-start.15 = (f32[288,128]{1,0:T(8,128)S(1)}, f32[288,128]{1,0:T(8,128)S(1)}, u32[]{:S(2)}, u32[]{:S(2)}) collective-permute-start(f32[288,128]{1,0:T(8,128)S(1)} %get-tuple-element.71), channel_id=1, source_target_pairs={{0,1},{1,0},{2,3},{3,2},{4,5},{5,4},{6,7},{7,6},{8,9},{9,8},{10,11... | collective-permute-start | bytes 442376 | tf_op jit(solution)/shard_map/ppermute | solution.py:396
  32.1 0.5 collective-permute-start.18
  32.7 0.9 collective-permute-start.21
  33.6 0.7 collective-permute-start.16
  34.3 1.5 %shard_map.86 = (f32[288,128]{1,0:T(8,128)S(1)}, f32[288,128]{1,0:T(8,128)S(1)}, f32[288,128]{1,0:T(8,128)S(1)}, f32[288,128]{1,0:T(8,128)S(1)}) custom-call(s32[2]{0:T(128)S(1)} %pad_add_fusion.scalars, f32[24,96,96]{2,1,0:T(8,128)S(1)} %bitcast.7, f32[576,128]{1,0:T(8,128)S(1)} %collective-permute-done.3.q_ref.refs_5_, ...), custom_call_target="tpu_custom_call" | custom-call | tf_op jit(solution)/shard_map/pallas_call | solution.py:384
  35.8 0.6 collective-permute-start.19
  36.4 0.8 collective-permute-start.22
  37.2 1.6 %collective-permute-done.18.refs_6_ = f32[288,128]{1,0:T(8,128)S(1)} collective-permute-done((f32[288,128]{1,0:T(8,128)S(1)}, f32[288,128]{1,0:T(8,128)S(1)}, u32[]{:S(2)}, u32[]{:S(2)}) %collective-permute-start.18) | collective-permute-done | bytes 147488 | tf_op jit(solution)/shard_map/ppermute | solution.py:396
  38.8 1.6 %collective-permute-done.21.refs_9_ = f32[288,128]{1,0:T(8,128)S(1)} collective-permute-done((f32[288,128]{1,0:T(8,128)S(1)}, f32[288,128]{1,0:T(8,128)S(1)}, u32[]{:S(2)}, u32[]{:S(2)}) %collective-permute-start.21) | collective-permute-done | bytes 147488 | tf_op jit(solution)/shard_map/ppermute | solution.py:396
  40.5 1.6 %collective-permute-start.20 = (f32[288,128]{1,0:T(8,128)S(1)}, f32[288,128]{1,0:T(8,128)S(1)}, u32[]{:S(2)}, u32[]{:S(2)}) collective-permute-start(f32[288,128]{1,0:T(8,128)S(1)} %get-tuple-element.76), channel_id=1, source_target_pairs={{0,2},{1,3},{2,0},{3,1},{4,6},{5,7},{6,4},{7,5},{8,10},{9,11},{10,... | collective-permute-start | bytes 442376 | tf_op jit(solution)/shard_map/ppermute | solution.py:396
  42.0 1.1 collective-permute-start.23
  43.2 1.3 %shard_map.87 = (f32[144,128]{1,0:T(8,128)S(1)}, f32[288,128]{1,0:T(8,128)S(1)}, f32[144,128]{1,0:T(8,128)S(1)}, f32[288,128]{1,0:T(8,128)S(1)}, f32[144,128]{1,...) custom-call(s32[2]{0:T(128)S(1)} %pad_add_fusion.scalars, ...), custom_call_target="tpu_custom_call" | custom-call | tf_op jit(solution)/shard_map/pallas_call | solution.py:384
  44.5 0.6 collective-permute-done.19.refs_7_
  45.2 1.6 %collective-permute-done.22.refs_10_ = f32[288,128]{1,0:T(8,128)S(1)} collective-permute-done((f32[288,128]{1,0:T(8,128)S(1)}, f32[288,128]{1,0:T(8,128)S(1)}, u32[]{:S(2)}, u32[]{:S(2)}) %collective-permute-start.22) | collective-permute-done | bytes 147488 | tf_op jit(solution)/shard_map/ppermute | solution.py:396
  46.8 4.7 %collective-permute-done.20.refs_8_ = f32[288,128]{1,0:T(8,128)S(1)} collective-permute-done((f32[288,128]{1,0:T(8,128)S(1)}, f32[288,128]{1,0:T(8,128)S(1)}, u32[]{:S(2)}, u32[]{:S(2)}) %collective-permute-start.20) | collective-permute-done | bytes 147488 | tf_op jit(solution)/shard_map/ppermute | solution.py:396
  51.5 1.4 %collective-permute-done.23.refs_11_ = f32[288,128]{1,0:T(8,128)S(1)} collective-permute-done((f32[288,128]{1,0:T(8,128)S(1)}, f32[288,128]{1,0:T(8,128)S(1)}, u32[]{:S(2)}, u32[]{:S(2)}) %collective-permute-start.23) | collective-permute-done | bytes 147488 | tf_op jit(solution)/shard_map/ppermute | solution.py:396
  52.9 1.9 %shard_map.88 = (f32[288,128]{1,0:T(8,128)S(1)}, f32[288,128]{1,0:T(8,128)S(1)}, f32[288,128]{1,0:T(8,128)S(1)}, f32[288,128]{1,0:T(8,128)S(1)}, f32[288,128]{1,...) custom-call(s32[2]{0:T(128)S(1)} %pad_add_fusion.scalars, ...), custom_call_target="tpu_custom_call" | custom-call | tf_op jit(solution)/shard_map/pallas_call | solution.py:384
  54.7 0.8 collective-permute-start.24
  55.5 1.4 %collective-permute-start.25 = (f32[288,128]{1,0:T(8,128)S(1)}, f32[288,128]{1,0:T(8,128)S(1)}, u32[]{:S(2)}, u32[]{:S(2)}) collective-permute-start(f32[288,128]{1,0:T(8,128)S(1)} %get-tuple-element.82), channel_id=1, source_target_pairs={{0,2},{1,3},{2,0},{3,1},{4,6},{5,7},{6,4},{7,5},{8,10},{9,11},{10,... | collective-permute-start | bytes 442376 | tf_op jit(solution)/shard_map/ppermute | solution.py:396
  56.9 0.7 collective-permute-start.27
  57.6 1.4 %collective-permute-start.28 = (f32[288,128]{1,0:T(8,128)S(1)}, f32[288,128]{1,0:T(8,128)S(1)}, u32[]{:S(2)}, u32[]{:S(2)}) collective-permute-start(f32[288,128]{1,0:T(8,128)S(1)} %get-tuple-element.87), channel_id=1, source_target_pairs={{0,2},{1,3},{2,0},{3,1},{4,6},{5,7},{6,4},{7,5},{8,10},{9,11},{10,... | collective-permute-start | bytes 442376 | tf_op jit(solution)/shard_map/ppermute | solution.py:396
  59.0 3.2 %collective-permute-done.25.refs_2_ = f32[288,128]{1,0:T(8,128)S(1)} collective-permute-done((f32[288,128]{1,0:T(8,128)S(1)}, f32[288,128]{1,0:T(8,128)S(1)}, u32[]{:S(2)}, u32[]{:S(2)}) %collective-permute-start.25) | collective-permute-done | bytes 147488 | tf_op jit(solution)/shard_map/ppermute | solution.py:396
  62.2 2.1 %collective-permute-done.26.refs_3_ = f32[288,128]{1,0:T(8,128)S(1)} collective-permute-done((f32[288,128]{1,0:T(8,128)S(1)}, f32[288,128]{1,0:T(8,128)S(1)}, u32[]{:S(2)}, u32[]{:S(2)}) %collective-permute-start.26) | collective-permute-done | bytes 147488 | tf_op jit(solution)/shard_map/ppermute | solution.py:396
  64.3 1.0 collective-permute-start.31
  65.3 1.3 %collective-permute-start.32 = (f32[288,128]{1,0:T(8,128)S(1)}, f32[288,128]{1,0:T(8,128)S(1)}, u32[]{:S(2)}, u32[]{:S(2)}) collective-permute-start(f32[288,128]{1,0:T(8,128)S(1)} %get-tuple-element.93), channel_id=1, source_target_pairs={{0,3},{1,2},{2,1},{3,0},{4,7},{5,6},{6,5},{7,4},{8,11},{9,10},{10,... | collective-permute-start | bytes 442376 | tf_op jit(solution)/shard_map/ppermute | solution.py:396
  66.6 1.6 %shard_map.89 = (f32[8,96,96]{2,1,0:T(8,128)S(1)}, f32[576,128]{1,0:T(8,128)S(1)}, f32[576,128]{1,0:T(8,128)S(1)}) custom-call(s32[2]{0:T(128)S(1)} %pad_add_fusion.scalars, f32[288,128]{1,0:T(8,128)S(1)} %get-tuple-element.80.refs_0_.refs_9_, f32[288,128]{1,0:T(8,128)S(1)} %collective-permute-done.24.refs_1_, ...), custom_call_target="tpu_custom_call" | custom-call | tf_op jit(solution)/shard_map/pallas_call | solution.py:384
  68.5 2.1 %collective-permute-done.29.refs_3_ = f32[288,128]{1,0:T(8,128)S(1)} collective-permute-done((f32[288,128]{1,0:T(8,128)S(1)}, f32[288,128]{1,0:T(8,128)S(1)}, u32[]{:S(2)}, u32[]{:S(2)}) %collective-permute-start.29) | collective-permute-done | bytes 147488 | tf_op jit(solution)/shard_map/ppermute | solution.py:396
  70.6 1.6 %shard_map.90 = (f32[8,96,96]{2,1,0:T(8,128)S(1)}, f32[576,128]{1,0:T(8,128)S(1)}, f32[576,128]{1,0:T(8,128)S(1)}) custom-call(s32[2]{0:T(128)S(1)} %pad_add_fusion.scalars, f32[288,128]{1,0:T(8,128)S(1)} %get-tuple-element.85.refs_0_, f32[288,128]{1,0:T(8,128)S(1)} %collective-permute-done.27.refs_1_, f32[288,128]{1,0:T(8,128)S(1)} %collective-permute-done.28.refs_2_, ...), custom_call_target="tpu_custom_call" | custom-call | tf_op jit(solution)/shard_map/pallas_call | solution.py:384
  72.2 2.7 %collective-permute-done.31.refs_2_ = f32[288,128]{1,0:T(8,128)S(1)} collective-permute-done((f32[288,128]{1,0:T(8,128)S(1)}, f32[288,128]{1,0:T(8,128)S(1)}, u32[]{:S(2)}, u32[]{:S(2)}) %collective-permute-start.31) | collective-permute-done | bytes 147488 | tf_op jit(solution)/shard_map/ppermute | solution.py:396
  74.9 1.4 %collective-permute-done.32.refs_3_ = f32[288,128]{1,0:T(8,128)S(1)} collective-permute-done((f32[288,128]{1,0:T(8,128)S(1)}, f32[288,128]{1,0:T(8,128)S(1)}, u32[]{:S(2)}, u32[]{:S(2)}) %collective-permute-start.32) | collective-permute-done | bytes 147488 | tf_op jit(solution)/shard_map/ppermute | solution.py:396
  76.2 1.6 %shard_map.91 = (f32[8,96,96]{2,1,0:T(8,128)S(1)}, f32[576,128]{1,0:T(8,128)S(1)}, f32[576,128]{1,0:T(8,128)S(1)}) custom-call(s32[2]{0:T(128)S(1)} %pad_add_fusion.scalars, f32[288,128]{1,0:T(8,128)S(1)} %get-tuple-element.90.refs_0_, f32[288,128]{1,0:T(8,128)S(1)} %collective-permute-done.30.refs_1_, f32[288,128]{1,0:T(8,128)S(1)} %collective-permute-done.31.refs_2_, ...), custom_call_target="tpu_custom_call" | custom-call | tf_op jit(solution)/shard_map/pallas_call | solution.py:384
  77.8 1.6 %collective-permute-start.35 = (f32[576,128]{1,0:T(8,128)S(1)}, f32[576,128]{1,0:T(8,128)S(1)}, u32[]{:S(2)}, u32[]{:S(2)}) collective-permute-start(f32[576,128]{1,0:T(8,128)S(1)} %get-tuple-element.97), channel_id=1, source_target_pairs={{0,4},{4,0},{8,12},{12,8},{16,20},{20,16},{24,28},{28,24},{1,5},{5... | collective-permute-start | bytes 884744 | tf_op jit(solution)/shard_map/ppermute | solution.py:495
  79.8 1.5 %collective-permute-start.11 = (f32[144,128]{1,0:T(8,128)S(1)}, f32[144,128]{1,0:T(8,128)S(1)}, u32[]{:S(2)}, u32[]{:S(2)}) collective-permute-start(f32[144,128]{1,0:T(8,128)S(1)} %get-tuple-element.67), channel_id=1, source_target_pairs={{0,2},{1,3},{2,0},{3,1},{4,6},{5,7},{6,4},{7,5},{8,10},{9,11},{10,... | collective-permute-start | bytes 221192 | tf_op jit(solution)/shard_map/ppermute | solution.py:396
  81.3 0.5 collective-permute-start.12
  81.9 1.4 %collective-permute-start.14 = (f32[288,128]{1,0:T(8,128)S(1)}, f32[288,128]{1,0:T(8,128)S(1)}, u32[]{:S(2)}, u32[]{:S(2)}) collective-permute-start(f32[288,128]{1,0:T(8,128)S(1)} %get-tuple-element.70), channel_id=1, source_target_pairs={{0,3},{1,2},{2,1},{3,0},{4,7},{5,6},{6,5},{7,4},{8,11},{9,10},{10,... | collective-permute-start | bytes 442376 | tf_op jit(solution)/shard_map/ppermute | solution.py:396
  83.2 1.0 collective-permute-done.11.refs_4_
  84.2 0.5 collective-permute-start.13
  84.7 7.2 %collective-permute-done.13.refs_6_ = f32[144,128]{1,0:T(8,128)S(1)} collective-permute-done((f32[144,128]{1,0:T(8,128)S(1)}, f32[144,128]{1,0:T(8,128)S(1)}, u32[]{:S(2)}, u32[]{:S(2)}) %collective-permute-start.13) | collective-permute-done | bytes 73760 | tf_op jit(solution)/shard_map/ppermute | solution.py:396
  92.2 0.5 collective-permute-start.34
  92.7 1.6 %collective-permute-start.37 = (f32[576,128]{1,0:T(8,128)S(1)}, f32[576,128]{1,0:T(8,128)S(1)}, u32[]{:S(2)}, u32[]{:S(2)}) collective-permute-start(f32[576,128]{1,0:T(8,128)S(1)} %get-tuple-element.99), channel_id=1, source_target_pairs={{0,8},{4,12},{8,16},{12,20},{16,24},{20,28},{24,0},{28,4},{1,9},{5... | collective-permute-start | bytes 884744 | tf_op jit(solution)/shard_map/ppermute | solution.py:494
  94.3 1.5 %collective-permute-start.33 = (f32[576,128]{1,0:T(8,128)S(1)}, f32[576,128]{1,0:T(8,128)S(1)}, u32[]{:S(2)}, u32[]{:S(2)}) collective-permute-start(f32[576,128]{1,0:T(8,128)S(1)} %get-tuple-element.95), channel_id=1, source_target_pairs={{0,4},{4,0},{8,12},{12,8},{16,20},{20,16},{24,28},{28,24},{1,5},{5... | collective-permute-start | bytes 884744 | tf_op jit(solution)/shard_map/ppermute | solution.py:495
  95.8 3.4 %collective-permute-start.36 = (f32[576,128]{1,0:T(8,128)S(1)}, f32[576,128]{1,0:T(8,128)S(1)}, u32[]{:S(2)}, u32[]{:S(2)}) collective-permute-start(f32[576,128]{1,0:T(8,128)S(1)} %get-tuple-element.98), channel_id=1, source_target_pairs={{0,8},{4,12},{8,16},{12,20},{16,24},{20,28},{24,0},{28,4},{1,9},{5... | collective-permute-start | bytes 884744 | tf_op jit(solution)/shard_map/ppermute | solution.py:494
  99.2 1.8 %shard_map.92.own_ref = f32[24,96,96]{2,1,0:T(8,128)S(1)} custom-call(s32[2]{0:T(128)S(1)} %pad_add_fusion.scalars, f32[144,128]{1,0:T(8,128)S(1)} %get-tuple-element.63.refs_15_.refs_0_, f32[288,128]{1,0:T(8,128)S(1)} %get-tuple-element.64.refs_1_, f32[144,128]{1,0:T(8,128)S(1)} %collective-permute-done.9.refs_2_, ...), custom_call_target="tpu_custom_call" | custom-call | tf_op jit(solution)/shard_map/pallas_call | solution.py:384
  100.9 2.9 %collective-permute-done.38.refs_5_ = f32[576,128]{1,0:T(8,128)S(1)} collective-permute-done((f32[576,128]{1,0:T(8,128)S(1)}, f32[576,128]{1,0:T(8,128)S(1)}, u32[]{:S(2)}, u32[]{:S(2)}) %collective-permute-start.38) | collective-permute-done | bytes 294944 | tf_op jit(solution)/shard_map/ppermute | solution.py:494
  103.8 6.3 %collective-permute-done.37.refs_4_ = f32[576,128]{1,0:T(8,128)S(1)} collective-permute-done((f32[576,128]{1,0:T(8,128)S(1)}, f32[576,128]{1,0:T(8,128)S(1)}, u32[]{:S(2)}, u32[]{:S(2)}) %collective-permute-start.37) | collective-permute-done | bytes 294944 | tf_op jit(solution)/shard_map/ppermute | solution.py:494
  110.2 5.9 %collective-permute-done.36.refs_3_ = f32[576,128]{1,0:T(8,128)S(1)} collective-permute-done((f32[576,128]{1,0:T(8,128)S(1)}, f32[576,128]{1,0:T(8,128)S(1)}, u32[]{:S(2)}, u32[]{:S(2)}) %collective-permute-start.36) | collective-permute-done | bytes 294944 | tf_op jit(solution)/shard_map/ppermute | solution.py:494
  116.1 1.9 %shard_map.93 = f32[24,96,96]{2,1,0:T(8,128)} custom-call(s32[2]{0:T(128)S(1)} %pad_add_fusion.scalars, f32[24,96,96]{2,1,0:T(8,128)S(1)} %shard_map.92.own_ref, f32[576,128]{1,0:T(8,128)S(1)} %collective-permute-done.33.refs_0_, f32[576,128]{1,0:T(8,128)S(1)} %collective-permute-done.34.refs_1_, f32[576,128]{1,0:T(8,128)S(1)} %collective-permute-done.35.refs_2_, ...), custom_call_target="tpu_custom_call" | custom-call | tf_op jit(solution)/shard_map/pallas_call | solution.py:384
  (47 shorter events, 1.8 us)
Async XLA Ops:
  0.0 26.5 %copy-start.8 = (f32[4,24,128]{2,1,0:T(8,128)S(1)}, f32[4,24,128]{2,1,0:T(8,128)}, u32[]{:S(2)}) copy-start(f32[4,24,128]{2,1,0:T(8,128)} %constant.43.clone.within_ref) | copy-start | bytes 147460
  0.1 1.3 %copy-start = (f32[1,24,96,96]{3,2,1,0:T(8,128)S(1)}, f32[1,24,96,96]{3,2,1,0:T(8,128)}, u32[]{:S(2)}) copy-start(f32[1,24,96,96]{3,2,1,0:T(8,128)} %param.8) | copy-start | bytes 2654212
  1.3 0.9 copy-start.2
  2.3 1.0 copy-start.4
  3.3 23.2 %copy-start.9 = (f32[96,128]{1,0:T(8,128)S(1)}, f32[96,128]{1,0:T(8,128)}, u32[]{:S(2)}) copy-start(f32[96,128]{1,0:T(8,128)} %constant.42.clone.across_ref) | copy-start | bytes 147460
  3.3 24.1 %copy-start.1 = (f32[1,24,96,96]{3,2,1,0:T(8,128)S(1)}, f32[1,24,96,96]{3,2,1,0:T(8,128)}, u32[]{:S(2)}) copy-start(f32[1,24,96,96]{3,2,1,0:T(8,128)} %param.8) | copy-start | bytes 2654212
  5.2 12.5 %collective-permute-start.6 = (f32[576,128]{1,0:T(8,128)S(1)}, f32[576,128]{1,0:T(8,128)S(1)}, u32[]{:S(2)}, u32[]{:S(2)}) collective-permute-start(f32[576,128]{1,0:T(8,128)S(1)} %get-tuple-element.58), channel_id=1, source_target_pairs={{0,24},{4,28},{8,0},{12,4},{16,8},{20,12},{24,16},{28,20},{1,25},{... | collective-permute-start | bytes 884744 | tf_op jit(solution)/shard_map/ppermute | solution.py:432
  10.3 9.9 %collective-permute-start.5 = (f32[576,128]{1,0:T(8,128)S(1)}, f32[576,128]{1,0:T(8,128)S(1)}, u32[]{:S(2)}, u32[]{:S(2)}) collective-permute-start(f32[576,128]{1,0:T(8,128)S(1)} %get-tuple-element.58), channel_id=1, source_target_pairs={{0,4},{4,0},{8,12},{12,8},{16,20},{20,16},{24,28},{28,24},{1,5},{5... | collective-permute-start | bytes 884744 | tf_op jit(solution)/shard_map/ppermute | solution.py:433
  11.8 12.2 %collective-permute-start.8 = (f32[576,128]{1,0:T(8,128)S(1)}, f32[576,128]{1,0:T(8,128)S(1)}, u32[]{:S(2)}, u32[]{:S(2)}) collective-permute-start(f32[576,128]{1,0:T(8,128)S(1)} %get-tuple-element.59), channel_id=1, source_target_pairs={{0,24},{4,28},{8,0},{12,4},{16,8},{20,12},{24,16},{28,20},{1,25},{... | collective-permute-start | bytes 884744 | tf_op jit(solution)/shard_map/ppermute | solution.py:432
  12.3 14.2 %collective-permute-start.7 = (f32[576,128]{1,0:T(8,128)S(1)}, f32[576,128]{1,0:T(8,128)S(1)}, u32[]{:S(2)}, u32[]{:S(2)}) collective-permute-start(f32[576,128]{1,0:T(8,128)S(1)} %get-tuple-element.59), channel_id=1, source_target_pairs={{0,4},{4,0},{8,12},{12,8},{16,20},{20,16},{24,28},{28,24},{1,5},{5... | collective-permute-start | bytes 884744 | tf_op jit(solution)/shard_map/ppermute | solution.py:433
  12.8 19.9 %collective-permute-start.4 = (f32[576,128]{1,0:T(8,128)S(1)}, f32[576,128]{1,0:T(8,128)S(1)}, u32[]{:S(2)}, u32[]{:S(2)}) collective-permute-start(f32[576,128]{1,0:T(8,128)S(1)} %get-tuple-element.57), channel_id=1, source_target_pairs={{0,24},{4,28},{8,0},{12,4},{16,8},{20,12},{24,16},{28,20},{1,25},{... | collective-permute-start | bytes 884744 | tf_op jit(solution)/shard_map/ppermute | solution.py:432
  17.7 15.9 %collective-permute-start.3 = (f32[576,128]{1,0:T(8,128)S(1)}, f32[576,128]{1,0:T(8,128)S(1)}, u32[]{:S(2)}, u32[]{:S(2)}) collective-permute-start(f32[576,128]{1,0:T(8,128)S(1)} %get-tuple-element.57), channel_id=1, source_target_pairs={{0,4},{4,0},{8,12},{12,8},{16,20},{20,16},{24,28},{28,24},{1,5},{5... | collective-permute-start | bytes 884744 | tf_op jit(solution)/shard_map/ppermute | solution.py:433
  20.2 10.3 %collective-permute-start = (f32[432,128]{1,0:T(8,128)S(1)}, f32[432,128]{1,0:T(8,128)S(1)}, u32[]{:S(2)}, u32[]{:S(2)}) collective-permute-start(f32[432,128]{1,0:T(8,128)S(1)} %get-tuple-element.54), channel_id=1, source_target_pairs={{0,1},{1,0},{2,3},{3,2},{4,5},{5,4},{6,7},{7,6},{8,9},{9,8},{10,11... | collective-permute-start | bytes 663560 | tf_op jit(solution)/shard_map/ppermute | solution.py:396
  24.0 8.1 %collective-permute-start.1 = (f32[432,128]{1,0:T(8,128)S(1)}, f32[432,128]{1,0:T(8,128)S(1)}, u32[]{:S(2)}, u32[]{:S(2)}) collective-permute-start(f32[432,128]{1,0:T(8,128)S(1)} %get-tuple-element.55), channel_id=1, source_target_pairs={{0,2},{1,3},{2,0},{3,1},{4,6},{5,7},{6,4},{7,5},{8,10},{9,11},{10,... | collective-permute-start | bytes 663560 | tf_op jit(solution)/shard_map/ppermute | solution.py:396
  26.5 9.3 %collective-permute-start.2 = (f32[432,128]{1,0:T(8,128)S(1)}, f32[432,128]{1,0:T(8,128)S(1)}, u32[]{:S(2)}, u32[]{:S(2)}) collective-permute-start(f32[432,128]{1,0:T(8,128)S(1)} %get-tuple-element.56), channel_id=1, source_target_pairs={{0,3},{1,2},{2,1},{3,0},{4,7},{5,6},{6,5},{7,4},{8,11},{9,10},{10,... | collective-permute-start | bytes 663560 | tf_op jit(solution)/shard_map/ppermute | solution.py:396
  30.5 6.0 %collective-permute-start.15 = (f32[288,128]{1,0:T(8,128)S(1)}, f32[288,128]{1,0:T(8,128)S(1)}, u32[]{:S(2)}, u32[]{:S(2)}) collective-permute-start(f32[288,128]{1,0:T(8,128)S(1)} %get-tuple-element.71), channel_id=1, source_target_pairs={{0,1},{1,0},{2,3},{3,2},{4,5},{5,4},{6,7},{7,6},{8,9},{9,8},{10,11... | collective-permute-start | bytes 442376 | tf_op jit(solution)/shard_map/ppermute | solution.py:396
  32.1 6.7 %collective-permute-start.18 = (f32[288,128]{1,0:T(8,128)S(1)}, f32[288,128]{1,0:T(8,128)S(1)}, u32[]{:S(2)}, u32[]{:S(2)}) collective-permute-start(f32[288,128]{1,0:T(8,128)S(1)} %get-tuple-element.74), channel_id=1, source_target_pairs={{0,2},{1,3},{2,0},{3,1},{4,6},{5,7},{6,4},{7,5},{8,10},{9,11},{10,... | collective-permute-start | bytes 442376 | tf_op jit(solution)/shard_map/ppermute | solution.py:396
  32.7 7.8 %collective-permute-start.21 = (f32[288,128]{1,0:T(8,128)S(1)}, f32[288,128]{1,0:T(8,128)S(1)}, u32[]{:S(2)}, u32[]{:S(2)}) collective-permute-start(f32[288,128]{1,0:T(8,128)S(1)} %get-tuple-element.77), channel_id=1, source_target_pairs={{0,3},{1,2},{2,1},{3,0},{4,7},{5,6},{6,5},{7,4},{8,11},{9,10},{10,... | collective-permute-start | bytes 442376 | tf_op jit(solution)/shard_map/ppermute | solution.py:396
  33.6 8.5 %collective-permute-start.16 = (f32[288,128]{1,0:T(8,128)S(1)}, f32[288,128]{1,0:T(8,128)S(1)}, u32[]{:S(2)}, u32[]{:S(2)}) collective-permute-start(f32[288,128]{1,0:T(8,128)S(1)} %get-tuple-element.72), channel_id=1, source_target_pairs={{0,1},{1,0},{2,3},{3,2},{4,5},{5,4},{6,7},{7,6},{8,9},{9,8},{10,11... | collective-permute-start | bytes 442376 | tf_op jit(solution)/shard_map/ppermute | solution.py:396
  34.3 8.9 %copy-start.6 = (bf16[4,192,192]{2,1,0:T(8,128)(2,1)S(1)}, bf16[4,192,192]{2,1,0:T(8,128)(2,1)}, u32[]{:S(2)}) copy-start(bf16[4,192,192]{2,1,0:T(8,128)(2,1)} %constant.41.clone.refs_6_.refs_14_) | copy-start | bytes 884740
  34.3 8.9 %copy-start.7 = (bf16[4,192,192]{2,1,0:T(8,128)(2,1)S(1)}, bf16[4,192,192]{2,1,0:T(8,128)(2,1)}, u32[]{:S(2)}) copy-start(bf16[4,192,192]{2,1,0:T(8,128)(2,1)} %constant.40.clone.refs_5_.refs_13_) | copy-start | bytes 884740
  35.8 9.4 %collective-permute-start.19 = (f32[288,128]{1,0:T(8,128)S(1)}, f32[288,128]{1,0:T(8,128)S(1)}, u32[]{:S(2)}, u32[]{:S(2)}) collective-permute-start(f32[288,128]{1,0:T(8,128)S(1)} %get-tuple-element.75), channel_id=1, source_target_pairs={{0,2},{1,3},{2,0},{3,1},{4,6},{5,7},{6,4},{7,5},{8,10},{9,11},{10,... | collective-permute-start | bytes 442376 | tf_op jit(solution)/shard_map/ppermute | solution.py:396
  36.4 10.4 %collective-permute-start.22 = (f32[288,128]{1,0:T(8,128)S(1)}, f32[288,128]{1,0:T(8,128)S(1)}, u32[]{:S(2)}, u32[]{:S(2)}) collective-permute-start(f32[288,128]{1,0:T(8,128)S(1)} %get-tuple-element.78), channel_id=1, source_target_pairs={{0,3},{1,2},{2,1},{3,0},{4,7},{5,6},{6,5},{7,4},{8,11},{9,10},{10,... | collective-permute-start | bytes 442376 | tf_op jit(solution)/shard_map/ppermute | solution.py:396
  38.8 8.0 %collective-permute-start.17 = (f32[288,128]{1,0:T(8,128)S(1)}, f32[288,128]{1,0:T(8,128)S(1)}, u32[]{:S(2)}, u32[]{:S(2)}) collective-permute-start(f32[288,128]{1,0:T(8,128)S(1)} %get-tuple-element.73), channel_id=1, source_target_pairs={{0,1},{1,0},{2,3},{3,2},{4,5},{5,4},{6,7},{7,6},{8,9},{9,8},{10,11... | collective-permute-start | bytes 442376 | tf_op jit(solution)/shard_map/ppermute | solution.py:396
  40.5 11.0 %collective-permute-start.20 = (f32[288,128]{1,0:T(8,128)S(1)}, f32[288,128]{1,0:T(8,128)S(1)}, u32[]{:S(2)}, u32[]{:S(2)}) collective-permute-start(f32[288,128]{1,0:T(8,128)S(1)} %get-tuple-element.76), channel_id=1, source_target_pairs={{0,2},{1,3},{2,0},{3,1},{4,6},{5,7},{6,4},{7,5},{8,10},{9,11},{10,... | collective-permute-start | bytes 442376 | tf_op jit(solution)/shard_map/ppermute | solution.py:396
  42.0 10.8 %collective-permute-start.23 = (f32[288,128]{1,0:T(8,128)S(1)}, f32[288,128]{1,0:T(8,128)S(1)}, u32[]{:S(2)}, u32[]{:S(2)}) collective-permute-start(f32[288,128]{1,0:T(8,128)S(1)} %get-tuple-element.79), channel_id=1, source_target_pairs={{0,3},{1,2},{2,1},{3,0},{4,7},{5,6},{6,5},{7,4},{8,11},{9,10},{10,... | collective-permute-start | bytes 442376 | tf_op jit(solution)/shard_map/ppermute | solution.py:396
  52.9 13.7 %copy-start.3 = (bf16[256,256]{1,0:T(8,128)(2,1)S(1)}, bf16[256,256]{1,0:T(8,128)(2,1)}, u32[]{:S(2)}) copy-start(bf16[256,256]{1,0:T(8,128)(2,1)} %constant.37.clone.tz_ref.refs_7_.refs_12_) | copy-start | bytes 393220
  52.9 13.7 %copy-start.5 = (bf16[4,192,256]{2,1,0:T(8,128)(2,1)S(1)}, bf16[4,192,256]{2,1,0:T(8,128)(2,1)}, u32[]{:S(2)}) copy-start(bf16[4,192,256]{2,1,0:T(8,128)(2,1)} %constant.39.clone.refs_8_.refs_13_) | copy-start | bytes 1179652
  54.7 4.3 %collective-permute-start.24 = (f32[288,128]{1,0:T(8,128)S(1)}, f32[288,128]{1,0:T(8,128)S(1)}, u32[]{:S(2)}, u32[]{:S(2)}) collective-permute-start(f32[288,128]{1,0:T(8,128)S(1)} %get-tuple-element.81), channel_id=1, source_target_pairs={{0,1},{1,0},{2,3},{3,2},{4,5},{5,4},{6,7},{7,6},{8,9},{9,8},{10,11... | collective-permute-start | bytes 442376 | tf_op jit(solution)/shard_map/ppermute | solution.py:396
  55.5 6.7 %collective-permute-start.25 = (f32[288,128]{1,0:T(8,128)S(1)}, f32[288,128]{1,0:T(8,128)S(1)}, u32[]{:S(2)}, u32[]{:S(2)}) collective-permute-start(f32[288,128]{1,0:T(8,128)S(1)} %get-tuple-element.82), channel_id=1, source_target_pairs={{0,2},{1,3},{2,0},{3,1},{4,6},{5,7},{6,4},{7,5},{8,10},{9,11},{10,... | collective-permute-start | bytes 442376 | tf_op jit(solution)/shard_map/ppermute | solution.py:396
  56.9 7.4 %collective-permute-start.26 = (f32[288,128]{1,0:T(8,128)S(1)}, f32[288,128]{1,0:T(8,128)S(1)}, u32[]{:S(2)}, u32[]{:S(2)}) collective-permute-start(f32[288,128]{1,0:T(8,128)S(1)} %get-tuple-element.83), channel_id=1, source_target_pairs={{0,3},{1,2},{2,1},{3,0},{4,7},{5,6},{6,5},{7,4},{8,11},{9,10},{10,... | collective-permute-start | bytes 442376 | tf_op jit(solution)/shard_map/ppermute | solution.py:396
  56.9 8.3 %collective-permute-start.27 = (f32[288,128]{1,0:T(8,128)S(1)}, f32[288,128]{1,0:T(8,128)S(1)}, u32[]{:S(2)}, u32[]{:S(2)}) collective-permute-start(f32[288,128]{1,0:T(8,128)S(1)} %get-tuple-element.86), channel_id=1, source_target_pairs={{0,1},{1,0},{2,3},{3,2},{4,5},{5,4},{6,7},{7,6},{8,9},{9,8},{10,11... | collective-permute-start | bytes 442376 | tf_op jit(solution)/shard_map/ppermute | solution.py:396
  57.6 10.9 %collective-permute-start.28 = (f32[288,128]{1,0:T(8,128)S(1)}, f32[288,128]{1,0:T(8,128)S(1)}, u32[]{:S(2)}, u32[]{:S(2)}) collective-permute-start(f32[288,128]{1,0:T(8,128)S(1)} %get-tuple-element.87), channel_id=1, source_target_pairs={{0,2},{1,3},{2,0},{3,1},{4,6},{5,7},{6,4},{7,5},{8,10},{9,11},{10,... | collective-permute-start | bytes 442376 | tf_op jit(solution)/shard_map/ppermute | solution.py:396
  59.0 11.6 %collective-permute-start.29 = (f32[288,128]{1,0:T(8,128)S(1)}, f32[288,128]{1,0:T(8,128)S(1)}, u32[]{:S(2)}, u32[]{:S(2)}) collective-permute-start(f32[288,128]{1,0:T(8,128)S(1)} %get-tuple-element.88), channel_id=1, source_target_pairs={{0,3},{1,2},{2,1},{3,0},{4,7},{5,6},{6,5},{7,4},{8,11},{9,10},{10,... | collective-permute-start | bytes 442376 | tf_op jit(solution)/shard_map/ppermute | solution.py:396
  62.2 9.9 %collective-permute-start.30 = (f32[288,128]{1,0:T(8,128)S(1)}, f32[288,128]{1,0:T(8,128)S(1)}, u32[]{:S(2)}, u32[]{:S(2)}) collective-permute-start(f32[288,128]{1,0:T(8,128)S(1)} %get-tuple-element.91), channel_id=1, source_target_pairs={{0,1},{1,0},{2,3},{3,2},{4,5},{5,4},{6,7},{7,6},{8,9},{9,8},{10,11... | collective-permute-start | bytes 442376 | tf_op jit(solution)/shard_map/ppermute | solution.py:396
  64.3 10.6 %collective-permute-start.31 = (f32[288,128]{1,0:T(8,128)S(1)}, f32[288,128]{1,0:T(8,128)S(1)}, u32[]{:S(2)}, u32[]{:S(2)}) collective-permute-start(f32[288,128]{1,0:T(8,128)S(1)} %get-tuple-element.92), channel_id=1, source_target_pairs={{0,2},{1,3},{2,0},{3,1},{4,6},{5,7},{6,4},{7,5},{8,10},{9,11},{10,... | collective-permute-start | bytes 442376 | tf_op jit(solution)/shard_map/ppermute | solution.py:396
  65.3 11.0 %collective-permute-start.32 = (f32[288,128]{1,0:T(8,128)S(1)}, f32[288,128]{1,0:T(8,128)S(1)}, u32[]{:S(2)}, u32[]{:S(2)}) collective-permute-start(f32[288,128]{1,0:T(8,128)S(1)} %get-tuple-element.93), channel_id=1, source_target_pairs={{0,3},{1,2},{2,1},{3,0},{4,7},{5,6},{6,5},{7,4},{8,11},{9,10},{10,... | collective-permute-start | bytes 442376 | tf_op jit(solution)/shard_map/ppermute | solution.py:396
  77.8 18.0 %collective-permute-start.35 = (f32[576,128]{1,0:T(8,128)S(1)}, f32[576,128]{1,0:T(8,128)S(1)}, u32[]{:S(2)}, u32[]{:S(2)}) collective-permute-start(f32[576,128]{1,0:T(8,128)S(1)} %get-tuple-element.97), channel_id=1, source_target_pairs={{0,4},{4,0},{8,12},{12,8},{16,20},{20,16},{24,28},{28,24},{1,5},{5... | collective-permute-start | bytes 884744 | tf_op jit(solution)/shard_map/ppermute | solution.py:495
  79.4 2.5 %collective-permute-start.9 = (f32[144,128]{1,0:T(8,128)S(1)}, f32[144,128]{1,0:T(8,128)S(1)}, u32[]{:S(2)}, u32[]{:S(2)}) collective-permute-start(f32[144,128]{1,0:T(8,128)S(1)} %get-tuple-element.65), channel_id=1, source_target_pairs={{0,1},{1,0},{2,3},{3,2},{4,5},{5,4},{6,7},{7,6},{8,9},{9,8},{10,11... | collective-permute-start | bytes 221192 | tf_op jit(solution)/shard_map/ppermute | solution.py:396
  79.8 4.4 %collective-permute-start.11 = (f32[144,128]{1,0:T(8,128)S(1)}, f32[144,128]{1,0:T(8,128)S(1)}, u32[]{:S(2)}, u32[]{:S(2)}) collective-permute-start(f32[144,128]{1,0:T(8,128)S(1)} %get-tuple-element.67), channel_id=1, source_target_pairs={{0,2},{1,3},{2,0},{3,1},{4,6},{5,7},{6,4},{7,5},{8,10},{9,11},{10,... | collective-permute-start | bytes 221192 | tf_op jit(solution)/shard_map/ppermute | solution.py:396
  81.3 10.8 %collective-permute-start.10 = (f32[288,128]{1,0:T(8,128)S(1)}, f32[288,128]{1,0:T(8,128)S(1)}, u32[]{:S(2)}, u32[]{:S(2)}) collective-permute-start(f32[288,128]{1,0:T(8,128)S(1)} %get-tuple-element.66), channel_id=1, source_target_pairs={{0,1},{1,0},{2,3},{3,2},{4,5},{5,4},{6,7},{7,6},{8,9},{9,8},{10,11... | collective-permute-start | bytes 442376 | tf_op jit(solution)/shard_map/ppermute | solution.py:396
  81.3 11.3 %collective-permute-start.12 = (f32[288,128]{1,0:T(8,128)S(1)}, f32[288,128]{1,0:T(8,128)S(1)}, u32[]{:S(2)}, u32[]{:S(2)}) collective-permute-start(f32[288,128]{1,0:T(8,128)S(1)} %get-tuple-element.68), channel_id=1, source_target_pairs={{0,2},{1,3},{2,0},{3,1},{4,6},{5,7},{6,4},{7,5},{8,10},{9,11},{10,... | collective-permute-start | bytes 442376 | tf_op jit(solution)/shard_map/ppermute | solution.py:396
  81.9 12.4 %collective-permute-start.14 = (f32[288,128]{1,0:T(8,128)S(1)}, f32[288,128]{1,0:T(8,128)S(1)}, u32[]{:S(2)}, u32[]{:S(2)}) collective-permute-start(f32[288,128]{1,0:T(8,128)S(1)} %get-tuple-element.70), channel_id=1, source_target_pairs={{0,3},{1,2},{2,1},{3,0},{4,7},{5,6},{6,5},{7,4},{8,11},{9,10},{10,... | collective-permute-start | bytes 442376 | tf_op jit(solution)/shard_map/ppermute | solution.py:396
  84.2 7.7 %collective-permute-start.13 = (f32[144,128]{1,0:T(8,128)S(1)}, f32[144,128]{1,0:T(8,128)S(1)}, u32[]{:S(2)}, u32[]{:S(2)}) collective-permute-start(f32[144,128]{1,0:T(8,128)S(1)} %get-tuple-element.69), channel_id=1, source_target_pairs={{0,3},{1,2},{2,1},{3,0},{4,7},{5,6},{6,5},{7,4},{8,11},{9,10},{10,... | collective-permute-start | bytes 221192 | tf_op jit(solution)/shard_map/ppermute | solution.py:396
  91.9 12.0 %collective-permute-start.38 = (f32[576,128]{1,0:T(8,128)S(1)}, f32[576,128]{1,0:T(8,128)S(1)}, u32[]{:S(2)}, u32[]{:S(2)}) collective-permute-start(f32[576,128]{1,0:T(8,128)S(1)} %get-tuple-element.100), channel_id=1, source_target_pairs={{0,8},{4,12},{8,16},{12,20},{16,24},{20,28},{24,0},{28,4},{1,9},{5... | collective-permute-start | bytes 884744 | tf_op jit(solution)/shard_map/ppermute | solution.py:494
  92.2 11.7 %collective-permute-start.34 = (f32[576,128]{1,0:T(8,128)S(1)}, f32[576,128]{1,0:T(8,128)S(1)}, u32[]{:S(2)}, u32[]{:S(2)}) collective-permute-start(f32[576,128]{1,0:T(8,128)S(1)} %get-tuple-element.96), channel_id=1, source_target_pairs={{0,4},{4,0},{8,12},{12,8},{16,20},{20,16},{24,28},{28,24},{1,5},{5... | collective-permute-start | bytes 884744 | tf_op jit(solution)/shard_map/ppermute | solution.py:495
  92.7 17.5 %collective-permute-start.37 = (f32[576,128]{1,0:T(8,128)S(1)}, f32[576,128]{1,0:T(8,128)S(1)}, u32[]{:S(2)}, u32[]{:S(2)}) collective-permute-start(f32[576,128]{1,0:T(8,128)S(1)} %get-tuple-element.99), channel_id=1, source_target_pairs={{0,8},{4,12},{8,16},{12,20},{16,24},{20,28},{24,0},{28,4},{1,9},{5... | collective-permute-start | bytes 884744 | tf_op jit(solution)/shard_map/ppermute | solution.py:494
  94.3 15.9 %collective-permute-start.33 = (f32[576,128]{1,0:T(8,128)S(1)}, f32[576,128]{1,0:T(8,128)S(1)}, u32[]{:S(2)}, u32[]{:S(2)}) collective-permute-start(f32[576,128]{1,0:T(8,128)S(1)} %get-tuple-element.95), channel_id=1, source_target_pairs={{0,4},{4,0},{8,12},{12,8},{16,20},{20,16},{24,28},{28,24},{1,5},{5... | collective-permute-start | bytes 884744 | tf_op jit(solution)/shard_map/ppermute | solution.py:495
  95.8 20.3 %collective-permute-start.36 = (f32[576,128]{1,0:T(8,128)S(1)}, f32[576,128]{1,0:T(8,128)S(1)}, u32[]{:S(2)}, u32[]{:S(2)}) collective-permute-start(f32[576,128]{1,0:T(8,128)S(1)} %get-tuple-element.98), channel_id=1, source_target_pairs={{0,8},{4,12},{8,16},{12,20},{16,24},{20,28},{24,0},{28,4},{1,9},{5... | collective-permute-start | bytes 884744 | tf_op jit(solution)/shard_map/ppermute | solution.py:494

commit v2 on v1

--- a/solution.py
+++ b/solution.py
@@ -52,6 +52,7 @@
         self.rows = 3 * self.extra
         assert self.extra <= 8
         self.block = self.rows * planes
+        self.packed = 3 * height // 4
 
     def table_z(self):
         high, low = halves(cas(np.arange(self.breadth), np.arange(self.breadth), self.breadth))
@@ -168,10 +169,6 @@
     return jnp.concatenate(
         [value, thirds([value[t * h : (t + 1) * h] for t in range(3)], plan)], axis=0
     )
-
-
-def clear(wide, plan):
-    return jnp.where(lanes(wide.shape) < plan.breadth, wide, 0.0)
 
 
 def store_spectrum(plan, density, tz, ty, outs, base, stride, plane):
@@ -218,41 +215,44 @@
 CHUNK = 8
 
 
-def forward_own_kernel(plan, scalars, own_ref, tz_ref, ty_ref, *outs):
-    blocks, chunks = outs[: plan.parts], outs[plan.parts :]
+def pack_kernel(plan, scalars, own_ref, out):
+    for i in range(CHUNK):
+        out[i * plan.packed : (i + 1) * plan.packed, :] = pack(widen(own_ref[i]), plan)
+
+
+def unpack_chunk(value, plan):
+    return jnp.concatenate(
+        [unpack(value[i * plan.packed : (i + 1) * plan.packed], plan) for i in range(CHUNK)],
+        axis=0,
+    )
+
+
+def pack_chunk(wide, plan):
     h = plan.height
-    packed_rows = 3 * h // 4
-    for c, chunk in enumerate(chunks):
-        own = own_ref[c * CHUNK : (c + 1) * CHUNK].reshape(CHUNK * h, plan.breadth)
-        wide = widen(own)
-        for i in range(CHUNK):
-            chunk[i * packed_rows : (i + 1) * packed_rows, :] = pack(
-                wide[i * h : (i + 1) * h], plan
-            )
-        store_spectrum(plan, wide * wide, tz_ref[...], ty_ref[0], blocks, 0, plan.planes, c * CHUNK)
-
-
-def load_packed(ref, plan):
-    packed_rows = 3 * plan.height // 4
     return jnp.concatenate(
-        [unpack(ref[i * packed_rows : (i + 1) * packed_rows, :], plan) for i in range(CHUNK)],
-        axis=0,
-    )
-
-
-def load_own(ref, plan):
-    return widen(ref[...].reshape(CHUNK * plan.height, plan.breadth))
-
-
-def forward_pair_kernel(plan, scalars, own_ref, q_ref, r_ref, tz_ref, ty_ref, after_ref, *outs):
+        [pack(wide[i * h : (i + 1) * h], plan) for i in range(CHUNK)], axis=0
+    )
+
+
+def forward_own_kernel(plan, scalars, own_ref, tz_ref, ty_ref, after_ref, *outs):
+    blocks, later = outs[: plan.parts], outs[plan.parts :]
+    for c in range(plan.planes // CHUNK):
+        here = slice(c * CHUNK, (c + 1) * CHUNK)
+        wide = widen(own_ref[here].reshape(CHUNK * plan.height, plan.breadth))
+        if c:
+            later[c - 1][...] = pack_chunk(wide, plan)
+        store_spectrum(
+            plan, wide * wide, tz_ref[...], ty_ref[0], blocks, 0, plan.planes, c * CHUNK
+        )
+
+
+def forward_pair_kernel(plan, scalars, p_ref, q_ref, r_ref, tz_ref, ty_ref, after_ref, *outs):
     even = scalars[1] == 1
-    p = load_own(own_ref, plan)
-    r = load_packed(r_ref, plan)
+    p, r = p_ref[...], r_ref[...]
     tz, ty = tz_ref[...], ty_ref[0]
-    store_spectrum(plan, p * r, tz, ty, outs, 0, CHUNK, 0)
-    q = load_packed(q_ref, plan)
-    mixed = clear(q * jnp.where(even, r, p), plan)
-    store_spectrum(plan, mixed, tz, ty, outs, plan.rows * CHUNK, CHUNK, 0)
+    store_spectrum(plan, unpack_chunk(p * r, plan), tz, ty, outs, 0, CHUNK, 0)
+    mixed = q_ref[...] * jnp.where(even, r, p)
+    store_spectrum(plan, unpack_chunk(mixed, plan), tz, ty, outs, plan.rows * CHUNK, CHUNK, 0)
 
 
 def screen_kernel(plan, scalars, across_ref, within_ref, after_ref, out_ref):
@@ -310,60 +310,48 @@
 def backward_pair_kernel(plan, scalars, *refs):
     n = plan.parts
     ins, refs = refs[:n], refs[n:]
-    own_ref, q_ref, r_ref, tz_ref, ty_ref, _, total_ref, y_ref, z_ref = refs
+    p_ref, q_ref, r_ref, tz_ref, ty_ref, _, total_ref, y_ref, z_ref = refs
     even = scalars[1] == 1
-    h = plan.height
     tz, ty = tz_ref[...], ty_ref[0]
-    visit = load_potential(plan, ins, 0, CHUNK, 0, tz, ty)
-    mixed = load_potential(plan, ins, plan.rows * CHUNK, CHUNK, 0, tz, ty)
-    p = load_own(own_ref, plan)
-    r = load_packed(r_ref, plan)
-    q = load_packed(q_ref, plan)
-    other = mixed * q
+    visit = pack_chunk(load_potential(plan, ins, 0, CHUNK, 0, tz, ty), plan)
+    mixed = pack_chunk(load_potential(plan, ins, plan.rows * CHUNK, CHUNK, 0, tz, ty), plan)
+    p, r = p_ref[...], r_ref[...]
+    other = mixed * q_ref[...]
     zero = jnp.zeros_like(other)
-    total = visit * r + jnp.where(even, zero, other)
-    total_ref[...] = total[:, : plan.breadth].reshape(CHUNK, h, plan.breadth)
-    to_z = visit * p + jnp.where(even, other, zero)
-    to_y = mixed * jnp.where(even, r, p)
-    packed_rows = 3 * h // 4
+    y_ref[...] = mixed * jnp.where(even, r, p)
+    z_ref[...] = visit * p + jnp.where(even, other, zero)
+    total_ref[...] = visit * r + jnp.where(even, zero, other)
+
+
+def store_result(out_ref, first, value, plan):
     for i in range(CHUNK):
-        rows = slice(i * packed_rows, (i + 1) * packed_rows)
-        y_ref[rows, :] = pack(to_y[i * h : (i + 1) * h], plan)
-        z_ref[rows, :] = pack(to_z[i * h : (i + 1) * h], plan)
-
-
-def backward_own_kernel(plan, sizes, scalars, *refs):
-    n, m = plan.parts, len(sizes)
-    ins = [refs[k * m : (k + 1) * m] for k in range(n)]
-    refs = refs[n * m :]
+        wide = unpack(value[i * plan.packed : (i + 1) * plan.packed], plan)
+        out_ref[first + i] = wide[:, : plan.breadth]
+
+
+def backward_own_kernel(plan, scalars, *refs):
+    n = plan.parts
+    ins, refs = refs[:n], refs[n:]
     chunks = plan.planes // CHUNK
     totals, refs = refs[:chunks], refs[chunks:]
-    own_ref, tz_ref, ty_ref, _, out_ref = refs
+    owns, refs = refs[:chunks], refs[chunks:]
+    returned, refs = refs[: 2 * (chunks - 1)], refs[2 * (chunks - 1) :]
+    tz_ref, ty_ref, _, out_ref, rest_ref = refs
     for c in range(chunks):
-        at, piece = c * CHUNK, 0
-        while at >= sizes[piece]:
-            at -= sizes[piece]
-            piece += 1
-        value = load_potential(
-            plan, [ins[k][piece] for k in range(n)], 0, sizes[piece], at, tz_ref[...], ty_ref[0]
-        )
-        value = value[:, : plan.breadth].reshape(CHUNK, plan.height, plan.breadth)
-        here = slice(c * CHUNK, (c + 1) * CHUNK)
-        out_ref[here] = totals[c][...] + value * own_ref[here]
-
-
-def final_kernel(plan, scalars, own_ref, *refs):
-    chunks = plan.planes // CHUNK
-    ys, zs, out_ref = refs[:chunks], refs[chunks : 2 * chunks], refs[-1]
-    packed_rows = 3 * plan.height // 4
-    for c in range(chunks):
-        for i in range(CHUNK):
-            rows = slice(i * packed_rows, (i + 1) * packed_rows)
-            returned = unpack(ys[c][rows, :] + zs[c][rows, :], plan)
-            out_ref[c * CHUNK + i] = own_ref[c * CHUNK + i] + returned[:, : plan.breadth]
-
-
-def call(kernel, scalars, operands, outs, selected=(), chunk=None, after=None):
+        value = load_potential(plan, ins, 0, plan.planes, c * CHUNK, tz_ref[...], ty_ref[0])
+        value = pack_chunk(value, plan) * owns[c][...] + totals[c][...]
+        if c < chunks - 1:
+            value = value + returned[2 * c][...] + returned[2 * c + 1][...]
+            store_result(out_ref, c * CHUNK, value, plan)
+        else:
+            rest_ref[...] = value
+
+
+def final_kernel(plan, scalars, partial_ref, rest_ref, y_ref, z_ref, out_ref):
+    store_result(out_ref, 0, rest_ref[...] + y_ref[...] + z_ref[...], plan)
+
+
+def call(kernel, scalars, operands, outs, selected=(), chunk=None, after=None, update=None):
     specs = []
     for operand in operands:
         if any(operand is s for s in selected):
@@ -381,11 +369,22 @@
         operands = (*operands, after)
         specs.append(pl.BlockSpec(memory_space=pl.ANY))
     out_specs = [pl.BlockSpec(o, lambda i, s, zeros=(0,) * len(o): zeros) for o in outs]
+    aliases = {}
+    if update is not None:
+        specs[0] = pl.BlockSpec(memory_space=pl.ANY)
+        out_specs = [
+            pl.BlockSpec((CHUNK,) + o[1:], lambda i, s, c=update: (c, 0, 0)) for o in outs
+        ]
+        aliases = {1: 0}
     return pl.pallas_call(
         kernel,
         grid_spec=pltpu.PrefetchScalarGridSpec(
-            num_scalar_prefetch=1, grid=(1,), in_specs=specs, out_specs=out_specs
+            num_scalar_prefetch=1,
+            grid=(1,),
+            in_specs=specs,
+            out_specs=out_specs,
         ),
+        input_output_aliases=aliases,
         out_shape=[jax.ShapeDtypeStruct(o, F32) for o in outs],
         compiler_params=pltpu.CompilerParams(vmem_limit_bytes=48 * 1024 * 1024),
     )(scalars, *operands)
@@ -415,22 +414,29 @@
     across, within = (jnp.asarray(t) for t in plan.waves())
     chunks = plan.planes // CHUNK
     whole = own.shape
-    packed = (CHUNK * 3 * plan.height // 4, LANES)
-    sizes = (CHUNK, plan.planes - CHUNK)
-
-    *blocks, = call(
+    packed = (CHUNK * plan.packed, LANES)
+    sizes = (plan.planes,)
+
+    (first,) = call(functools.partial(pack_kernel, plan), scalars, (own,), [packed], chunk=(own, 0))
+    q, r = [], []
+
+    def shift(chunk):
+        q.append(lax.ppermute(chunk, "band", swap))
+        r.append(lax.ppermute(chunk, "band", behind))
+
+    shift(first)
+    out = call(
         functools.partial(forward_own_kernel, plan),
         scalars,
         (own, tz, ty_forward),
-        [(plan.block, LANES)] * parts + [packed] * chunks,
+        [(plan.block, LANES)] * parts + [packed] * (chunks - 1),
         (ty_forward,),
-    )
-    blocks, mine = blocks[:parts], blocks[parts:]
+        after=first,
+    )
+    blocks, mine = out[:parts], [first, *out[parts:]]
     own_in = exchange(blocks, parts)
-    q, r = [], []
-    for chunk in mine:
-        r.append(lax.ppermute(chunk, "band", behind))
-        q.append(lax.ppermute(chunk, "band", swap))
+    for c in range(1, chunks):
+        shift(mine[c])
     (screen,) = call(
         functools.partial(screen_kernel, plan),
         scalars,
@@ -445,11 +451,10 @@
         out = call(
             functools.partial(forward_pair_kernel, plan),
             scalars,
-            (own, q[c], r[c], tz, ty_forward),
+            (mine[c], q[c], r[c], tz, ty_forward),
             [(2 * plan.rows * CHUNK, LANES)] * parts,
             (ty_forward,),
-            (own, c),
-            after,
+            after=after,
         )
         after = out[0]
         pair_in.append(exchange(out, parts))
@@ -466,7 +471,6 @@
         return [out[i :: len(sizes_out)] for i in range(len(sizes_out))]
 
     own_mid = middle([[b] for b in own_in], (plan.planes,), sizes, 1, after)
-    own_back = [exchange(own_mid[0], parts)]
     even_chunks = (CHUNK,) * chunks
     pair_mid = middle(
         [[pair_in[c][k] for c in range(chunks)] for k in range(parts)],
@@ -476,33 +480,43 @@
         own_mid[0][0],
     )
     pair_back = [exchange(blocks, parts) for blocks in pair_mid]
-    own_back.append(exchange(own_mid[1], parts))
+    own_back = exchange(own_mid[0], parts)
     after = pair_mid[0][0]
     totals, from_y, from_z = [], [], []
     for c in range(chunks):
         total, y, z = call(
             functools.partial(backward_pair_kernel, plan),
             scalars,
-            (*pair_back[c], own, q[c], r[c], tz, ty_backward),
-            [(CHUNK,) + whole[1:], packed, packed],
+            (*pair_back[c], mine[c], q[c], r[c], tz, ty_backward),
+            [packed] * 3,
             (ty_backward,),
-            (own, c),
-            after,
+            after=after,
         )
         after = total
         totals.append(total)
         from_z.append(lax.ppermute(z, "band", ahead))
         from_y.append(lax.ppermute(y, "band", swap))
-    (total,) = call(
-        functools.partial(backward_own_kernel, plan, sizes),
+    partial, rest = call(
+        functools.partial(backward_own_kernel, plan),
         scalars,
-        (*[own_back[i][k] for k in range(parts) for i in range(2)], *totals, own, tz, ty_backward),
-        [whole],
+        (
+            *own_back,
+            *totals,
+            *mine,
+            *[part[c] for c in range(chunks - 1) for part in (from_y, from_z)],
+            tz,
+            ty_backward,
+        ),
+        [whole, packed],
         (ty_backward,),
         after=after,
     )
     (result,) = call(
-        functools.partial(final_kernel, plan), scalars, (total, *from_y, *from_z), [whole]
+        functools.partial(final_kernel, plan),
+        scalars,
+        (partial, rest, from_y[-1], from_z[-1]),
+        [whole],
+        update=chunks - 1,
     )
     return result[None]
 

time: 118 us -> 112 us (0.949)
  waiting for transfers between devices: 56.9 us -> 53 us
  local copies, waits for them, and re-layouts: 3.24 us -> 1.37 us
  starting transfers between devices: 38.8 us -> 37.1 us
    ppermute x3, waiting for transfers between devices: 15.1 us -> 12.9 us  [exchange_term(): from_z.append(lax.ppermute(z, 'band', ahead))]
    ppermute x27 -> x24, starting transfers between devices: 20.4 us -> 18.5 us  [exchange(): lax.ppermute(blocks[k], 'grid', [(i, i ^ k) for i in range(parts)])]
    ppermute x6, waiting for transfers between devices: 10.3 us -> 8.36 us  [the longest x3 6.41 us: shift(): r.append(lax.ppermute(chunk, 'band', behind))]
    unnamed x20 -> x16, local copies, waits for them, and re-layouts: 3.24 us -> 1.37 us
    pallas_call x12 -> x13, Pallas kernels: 18.8 us -> 19.8 us  [call(): pl.pallas_call(kernel, grid_spec=pltpu.PrefetchScalarGridSpec(num_scalar_...]
    ppermute x27 -> x24, waiting for transfers between devices: 31.5 us -> 31.8 us  [exchange(): lax.ppermute(blocks[k], 'grid', [(i, i ^ k) for i in range(parts)])]
  transfers between devices with their start and end apart: 39 -> 36, of which waited for: 21 -> 18; matrix products, arithmetic and copies ran while one was open for 0% -> 0% of each run, Pallas kernels for 10% -> 14%
where the time goes in v2:
time: 112 us
  waiting for transfers between devices  53 us (47%)
  starting transfers between devices  37.1 us (33%)
  Pallas kernels  19.8 us (18%)
  local copies, waits for them, and re-layouts  1.37 us (1%)
    ppermute x24, waiting for transfers between devices, exchange(): lax.ppermute(blocks[k], 'grid', [(i, i ^ k) for i in range(parts)])  31.8 us
    pallas_call x13, Pallas kernels, call(): pl.pallas_call(kernel, grid_spec=pltpu.PrefetchScalarGridSpec(num_scalar_...  19.8 us
    ppermute x24, starting transfers between devices, exchange(): lax.ppermute(blocks[k], 'grid', [(i, i ^ k) for i in range(parts)])  18.5 us
    ppermute x3, waiting for transfers between devices, exchange_term(): from_z.append(lax.ppermute(z, 'band', ahead))  12.9 us
    ppermute x3, waiting for transfers between devices, shift(): r.append(lax.ppermute(chunk, 'band', behind))  6.41 us
    ppermute x3, starting transfers between devices, shift(): r.append(lax.ppermute(chunk, 'band', behind))  6.08 us
    ppermute x3, starting transfers between devices, exchange_term(): from_z.append(lax.ppermute(z, 'band', ahead))  5.33 us
    ppermute x3, starting transfers between devices, exchange_term(): from_y.append(lax.ppermute(y, 'band', swap))  3.69 us
  transfers between devices with their start and end apart: 36, of which 18 were waited for; matrix products, arithmetic and copies ran while one was open for 0% of the time, Pallas kernels for 14%

profile of v2, /device:TPU:0, one launch (start us, length us, event | category | flops | bytes accessed | tf_op | source)
XLA Modules:
  0.0 111.6 jit_solution(5409456603364504866)
XLA Ops:
  0.0 0.1 pad_add_fusion.scalars
  0.1 1.3 %copy-done.3 = f32[1,24,96,96]{3,2,1,0:T(8,128)S(1)} copy-done((f32[1,24,96,96]{3,2,1,0:T(8,128)S(1)}, f32[1,24,96,96]{3,2,1,0:T(8,128)}, u32[]{:S(2)}) %copy-start.3) | copy-done | bytes 884760
  1.4 0.7 shard_map.82.after_ref.p_ref.refs_4_.refs_7_
  2.1 0.0 copy-start.7
  2.1 5.1 %collective-permute-start.8 = (f32[576,128]{1,0:T(8,128)S(1)}, f32[576,128]{1,0:T(8,128)S(1)}, u32[]{:S(2)}, u32[]{:S(2)}) collective-permute-start(f32[576,128]{1,0:T(8,128)S(1)} %shard_map.82.after_ref.p_ref.refs_4_.refs_7_), channel_id=1, source_target_pairs={{0,24},{4,28},{8,0},{12,4},{16,8},{20,12},{24,16},{28,20},{1,25},{... | collective-permute-start | bytes 884744 | tf_op jit(solution)/shard_map/ppermute | solution.py:425
  7.3 1.5 %collective-permute-start.7 = (f32[576,128]{1,0:T(8,128)S(1)}, f32[576,128]{1,0:T(8,128)S(1)}, u32[]{:S(2)}, u32[]{:S(2)}) collective-permute-start(f32[576,128]{1,0:T(8,128)S(1)} %shard_map.82.after_ref.p_ref.refs_4_.refs_7_), channel_id=1, source_target_pairs={{0,4},{4,0},{8,12},{12,8},{16,20},{20,16},{24,28},{28,24},{1,5},{5... | collective-permute-start | bytes 884744 | tf_op jit(solution)/shard_map/ppermute | solution.py:424
  8.8 1.8 %shard_map.83 = (f32[432,128]{1,0:T(8,128)S(1)}, f32[432,128]{1,0:T(8,128)S(1)}, f32[432,128]{1,0:T(8,128)S(1)}, f32[432,128]{1,0:T(8,128)S(1)}, f32[576,128]{1,0:T(8,128)S(1)}, /*index=5*/f32[576,128]{1,0:T(8,128)S(1)}) custom-call(s32[2]{0:T(128)S(1)} %pad_add_fusion.scalars, f32[24,96,96]{2,1,0:T(8,128)S(1)} %bitcast.5, bf16[256,256]{1,0:T(8,128)(2,1)S(1)} %copy-done.1, ...), custom_call_target="tpu_custom_call" | custom-call | tf_op jit(solution)/shard_map/pallas_call | solution.py:379
  10.6 0.5 collective-permute-start.6
  11.1 0.5 collective-permute-start.5
  11.6 0.4 collective-permute-start.4
  12.1 2.6 %collective-permute-done.8.r_ref.refs_6_ = f32[576,128]{1,0:T(8,128)S(1)} collective-permute-done((f32[576,128]{1,0:T(8,128)S(1)}, f32[576,128]{1,0:T(8,128)S(1)}, u32[]{:S(2)}, u32[]{:S(2)}) %collective-permute-start.8) | collective-permute-done | bytes 294944 | tf_op jit(solution)/shard_map/ppermute | solution.py:425
  14.6 1.5 %collective-permute-start.3 = (f32[576,128]{1,0:T(8,128)S(1)}, f32[576,128]{1,0:T(8,128)S(1)}, u32[]{:S(2)}, u32[]{:S(2)}) collective-permute-start(f32[576,128]{1,0:T(8,128)S(1)} %get-tuple-element.54.p_ref.refs_4_.refs_9_), channel_id=1, source_target_pairs={{0,4},{4,0},{8,12},{12,8},{16,20},{20,16},{24,28},{28,24},{1,5},{5... | collective-permute-start | bytes 884744 | tf_op jit(solution)/shard_map/ppermute | solution.py:424
  16.2 1.0 collective-permute-done.7.q_ref.refs_5_
  17.1 3.8 %collective-permute-done.6.r_ref.refs_6_ = f32[576,128]{1,0:T(8,128)S(1)} collective-permute-done((f32[576,128]{1,0:T(8,128)S(1)}, f32[576,128]{1,0:T(8,128)S(1)}, u32[]{:S(2)}, u32[]{:S(2)}) %collective-permute-start.6) | collective-permute-done | bytes 294944 | tf_op jit(solution)/shard_map/ppermute | solution.py:425
  21.0 1.5 %collective-permute-start.1 = (f32[432,128]{1,0:T(8,128)S(1)}, f32[432,128]{1,0:T(8,128)S(1)}, u32[]{:S(2)}, u32[]{:S(2)}) collective-permute-start(f32[432,128]{1,0:T(8,128)S(1)} %get-tuple-element.52), channel_id=1, source_target_pairs={{0,2},{1,3},{2,0},{3,1},{4,6},{5,7},{6,4},{7,5},{8,10},{9,11},{10,... | collective-permute-start | bytes 663560 | tf_op jit(solution)/shard_map/ppermute | solution.py:395
  22.5 1.0 collective-permute-done.5.q_ref.refs_5_
  23.5 0.9 shard_map.84.after_ref.refs_4_.refs_12_
  24.3 1.5 %shard_map.85 = (f32[288,128]{1,0:T(8,128)S(1)}, f32[288,128]{1,0:T(8,128)S(1)}, f32[288,128]{1,0:T(8,128)S(1)}, f32[288,128]{1,0:T(8,128)S(1)}) custom-call(s32[2]{0:T(128)S(1)} %pad_add_fusion.scalars, f32[576,128]{1,0:T(8,128)S(1)} %shard_map.82.after_ref.p_ref.refs_4_.refs_7_, f32[576,128]{1,0:T(8,128)S(1)} %collective-permute-done.7.q_ref.refs_5_, ...), custom_call_target="tpu_custom_call" | custom-call | tf_op jit(solution)/shard_map/pallas_call | solution.py:379
  25.8 1.5 %shard_map.86 = (f32[288,128]{1,0:T(8,128)S(1)}, f32[288,128]{1,0:T(8,128)S(1)}, f32[288,128]{1,0:T(8,128)S(1)}, f32[288,128]{1,0:T(8,128)S(1)}) custom-call(s32[2]{0:T(128)S(1)} %pad_add_fusion.scalars, f32[576,128]{1,0:T(8,128)S(1)} %get-tuple-element.55.p_ref.refs_4_.refs_8_, f32[576,128]{1,0:T(8,128)S(1)} %collective-permute-done.5.q_ref.refs_5_, ...), custom_call_target="tpu_custom_call" | custom-call | tf_op jit(solution)/shard_map/pallas_call | solution.py:379
  27.4 1.7 %collective-permute-start.12 = (f32[288,128]{1,0:T(8,128)S(1)}, f32[288,128]{1,0:T(8,128)S(1)}, u32[]{:S(2)}, u32[]{:S(2)}) collective-permute-start(f32[288,128]{1,0:T(8,128)S(1)} %get-tuple-element.63), channel_id=1, source_target_pairs={{0,1},{1,0},{2,3},{3,2},{4,5},{5,4},{6,7},{7,6},{8,9},{9,8},{10,11... | collective-permute-start | bytes 442376 | tf_op jit(solution)/shard_map/ppermute | solution.py:395
  29.0 0.5 collective-permute-start.15
  29.6 0.9 collective-permute-start.18
  30.5 0.7 collective-permute-start.13
  31.2 1.5 %shard_map.87 = (f32[288,128]{1,0:T(8,128)S(1)}, f32[288,128]{1,0:T(8,128)S(1)}, f32[288,128]{1,0:T(8,128)S(1)}, f32[288,128]{1,0:T(8,128)S(1)}) custom-call(s32[2]{0:T(128)S(1)} %pad_add_fusion.scalars, f32[576,128]{1,0:T(8,128)S(1)} %get-tuple-element.54.p_ref.refs_4_.refs_9_, f32[576,128]{1,0:T(8,128)S(1)} %collective-permute-done.3.q_ref.refs_5_, ...), custom_call_target="tpu_custom_call" | custom-call | tf_op jit(solution)/shard_map/pallas_call | solution.py:379
  32.7 0.6 collective-permute-start.16
  33.3 0.8 collective-permute-start.19
  34.1 1.6 %collective-permute-done.15.refs_6_ = f32[288,128]{1,0:T(8,128)S(1)} collective-permute-done((f32[288,128]{1,0:T(8,128)S(1)}, f32[288,128]{1,0:T(8,128)S(1)}, u32[]{:S(2)}, u32[]{:S(2)}) %collective-permute-start.15) | collective-permute-done | bytes 147488 | tf_op jit(solution)/shard_map/ppermute | solution.py:395
  35.8 1.7 %collective-permute-done.18.refs_9_ = f32[288,128]{1,0:T(8,128)S(1)} collective-permute-done((f32[288,128]{1,0:T(8,128)S(1)}, f32[288,128]{1,0:T(8,128)S(1)}, u32[]{:S(2)}, u32[]{:S(2)}) %collective-permute-start.18) | collective-permute-done | bytes 147488 | tf_op jit(solution)/shard_map/ppermute | solution.py:395
  37.4 1.6 %collective-permute-start.17 = (f32[288,128]{1,0:T(8,128)S(1)}, f32[288,128]{1,0:T(8,128)S(1)}, u32[]{:S(2)}, u32[]{:S(2)}) collective-permute-start(f32[288,128]{1,0:T(8,128)S(1)} %get-tuple-element.68), channel_id=1, source_target_pairs={{0,2},{1,3},{2,0},{3,1},{4,6},{5,7},{6,4},{7,5},{8,10},{9,11},{10,... | collective-permute-start | bytes 442376 | tf_op jit(solution)/shard_map/ppermute | solution.py:395
  39.0 1.1 collective-permute-start.20
  40.1 1.4 %shard_map.88 = (f32[432,128]{1,0:T(8,128)S(1)}, f32[432,128]{1,0:T(8,128)S(1)}, f32[432,128]{1,0:T(8,128)S(1)}, f32[432,128]{1,0:T(8,128)S(1)}) custom-call(s32[2]{0:T(128)S(1)} %pad_add_fusion.scalars, f32[432,128]{1,0:T(8,128)S(1)} %get-tuple-element.50.after_ref.refs_0_, f32[432,128]{1,0:T(8,128)S(1)} %collective-permute-done.refs_1_, ...), custom_call_target="tpu_custom_call" | custom-call | tf_op jit(solution)/shard_map/pallas_call | solution.py:379
  41.5 0.6 collective-permute-done.16.refs_7_
  42.1 1.7 %collective-permute-done.19.refs_10_ = f32[288,128]{1,0:T(8,128)S(1)} collective-permute-done((f32[288,128]{1,0:T(8,128)S(1)}, f32[288,128]{1,0:T(8,128)S(1)}, u32[]{:S(2)}, u32[]{:S(2)}) %collective-permute-start.19) | collective-permute-done | bytes 147488 | tf_op jit(solution)/shard_map/ppermute | solution.py:395
  43.8 4.6 %collective-permute-done.17.refs_8_ = f32[288,128]{1,0:T(8,128)S(1)} collective-permute-done((f32[288,128]{1,0:T(8,128)S(1)}, f32[288,128]{1,0:T(8,128)S(1)}, u32[]{:S(2)}, u32[]{:S(2)}) %collective-permute-start.17) | collective-permute-done | bytes 147488 | tf_op jit(solution)/shard_map/ppermute | solution.py:395
  48.4 1.4 %collective-permute-done.20.refs_11_ = f32[288,128]{1,0:T(8,128)S(1)} collective-permute-done((f32[288,128]{1,0:T(8,128)S(1)}, f32[288,128]{1,0:T(8,128)S(1)}, u32[]{:S(2)}, u32[]{:S(2)}) %collective-permute-start.20) | collective-permute-done | bytes 147488 | tf_op jit(solution)/shard_map/ppermute | solution.py:395
  49.8 1.8 %shard_map.89 = (f32[288,128]{1,0:T(8,128)S(1)}, f32[288,128]{1,0:T(8,128)S(1)}, f32[288,128]{1,0:T(8,128)S(1)}, f32[288,128]{1,0:T(8,128)S(1)}, f32[288,128]{1,...) custom-call(s32[2]{0:T(128)S(1)} %pad_add_fusion.scalars, ...), custom_call_target="tpu_custom_call" | custom-call | tf_op jit(solution)/shard_map/pallas_call | solution.py:379
  51.6 0.8 collective-permute-start.21
  52.4 1.4 %collective-permute-start.22 = (f32[288,128]{1,0:T(8,128)S(1)}, f32[288,128]{1,0:T(8,128)S(1)}, u32[]{:S(2)}, u32[]{:S(2)}) collective-permute-start(f32[288,128]{1,0:T(8,128)S(1)} %get-tuple-element.74), channel_id=1, source_target_pairs={{0,2},{1,3},{2,0},{3,1},{4,6},{5,7},{6,4},{7,5},{8,10},{9,11},{10,... | collective-permute-start | bytes 442376 | tf_op jit(solution)/shard_map/ppermute | solution.py:395
  53.8 0.0 collective-permute-start.23
  53.8 0.7 collective-permute-start.24
  54.6 1.4 %collective-permute-start.25 = (f32[288,128]{1,0:T(8,128)S(1)}, f32[288,128]{1,0:T(8,128)S(1)}, u32[]{:S(2)}, u32[]{:S(2)}) collective-permute-start(f32[288,128]{1,0:T(8,128)S(1)} %get-tuple-element.79), channel_id=1, source_target_pairs={{0,2},{1,3},{2,0},{3,1},{4,6},{5,7},{6,4},{7,5},{8,10},{9,11},{10,... | collective-permute-start | bytes 442376 | tf_op jit(solution)/shard_map/ppermute | solution.py:395
  56.0 3.2 %collective-permute-done.22.refs_2_ = f32[288,128]{1,0:T(8,128)S(1)} collective-permute-done((f32[288,128]{1,0:T(8,128)S(1)}, f32[288,128]{1,0:T(8,128)S(1)}, u32[]{:S(2)}, u32[]{:S(2)}) %collective-permute-start.22) | collective-permute-done | bytes 147488 | tf_op jit(solution)/shard_map/ppermute | solution.py:395
  59.1 2.1 %collective-permute-done.23.refs_3_ = f32[288,128]{1,0:T(8,128)S(1)} collective-permute-done((f32[288,128]{1,0:T(8,128)S(1)}, f32[288,128]{1,0:T(8,128)S(1)}, u32[]{:S(2)}, u32[]{:S(2)}) %collective-permute-start.23) | collective-permute-done | bytes 147488 | tf_op jit(solution)/shard_map/ppermute | solution.py:395
  61.2 1.0 collective-permute-start.28
  62.2 1.5 %shard_map.90 = (f32[576,128]{1,0:T(8,128)S(1)}, f32[576,128]{1,0:T(8,128)S(1)}, f32[576,128]{1,0:T(8,128)S(1)}) custom-call(s32[2]{0:T(128)S(1)} %pad_add_fusion.scalars, f32[288,128]{1,0:T(8,128)S(1)} %get-tuple-element.72.refs_0_.refs_9_, f32[288,128]{1,0:T(8,128)S(1)} %collective-permute-done.21.refs_1_, f32[288,128]{1,0:T(8,128)S(1)} %collective-permute-done.22.refs_2_, ...), custom_call_target="tpu_custom_call" | custom-call | tf_op jit(solution)/shard_map/pallas_call | solution.py:379
  63.8 1.7 %collective-permute-done.25.refs_2_ = f32[288,128]{1,0:T(8,128)S(1)} collective-permute-done((f32[288,128]{1,0:T(8,128)S(1)}, f32[288,128]{1,0:T(8,128)S(1)}, u32[]{:S(2)}, u32[]{:S(2)}) %collective-permute-start.25) | collective-permute-done | bytes 147488 | tf_op jit(solution)/shard_map/ppermute | solution.py:395
  65.5 2.1 %collective-permute-done.26.refs_3_ = f32[288,128]{1,0:T(8,128)S(1)} collective-permute-done((f32[288,128]{1,0:T(8,128)S(1)}, f32[288,128]{1,0:T(8,128)S(1)}, u32[]{:S(2)}, u32[]{:S(2)}) %collective-permute-start.26) | collective-permute-done | bytes 147488 | tf_op jit(solution)/shard_map/ppermute | solution.py:395
  67.5 1.5 %shard_map.91 = (f32[576,128]{1,0:T(8,128)S(1)}, f32[576,128]{1,0:T(8,128)S(1)}, f32[576,128]{1,0:T(8,128)S(1)}) custom-call(s32[2]{0:T(128)S(1)} %pad_add_fusion.scalars, f32[288,128]{1,0:T(8,128)S(1)} %get-tuple-element.77.refs_0_, f32[288,128]{1,0:T(8,128)S(1)} %collective-permute-done.24.refs_1_, f32[288,128]{1,0:T(8,128)S(1)} %collective-permute-done.25.refs_2_, ...), custom_call_target="tpu_custom_call" | custom-call | tf_op jit(solution)/shard_map/pallas_call | solution.py:379
  69.1 1.6 %collective-permute-start.32 = (f32[576,128]{1,0:T(8,128)S(1)}, f32[576,128]{1,0:T(8,128)S(1)}, u32[]{:S(2)}, u32[]{:S(2)}) collective-permute-start(f32[576,128]{1,0:T(8,128)S(1)} %get-tuple-element.89), channel_id=1, source_target_pairs={{0,4},{4,0},{8,12},{12,8},{16,20},{20,16},{24,28},{28,24},{1,5},{5... | collective-permute-start | bytes 884744 | tf_op jit(solution)/shard_map/ppermute | solution.py:498
  70.7 0.6 collective-permute-start.9
  71.3 1.4 %collective-permute-start.10 = (f32[432,128]{1,0:T(8,128)S(1)}, f32[432,128]{1,0:T(8,128)S(1)}, u32[]{:S(2)}, u32[]{:S(2)}) collective-permute-start(f32[432,128]{1,0:T(8,128)S(1)} %get-tuple-element.61), channel_id=1, source_target_pairs={{0,2},{1,3},{2,0},{3,1},{4,6},{5,7},{6,4},{7,5},{8,10},{9,11},{10,... | collective-permute-start | bytes 663560 | tf_op jit(solution)/shard_map/ppermute | solution.py:395
  72.7 1.7 %collective-permute-start.29 = (f32[288,128]{1,0:T(8,128)S(1)}, f32[288,128]{1,0:T(8,128)S(1)}, u32[]{:S(2)}, u32[]{:S(2)}) collective-permute-start(f32[288,128]{1,0:T(8,128)S(1)} %get-tuple-element.85), channel_id=1, source_target_pairs={{0,3},{1,2},{2,1},{3,0},{4,7},{5,6},{6,5},{7,4},{8,11},{9,10},{10,... | collective-permute-start | bytes 442376 | tf_op jit(solution)/shard_map/ppermute | solution.py:395
  74.5 11.1 %collective-permute-done.29.refs_3_ = f32[288,128]{1,0:T(8,128)S(1)} collective-permute-done((f32[288,128]{1,0:T(8,128)S(1)}, f32[288,128]{1,0:T(8,128)S(1)}, u32[]{:S(2)}, u32[]{:S(2)}) %collective-permute-start.29) | collective-permute-done | bytes 147488 | tf_op jit(solution)/shard_map/ppermute | solution.py:395
  85.5 0.4 collective-permute-start.33
  85.9 1.5 %shard_map.92 = (f32[576,128]{1,0:T(8,128)S(1)}, f32[576,128]{1,0:T(8,128)S(1)}, f32[576,128]{1,0:T(8,128)S(1)}) custom-call(s32[2]{0:T(128)S(1)} %pad_add_fusion.scalars, f32[288,128]{1,0:T(8,128)S(1)} %get-tuple-element.82.refs_0_, f32[288,128]{1,0:T(8,128)S(1)} %collective-permute-done.27.refs_1_, f32[288,128]{1,0:T(8,128)S(1)} %collective-permute-done.28.refs_2_, ...), custom_call_target="tpu_custom_call" | custom-call | tf_op jit(solution)/shard_map/pallas_call | solution.py:379
  87.5 0.6 collective-permute-start.30
  88.1 1.6 %collective-permute-start.31 = (f32[576,128]{1,0:T(8,128)S(1)}, f32[576,128]{1,0:T(8,128)S(1)}, u32[]{:S(2)}, u32[]{:S(2)}) collective-permute-start(f32[576,128]{1,0:T(8,128)S(1)} %get-tuple-element.88), channel_id=1, source_target_pairs={{0,8},{4,12},{8,16},{12,20},{16,24},{20,28},{24,0},{28,4},{1,9},{5... | collective-permute-start | bytes 884744 | tf_op jit(solution)/shard_map/ppermute | solution.py:497
  89.6 1.5 %collective-permute-start.34 = (f32[576,128]{1,0:T(8,128)S(1)}, f32[576,128]{1,0:T(8,128)S(1)}, u32[]{:S(2)}, u32[]{:S(2)}) collective-permute-start(f32[576,128]{1,0:T(8,128)S(1)} %get-tuple-element.93), channel_id=1, source_target_pairs={{0,4},{4,0},{8,12},{12,8},{16,20},{20,16},{24,28},{28,24},{1,5},{5... | collective-permute-start | bytes 884744 | tf_op jit(solution)/shard_map/ppermute | solution.py:498
  91.2 3.4 %collective-permute-start.35 = (f32[576,128]{1,0:T(8,128)S(1)}, f32[576,128]{1,0:T(8,128)S(1)}, u32[]{:S(2)}, u32[]{:S(2)}) collective-permute-start(f32[576,128]{1,0:T(8,128)S(1)} %get-tuple-element.94), channel_id=1, source_target_pairs={{0,8},{4,12},{8,16},{12,20},{16,24},{20,28},{24,0},{28,4},{1,9},{5... | collective-permute-start | bytes 884744 | tf_op jit(solution)/shard_map/ppermute | solution.py:497
  94.5 3.0 %collective-permute-done.33.refs_13_ = f32[576,128]{1,0:T(8,128)S(1)} collective-permute-done((f32[576,128]{1,0:T(8,128)S(1)}, f32[576,128]{1,0:T(8,128)S(1)}, u32[]{:S(2)}, u32[]{:S(2)}) %collective-permute-start.33) | collective-permute-done | bytes 294944 | tf_op jit(solution)/shard_map/ppermute | solution.py:497
  97.5 6.3 %collective-permute-done.31.refs_11_ = f32[576,128]{1,0:T(8,128)S(1)} collective-permute-done((f32[576,128]{1,0:T(8,128)S(1)}, f32[576,128]{1,0:T(8,128)S(1)}, u32[]{:S(2)}, u32[]{:S(2)}) %collective-permute-start.31) | collective-permute-done | bytes 294944 | tf_op jit(solution)/shard_map/ppermute | solution.py:497
  103.8 2.8 %shard_map.93 = (f32[24,96,96]{2,1,0:T(8,128)}, f32[576,128]{1,0:T(8,128)S(1)}) custom-call(s32[2]{0:T(128)S(1)} %pad_add_fusion.scalars, f32[432,128]{1,0:T(8,128)S(1)} %get-tuple-element.59.refs_15_.refs_0_, f32[432,128]{1,0:T(8,128)S(1)} %collective-permute-done.9.refs_1_, f32[432,128]{1,0:T(8,128)S(1)} %collective-permute-done.10.refs_2_, ...), custom_call_target="tpu_custom_call" | custom-call | tf_op jit(solution)/shard_map/pallas_call | solution.py:379
  106.6 3.6 %collective-permute-done.35.z_ref = f32[576,128]{1,0:T(8,128)S(1)} collective-permute-done((f32[576,128]{1,0:T(8,128)S(1)}, f32[576,128]{1,0:T(8,128)S(1)}, u32[]{:S(2)}, u32[]{:S(2)}) %collective-permute-start.35) | collective-permute-done | bytes 294944 | tf_op jit(solution)/shard_map/ppermute | solution.py:497
  110.1 1.4 %shard_map.94 = f32[24,96,96]{2,1,0:T(8,128)} custom-call(s32[2]{0:T(128)S(1)} %pad_add_fusion.scalars, f32[24,96,96]{2,1,0:T(8,128)} %get-tuple-element.91.partial_ref, f32[576,128]{1,0:T(8,128)S(1)} %get-tuple-element.92.rest_ref, f32[576,128]{1,0:T(8,128)S(1)} %collective-permute-done.34.y_ref, ...), custom_call_target="tpu_custom_call", output_to_operand_aliasing={{}: (1, {})} | custom-call | tf_op jit(solution)/shard_map/pallas_call | solution.py:379
  (38 shorter events, 0.1 us)
Async XLA Ops:
  0.0 8.8 %copy-start.1 = (bf16[256,256]{1,0:T(8,128)(2,1)S(1)}, bf16[256,256]{1,0:T(8,128)(2,1)}, u32[]{:S(2)}) copy-start(bf16[256,256]{1,0:T(8,128)(2,1)} %constant.37.clone.tz_ref.refs_7_.refs_14_) | copy-start | bytes 393220
  0.0 8.8 %copy-start = (bf16[4,256,192]{2,1,0:T(8,128)(2,1)S(1)}, bf16[4,256,192]{2,1,0:T(8,128)(2,1)}, u32[]{:S(2)}) copy-start(bf16[4,256,192]{2,1,0:T(8,128)(2,1)} %constant.38.clone.ty_ref) | copy-start | bytes 1179652
  0.1 1.3 %copy-start.3 = (f32[1,24,96,96]{3,2,1,0:T(8,128)S(1)}, f32[1,24,96,96]{3,2,1,0:T(8,128)}, u32[]{:S(2)}) copy-start(f32[1,24,96,96]{3,2,1,0:T(8,128)} %param.8) | copy-start | bytes 2654212
  2.1 21.4 %copy-start.6 = (f32[4,24,128]{2,1,0:T(8,128)S(1)}, f32[4,24,128]{2,1,0:T(8,128)}, u32[]{:S(2)}) copy-start(f32[4,24,128]{2,1,0:T(8,128)} %constant.43.clone.within_ref) | copy-start | bytes 147460
  2.1 21.3 %copy-start.7 = (f32[96,128]{1,0:T(8,128)S(1)}, f32[96,128]{1,0:T(8,128)}, u32[]{:S(2)}) copy-start(f32[96,128]{1,0:T(8,128)} %constant.42.clone.across_ref) | copy-start | bytes 147460
  2.1 12.5 %collective-permute-start.8 = (f32[576,128]{1,0:T(8,128)S(1)}, f32[576,128]{1,0:T(8,128)S(1)}, u32[]{:S(2)}, u32[]{:S(2)}) collective-permute-start(f32[576,128]{1,0:T(8,128)S(1)} %shard_map.82.after_ref.p_ref.refs_4_.refs_7_), channel_id=1, source_target_pairs={{0,24},{4,28},{8,0},{12,4},{16,8},{20,12},{24,16},{28,20},{1,25},{... | collective-permute-start | bytes 884744 | tf_op jit(solution)/shard_map/ppermute | solution.py:425
  7.3 9.9 %collective-permute-start.7 = (f32[576,128]{1,0:T(8,128)S(1)}, f32[576,128]{1,0:T(8,128)S(1)}, u32[]{:S(2)}, u32[]{:S(2)}) collective-permute-start(f32[576,128]{1,0:T(8,128)S(1)} %shard_map.82.after_ref.p_ref.refs_4_.refs_7_), channel_id=1, source_target_pairs={{0,4},{4,0},{8,12},{12,8},{16,20},{20,16},{24,28},{28,24},{1,5},{5... | collective-permute-start | bytes 884744 | tf_op jit(solution)/shard_map/ppermute | solution.py:424
  10.6 10.3 %collective-permute-start.6 = (f32[576,128]{1,0:T(8,128)S(1)}, f32[576,128]{1,0:T(8,128)S(1)}, u32[]{:S(2)}, u32[]{:S(2)}) collective-permute-start(f32[576,128]{1,0:T(8,128)S(1)} %get-tuple-element.55.p_ref.refs_4_.refs_8_), channel_id=1, source_target_pairs={{0,24},{4,28},{8,0},{12,4},{16,8},{20,12},{24,16},{28,20},{1,25},{... | collective-permute-start | bytes 884744 | tf_op jit(solution)/shard_map/ppermute | solution.py:425
  11.1 12.3 %collective-permute-start.5 = (f32[576,128]{1,0:T(8,128)S(1)}, f32[576,128]{1,0:T(8,128)S(1)}, u32[]{:S(2)}, u32[]{:S(2)}) collective-permute-start(f32[576,128]{1,0:T(8,128)S(1)} %get-tuple-element.55.p_ref.refs_4_.refs_8_), channel_id=1, source_target_pairs={{0,4},{4,0},{8,12},{12,8},{16,20},{20,16},{24,28},{28,24},{1,5},{5... | collective-permute-start | bytes 884744 | tf_op jit(solution)/shard_map/ppermute | solution.py:424
  11.6 17.9 %collective-permute-start.4 = (f32[576,128]{1,0:T(8,128)S(1)}, f32[576,128]{1,0:T(8,128)S(1)}, u32[]{:S(2)}, u32[]{:S(2)}) collective-permute-start(f32[576,128]{1,0:T(8,128)S(1)} %get-tuple-element.54.p_ref.refs_4_.refs_9_), channel_id=1, source_target_pairs={{0,24},{4,28},{8,0},{12,4},{16,8},{20,12},{24,16},{28,20},{1,25},{... | collective-permute-start | bytes 884744 | tf_op jit(solution)/shard_map/ppermute | solution.py:425
  14.6 15.8 %collective-permute-start.3 = (f32[576,128]{1,0:T(8,128)S(1)}, f32[576,128]{1,0:T(8,128)S(1)}, u32[]{:S(2)}, u32[]{:S(2)}) collective-permute-start(f32[576,128]{1,0:T(8,128)S(1)} %get-tuple-element.54.p_ref.refs_4_.refs_9_), channel_id=1, source_target_pairs={{0,4},{4,0},{8,12},{12,8},{16,20},{20,16},{24,28},{28,24},{1,5},{5... | collective-permute-start | bytes 884744 | tf_op jit(solution)/shard_map/ppermute | solution.py:424
  17.1 10.2 %collective-permute-start = (f32[432,128]{1,0:T(8,128)S(1)}, f32[432,128]{1,0:T(8,128)S(1)}, u32[]{:S(2)}, u32[]{:S(2)}) collective-permute-start(f32[432,128]{1,0:T(8,128)S(1)} %get-tuple-element.51), channel_id=1, source_target_pairs={{0,1},{1,0},{2,3},{3,2},{4,5},{5,4},{6,7},{7,6},{8,9},{9,8},{10,11... | collective-permute-start | bytes 663560 | tf_op jit(solution)/shard_map/ppermute | solution.py:395
  21.0 8.1 %collective-permute-start.1 = (f32[432,128]{1,0:T(8,128)S(1)}, f32[432,128]{1,0:T(8,128)S(1)}, u32[]{:S(2)}, u32[]{:S(2)}) collective-permute-start(f32[432,128]{1,0:T(8,128)S(1)} %get-tuple-element.52), channel_id=1, source_target_pairs={{0,2},{1,3},{2,0},{3,1},{4,6},{5,7},{6,4},{7,5},{8,10},{9,11},{10,... | collective-permute-start | bytes 663560 | tf_op jit(solution)/shard_map/ppermute | solution.py:395
  23.4 9.2 %collective-permute-start.2 = (f32[432,128]{1,0:T(8,128)S(1)}, f32[432,128]{1,0:T(8,128)S(1)}, u32[]{:S(2)}, u32[]{:S(2)}) collective-permute-start(f32[432,128]{1,0:T(8,128)S(1)} %get-tuple-element.53), channel_id=1, source_target_pairs={{0,3},{1,2},{2,1},{3,0},{4,7},{5,6},{6,5},{7,4},{8,11},{9,10},{10,... | collective-permute-start | bytes 663560 | tf_op jit(solution)/shard_map/ppermute | solution.py:395
  27.3 12.8 %copy-start.4 = (bf16[4,192,192]{2,1,0:T(8,128)(2,1)S(1)}, bf16[4,192,192]{2,1,0:T(8,128)(2,1)}, u32[]{:S(2)}) copy-start(bf16[4,192,192]{2,1,0:T(8,128)(2,1)} %constant.41.clone.refs_6_.refs_14_) | copy-start | bytes 884740
  27.3 12.8 %copy-start.5 = (bf16[4,192,192]{2,1,0:T(8,128)(2,1)S(1)}, bf16[4,192,192]{2,1,0:T(8,128)(2,1)}, u32[]{:S(2)}) copy-start(bf16[4,192,192]{2,1,0:T(8,128)(2,1)} %constant.40.clone.refs_5_.refs_13_) | copy-start | bytes 884740
  27.4 5.9 %collective-permute-start.12 = (f32[288,128]{1,0:T(8,128)S(1)}, f32[288,128]{1,0:T(8,128)S(1)}, u32[]{:S(2)}, u32[]{:S(2)}) collective-permute-start(f32[288,128]{1,0:T(8,128)S(1)} %get-tuple-element.63), channel_id=1, source_target_pairs={{0,1},{1,0},{2,3},{3,2},{4,5},{5,4},{6,7},{7,6},{8,9},{9,8},{10,11... | collective-permute-start | bytes 442376 | tf_op jit(solution)/shard_map/ppermute | solution.py:395
  29.0 6.7 %collective-permute-start.15 = (f32[288,128]{1,0:T(8,128)S(1)}, f32[288,128]{1,0:T(8,128)S(1)}, u32[]{:S(2)}, u32[]{:S(2)}) collective-permute-start(f32[288,128]{1,0:T(8,128)S(1)} %get-tuple-element.66), channel_id=1, source_target_pairs={{0,2},{1,3},{2,0},{3,1},{4,6},{5,7},{6,4},{7,5},{8,10},{9,11},{10,... | collective-permute-start | bytes 442376 | tf_op jit(solution)/shard_map/ppermute | solution.py:395
  29.6 7.9 %collective-permute-start.18 = (f32[288,128]{1,0:T(8,128)S(1)}, f32[288,128]{1,0:T(8,128)S(1)}, u32[]{:S(2)}, u32[]{:S(2)}) collective-permute-start(f32[288,128]{1,0:T(8,128)S(1)} %get-tuple-element.69), channel_id=1, source_target_pairs={{0,3},{1,2},{2,1},{3,0},{4,7},{5,6},{6,5},{7,4},{8,11},{9,10},{10,... | collective-permute-start | bytes 442376 | tf_op jit(solution)/shard_map/ppermute | solution.py:395
  30.5 8.5 %collective-permute-start.13 = (f32[288,128]{1,0:T(8,128)S(1)}, f32[288,128]{1,0:T(8,128)S(1)}, u32[]{:S(2)}, u32[]{:S(2)}) collective-permute-start(f32[288,128]{1,0:T(8,128)S(1)} %get-tuple-element.64), channel_id=1, source_target_pairs={{0,1},{1,0},{2,3},{3,2},{4,5},{5,4},{6,7},{7,6},{8,9},{9,8},{10,11... | collective-permute-start | bytes 442376 | tf_op jit(solution)/shard_map/ppermute | solution.py:395
  32.7 9.4 %collective-permute-start.16 = (f32[288,128]{1,0:T(8,128)S(1)}, f32[288,128]{1,0:T(8,128)S(1)}, u32[]{:S(2)}, u32[]{:S(2)}) collective-permute-start(f32[288,128]{1,0:T(8,128)S(1)} %get-tuple-element.67), channel_id=1, source_target_pairs={{0,2},{1,3},{2,0},{3,1},{4,6},{5,7},{6,4},{7,5},{8,10},{9,11},{10,... | collective-permute-start | bytes 442376 | tf_op jit(solution)/shard_map/ppermute | solution.py:395
  33.3 10.5 %collective-permute-start.19 = (f32[288,128]{1,0:T(8,128)S(1)}, f32[288,128]{1,0:T(8,128)S(1)}, u32[]{:S(2)}, u32[]{:S(2)}) collective-permute-start(f32[288,128]{1,0:T(8,128)S(1)} %get-tuple-element.70), channel_id=1, source_target_pairs={{0,3},{1,2},{2,1},{3,0},{4,7},{5,6},{6,5},{7,4},{8,11},{9,10},{10,... | collective-permute-start | bytes 442376 | tf_op jit(solution)/shard_map/ppermute | solution.py:395
  35.8 8.0 %collective-permute-start.14 = (f32[288,128]{1,0:T(8,128)S(1)}, f32[288,128]{1,0:T(8,128)S(1)}, u32[]{:S(2)}, u32[]{:S(2)}) collective-permute-start(f32[288,128]{1,0:T(8,128)S(1)} %get-tuple-element.65), channel_id=1, source_target_pairs={{0,1},{1,0},{2,3},{3,2},{4,5},{5,4},{6,7},{7,6},{8,9},{9,8},{10,11... | collective-permute-start | bytes 442376 | tf_op jit(solution)/shard_map/ppermute | solution.py:395
  37.4 11.0 %collective-permute-start.17 = (f32[288,128]{1,0:T(8,128)S(1)}, f32[288,128]{1,0:T(8,128)S(1)}, u32[]{:S(2)}, u32[]{:S(2)}) collective-permute-start(f32[288,128]{1,0:T(8,128)S(1)} %get-tuple-element.68), channel_id=1, source_target_pairs={{0,2},{1,3},{2,0},{3,1},{4,6},{5,7},{6,4},{7,5},{8,10},{9,11},{10,... | collective-permute-start | bytes 442376 | tf_op jit(solution)/shard_map/ppermute | solution.py:395
  39.0 10.8 %collective-permute-start.20 = (f32[288,128]{1,0:T(8,128)S(1)}, f32[288,128]{1,0:T(8,128)S(1)}, u32[]{:S(2)}, u32[]{:S(2)}) collective-permute-start(f32[288,128]{1,0:T(8,128)S(1)} %get-tuple-element.71), channel_id=1, source_target_pairs={{0,3},{1,2},{2,1},{3,0},{4,7},{5,6},{6,5},{7,4},{8,11},{9,10},{10,... | collective-permute-start | bytes 442376 | tf_op jit(solution)/shard_map/ppermute | solution.py:395
  49.8 12.4 %copy-start.2 = (bf16[4,192,256]{2,1,0:T(8,128)(2,1)S(1)}, bf16[4,192,256]{2,1,0:T(8,128)(2,1)}, u32[]{:S(2)}) copy-start(bf16[4,192,256]{2,1,0:T(8,128)(2,1)} %constant.39.clone.refs_8_.refs_15_) | copy-start | bytes 1179652
  51.6 4.3 %collective-permute-start.21 = (f32[288,128]{1,0:T(8,128)S(1)}, f32[288,128]{1,0:T(8,128)S(1)}, u32[]{:S(2)}, u32[]{:S(2)}) collective-permute-start(f32[288,128]{1,0:T(8,128)S(1)} %get-tuple-element.73), channel_id=1, source_target_pairs={{0,1},{1,0},{2,3},{3,2},{4,5},{5,4},{6,7},{7,6},{8,9},{9,8},{10,11... | collective-permute-start | bytes 442376 | tf_op jit(solution)/shard_map/ppermute | solution.py:395
  52.4 6.7 %collective-permute-start.22 = (f32[288,128]{1,0:T(8,128)S(1)}, f32[288,128]{1,0:T(8,128)S(1)}, u32[]{:S(2)}, u32[]{:S(2)}) collective-permute-start(f32[288,128]{1,0:T(8,128)S(1)} %get-tuple-element.74), channel_id=1, source_target_pairs={{0,2},{1,3},{2,0},{3,1},{4,6},{5,7},{6,4},{7,5},{8,10},{9,11},{10,... | collective-permute-start | bytes 442376 | tf_op jit(solution)/shard_map/ppermute | solution.py:395
  53.8 7.4 %collective-permute-start.23 = (f32[288,128]{1,0:T(8,128)S(1)}, f32[288,128]{1,0:T(8,128)S(1)}, u32[]{:S(2)}, u32[]{:S(2)}) collective-permute-start(f32[288,128]{1,0:T(8,128)S(1)} %get-tuple-element.75), channel_id=1, source_target_pairs={{0,3},{1,2},{2,1},{3,0},{4,7},{5,6},{6,5},{7,4},{8,11},{9,10},{10,... | collective-permute-start | bytes 442376 | tf_op jit(solution)/shard_map/ppermute | solution.py:395
  53.8 9.9 %collective-permute-start.24 = (f32[288,128]{1,0:T(8,128)S(1)}, f32[288,128]{1,0:T(8,128)S(1)}, u32[]{:S(2)}, u32[]{:S(2)}) collective-permute-start(f32[288,128]{1,0:T(8,128)S(1)} %get-tuple-element.78), channel_id=1, source_target_pairs={{0,1},{1,0},{2,3},{3,2},{4,5},{5,4},{6,7},{7,6},{8,9},{9,8},{10,11... | collective-permute-start | bytes 442376 | tf_op jit(solution)/shard_map/ppermute | solution.py:395
  54.6 10.9 %collective-permute-start.25 = (f32[288,128]{1,0:T(8,128)S(1)}, f32[288,128]{1,0:T(8,128)S(1)}, u32[]{:S(2)}, u32[]{:S(2)}) collective-permute-start(f32[288,128]{1,0:T(8,128)S(1)} %get-tuple-element.79), channel_id=1, source_target_pairs={{0,2},{1,3},{2,0},{3,1},{4,6},{5,7},{6,4},{7,5},{8,10},{9,11},{10,... | collective-permute-start | bytes 442376 | tf_op jit(solution)/shard_map/ppermute | solution.py:395
  56.0 11.6 %collective-permute-start.26 = (f32[288,128]{1,0:T(8,128)S(1)}, f32[288,128]{1,0:T(8,128)S(1)}, u32[]{:S(2)}, u32[]{:S(2)}) collective-permute-start(f32[288,128]{1,0:T(8,128)S(1)} %get-tuple-element.80), channel_id=1, source_target_pairs={{0,3},{1,2},{2,1},{3,0},{4,7},{5,6},{6,5},{7,4},{8,11},{9,10},{10,... | collective-permute-start | bytes 442376 | tf_op jit(solution)/shard_map/ppermute | solution.py:395
  59.1 13.6 %collective-permute-start.27 = (f32[288,128]{1,0:T(8,128)S(1)}, f32[288,128]{1,0:T(8,128)S(1)}, u32[]{:S(2)}, u32[]{:S(2)}) collective-permute-start(f32[288,128]{1,0:T(8,128)S(1)} %get-tuple-element.83), channel_id=1, source_target_pairs={{0,1},{1,0},{2,3},{3,2},{4,5},{5,4},{6,7},{7,6},{8,9},{9,8},{10,11... | collective-permute-start | bytes 442376 | tf_op jit(solution)/shard_map/ppermute | solution.py:395
  61.2 11.5 %collective-permute-start.28 = (f32[288,128]{1,0:T(8,128)S(1)}, f32[288,128]{1,0:T(8,128)S(1)}, u32[]{:S(2)}, u32[]{:S(2)}) collective-permute-start(f32[288,128]{1,0:T(8,128)S(1)} %get-tuple-element.84), channel_id=1, source_target_pairs={{0,2},{1,3},{2,0},{3,1},{4,6},{5,7},{6,4},{7,5},{8,10},{9,11},{10,... | collective-permute-start | bytes 442376 | tf_op jit(solution)/shard_map/ppermute | solution.py:395
  69.1 22.1 %collective-permute-start.32 = (f32[576,128]{1,0:T(8,128)S(1)}, f32[576,128]{1,0:T(8,128)S(1)}, u32[]{:S(2)}, u32[]{:S(2)}) collective-permute-start(f32[576,128]{1,0:T(8,128)S(1)} %get-tuple-element.89), channel_id=1, source_target_pairs={{0,4},{4,0},{8,12},{12,8},{16,20},{20,16},{24,28},{28,24},{1,5},{5... | collective-permute-start | bytes 884744 | tf_op jit(solution)/shard_map/ppermute | solution.py:498
  70.7 16.8 %collective-permute-start.9 = (f32[432,128]{1,0:T(8,128)S(1)}, f32[432,128]{1,0:T(8,128)S(1)}, u32[]{:S(2)}, u32[]{:S(2)}) collective-permute-start(f32[432,128]{1,0:T(8,128)S(1)} %get-tuple-element.60), channel_id=1, source_target_pairs={{0,1},{1,0},{2,3},{3,2},{4,5},{5,4},{6,7},{7,6},{8,9},{9,8},{10,11... | collective-permute-start | bytes 663560 | tf_op jit(solution)/shard_map/ppermute | solution.py:395
  71.3 16.8 %collective-permute-start.10 = (f32[432,128]{1,0:T(8,128)S(1)}, f32[432,128]{1,0:T(8,128)S(1)}, u32[]{:S(2)}, u32[]{:S(2)}) collective-permute-start(f32[432,128]{1,0:T(8,128)S(1)} %get-tuple-element.61), channel_id=1, source_target_pairs={{0,2},{1,3},{2,0},{3,1},{4,6},{5,7},{6,4},{7,5},{8,10},{9,11},{10,... | collective-permute-start | bytes 663560 | tf_op jit(solution)/shard_map/ppermute | solution.py:395
  72.7 16.9 %collective-permute-start.11 = (f32[432,128]{1,0:T(8,128)S(1)}, f32[432,128]{1,0:T(8,128)S(1)}, u32[]{:S(2)}, u32[]{:S(2)}) collective-permute-start(f32[432,128]{1,0:T(8,128)S(1)} %get-tuple-element.62), channel_id=1, source_target_pairs={{0,3},{1,2},{2,1},{3,0},{4,7},{5,6},{6,5},{7,4},{8,11},{9,10},{10,... | collective-permute-start | bytes 663560 | tf_op jit(solution)/shard_map/ppermute | solution.py:395
  72.7 12.8 %collective-permute-start.29 = (f32[288,128]{1,0:T(8,128)S(1)}, f32[288,128]{1,0:T(8,128)S(1)}, u32[]{:S(2)}, u32[]{:S(2)}) collective-permute-start(f32[288,128]{1,0:T(8,128)S(1)} %get-tuple-element.85), channel_id=1, source_target_pairs={{0,3},{1,2},{2,1},{3,0},{4,7},{5,6},{6,5},{7,4},{8,11},{9,10},{10,... | collective-permute-start | bytes 442376 | tf_op jit(solution)/shard_map/ppermute | solution.py:395
  85.5 12.0 %collective-permute-start.33 = (f32[576,128]{1,0:T(8,128)S(1)}, f32[576,128]{1,0:T(8,128)S(1)}, u32[]{:S(2)}, u32[]{:S(2)}) collective-permute-start(f32[576,128]{1,0:T(8,128)S(1)} %get-tuple-element.90), channel_id=1, source_target_pairs={{0,8},{4,12},{8,16},{12,20},{16,24},{20,28},{24,0},{28,4},{1,9},{5... | collective-permute-start | bytes 884744 | tf_op jit(solution)/shard_map/ppermute | solution.py:497
  87.5 10.0 %collective-permute-start.30 = (f32[576,128]{1,0:T(8,128)S(1)}, f32[576,128]{1,0:T(8,128)S(1)}, u32[]{:S(2)}, u32[]{:S(2)}) collective-permute-start(f32[576,128]{1,0:T(8,128)S(1)} %get-tuple-element.87), channel_id=1, source_target_pairs={{0,4},{4,0},{8,12},{12,8},{16,20},{20,16},{24,28},{28,24},{1,5},{5... | collective-permute-start | bytes 884744 | tf_op jit(solution)/shard_map/ppermute | solution.py:498
  88.1 15.8 %collective-permute-start.31 = (f32[576,128]{1,0:T(8,128)S(1)}, f32[576,128]{1,0:T(8,128)S(1)}, u32[]{:S(2)}, u32[]{:S(2)}) collective-permute-start(f32[576,128]{1,0:T(8,128)S(1)} %get-tuple-element.88), channel_id=1, source_target_pairs={{0,8},{4,12},{8,16},{12,20},{16,24},{20,28},{24,0},{28,4},{1,9},{5... | collective-permute-start | bytes 884744 | tf_op jit(solution)/shard_map/ppermute | solution.py:497
  89.6 16.9 %collective-permute-start.34 = (f32[576,128]{1,0:T(8,128)S(1)}, f32[576,128]{1,0:T(8,128)S(1)}, u32[]{:S(2)}, u32[]{:S(2)}) collective-permute-start(f32[576,128]{1,0:T(8,128)S(1)} %get-tuple-element.93), channel_id=1, source_target_pairs={{0,4},{4,0},{8,12},{12,8},{16,20},{20,16},{24,28},{28,24},{1,5},{5... | collective-permute-start | bytes 884744 | tf_op jit(solution)/shard_map/ppermute | solution.py:498
  91.2 19.0 %collective-permute-start.35 = (f32[576,128]{1,0:T(8,128)S(1)}, f32[576,128]{1,0:T(8,128)S(1)}, u32[]{:S(2)}, u32[]{:S(2)}) collective-permute-start(f32[576,128]{1,0:T(8,128)S(1)} %get-tuple-element.94), channel_id=1, source_target_pairs={{0,8},{4,12},{8,16},{12,20},{16,24},{20,28},{24,0},{28,4},{1,9},{5... | collective-permute-start | bytes 884744 | tf_op jit(solution)/shard_map/ppermute | solution.py:497

commit v3 on v2

--- a/solution.py
+++ b/solution.py
@@ -191,25 +191,26 @@
                     outs[k][pl.ds(first, e, stride=stride), :] = packed[:e]
 
 
-def load_potential(plan, ins, base, stride, plane, tz, ty):
+def load_potential(plan, place, planes, tz, ty):
     e = plan.extra
-    planes = []
-    for pair in range(CHUNK // 2):
+    found = []
+    for first in range(0, len(planes), 2):
         two = []
-        for i in range(2):
+        for plane in planes[first : first + 2]:
+            ins, stride, offset = place(plane)
             rows, tails = [], []
-            for k in range(plan.parts):
+            for ref, base in ins:
                 parts = []
                 for t in range(3):
-                    first = base + t * e * stride + plane + 2 * pair + i
-                    part = ins[k][pl.ds(first, e, stride=stride), :]
+                    at = base + t * e * stride + offset
+                    part = ref[pl.ds(at, e, stride=stride), :]
                     parts.append(jnp.concatenate([part, jnp.zeros((8 - e, LANES), F32)], axis=0))
                 rows += parts
                 tails.append(thirds(parts, plan))
             two.append(jnp.concatenate(rows + tails, axis=0))
         once = along_rows(ty, jnp.concatenate(two, axis=1))
-        planes += [once[:, :LANES], once[:, LANES:]]
-    return along_lanes(jnp.concatenate(planes, axis=0), tz)
+        found += [once[:, :LANES], once[:, LANES:]]
+    return along_lanes(jnp.concatenate(found, axis=0), tz)
 
 
 CHUNK = 8
@@ -230,8 +231,18 @@
 def pack_chunk(wide, plan):
     h = plan.height
     return jnp.concatenate(
-        [pack(wide[i * h : (i + 1) * h], plan) for i in range(CHUNK)], axis=0
-    )
+        [pack(wide[i * h : (i + 1) * h], plan) for i in range(wide.shape[0] // h)], axis=0
+    )
+
+
+def planes_of(refs, first, size, plan):
+    parts = []
+    while size:
+        c, at = divmod(first, CHUNK)
+        count = min(size, CHUNK - at)
+        parts.append(refs[c][at * plan.packed : (at + count) * plan.packed, :])
+        first, size = first + count, size - count
+    return jnp.concatenate(parts, axis=0)
 
 
 def forward_own_kernel(plan, scalars, own_ref, tz_ref, ty_ref, after_ref, *outs):
@@ -268,12 +279,29 @@
         )
 
 
+JOINED = 2
+
+
+def places(refs, plan, sizes, count):
+    joined, cut = refs[:JOINED], refs[JOINED:]
+    result, row = [], 0
+    for i, size in enumerate(sizes):
+        result.append([(ref, row) for ref in joined] + [(ref, 0) for ref in cut[i :: len(sizes)]])
+        row += count * plan.rows * size
+    return result
+
+
+def shapes_of(plan, sizes, count):
+    rows = [count * plan.rows * size for size in sizes]
+    return [(sum(rows), LANES)] * JOINED + [(n, LANES) for n in rows] * (plan.parts - JOINED)
+
+
 def middle_kernel(plan, sizes_in, sizes_out, count, scalars, *refs):
     n = plan.parts
     ins = [refs[k * len(sizes_in) : (k + 1) * len(sizes_in)] for k in range(n)]
     refs = refs[n * len(sizes_in) :]
     screen_ref, tf_ref, tb_ref, after_ref, *refs = refs
-    outs = [refs[k * len(sizes_out) : (k + 1) * len(sizes_out)] for k in range(n)]
+    outs = places(refs, plan, sizes_out, count)
     length = plan.length
     for pair in range(plan.rows // 2):
         for solve in range(count):
@@ -297,26 +325,37 @@
             back = along_rows(tb_ref[0], spectrum * screen)
             for i in range(2):
                 row = pair * 2 + i
-                for k in range(n):
-                    at = k * plan.planes
-                    for ref, size in zip(outs[k], sizes_out):
-                        first = (solve * plan.rows + row) * size
+                at = 0
+                for out, size in zip(outs, sizes_out):
+                    for k, (ref, base) in enumerate(out):
+                        first = base + (solve * plan.rows + row) * size
                         ref[first : first + size, :] = back[
-                            at : at + size, i * LANES : (i + 1) * LANES
+                            k * plan.planes + at : k * plan.planes + at + size,
+                            i * LANES : (i + 1) * LANES,
                         ]
-                        at += size
-
-
-def backward_pair_kernel(plan, scalars, *refs):
+                    at += size
+
+
+def backward_pair_kernel(plan, pieces, piece, scalars, *refs):
     n = plan.parts
     ins, refs = refs[:n], refs[n:]
-    p_ref, q_ref, r_ref, tz_ref, ty_ref, _, total_ref, y_ref, z_ref = refs
+    first, size = sum(pieces[:piece]), pieces[piece]
+    skipped = 2 * plan.rows * first
+    chunks = plan.planes // CHUNK
+    fields = [planes_of(refs[i * chunks : (i + 1) * chunks], first, size, plan) for i in range(3)]
+    tz_ref, ty_ref, _, total_ref, y_ref, z_ref = refs[3 * chunks :]
     even = scalars[1] == 1
     tz, ty = tz_ref[...], ty_ref[0]
-    visit = pack_chunk(load_potential(plan, ins, 0, CHUNK, 0, tz, ty), plan)
-    mixed = pack_chunk(load_potential(plan, ins, plan.rows * CHUNK, CHUNK, 0, tz, ty), plan)
-    p, r = p_ref[...], r_ref[...]
-    other = mixed * q_ref[...]
+
+    def solved(which):
+        base = which * plan.rows * size
+        found = [(ref, base + (skipped if k < JOINED else 0)) for k, ref in enumerate(ins)]
+        wide = load_potential(plan, lambda i: (found, size, i), range(size), tz, ty)
+        return pack_chunk(wide, plan)
+
+    visit, mixed = solved(0), solved(1)
+    p, q, r = fields
+    other = mixed * q
     zero = jnp.zeros_like(other)
     y_ref[...] = mixed * jnp.where(even, r, p)
     z_ref[...] = visit * p + jnp.where(even, other, zero)
@@ -324,31 +363,49 @@
 
 
 def store_result(out_ref, first, value, plan):
-    for i in range(CHUNK):
+    for i in range(value.shape[0] // plan.packed):
         wide = unpack(value[i * plan.packed : (i + 1) * plan.packed], plan)
         out_ref[first + i] = wide[:, : plan.breadth]
 
 
-def backward_own_kernel(plan, scalars, *refs):
-    n = plan.parts
-    ins, refs = refs[:n], refs[n:]
-    chunks = plan.planes // CHUNK
-    totals, refs = refs[:chunks], refs[chunks:]
+LATE = 1
+
+
+def backward_own_kernel(plan, sizes, pieces, scalars, *refs):
+    used = JOINED + (plan.parts - JOINED) * len(sizes)
+    ins, refs = places(refs[:used], plan, sizes, 1), refs[used:]
+    count, chunks = len(pieces), plan.planes // CHUNK
+    ready = count - LATE
+    totals, refs = refs[:count], refs[count:]
     owns, refs = refs[:chunks], refs[chunks:]
-    returned, refs = refs[: 2 * (chunks - 1)], refs[2 * (chunks - 1) :]
-    tz_ref, ty_ref, _, out_ref, rest_ref = refs
-    for c in range(chunks):
-        value = load_potential(plan, ins, 0, plan.planes, c * CHUNK, tz_ref[...], ty_ref[0])
-        value = pack_chunk(value, plan) * owns[c][...] + totals[c][...]
-        if c < chunks - 1:
+    returned, refs = refs[: 2 * ready], refs[2 * ready :]
+    tz_ref, ty_ref, after_ref, out_ref, *rest = refs
+
+    def place(plane):
+        which = 0
+        while plane >= sizes[which]:
+            plane -= sizes[which]
+            which += 1
+        return ins[which], sizes[which], plane
+
+    first = 0
+    for c, size in enumerate(pieces):
+        value = load_potential(plan, place, range(first, first + size), tz_ref[...], ty_ref[0])
+        value = pack_chunk(value, plan) * planes_of(owns, first, size, plan) + totals[c][...]
+        if c < ready:
             value = value + returned[2 * c][...] + returned[2 * c + 1][...]
-            store_result(out_ref, c * CHUNK, value, plan)
+            store_result(out_ref, first, value, plan)
         else:
-            rest_ref[...] = value
-
-
-def final_kernel(plan, scalars, partial_ref, rest_ref, y_ref, z_ref, out_ref):
-    store_result(out_ref, 0, rest_ref[...] + y_ref[...] + z_ref[...], plan)
+            rest[c - ready][...] = value
+        first += size
+
+
+def final_kernel(plan, scalars, partial_ref, *refs):
+    rest, ys, zs, out_ref = refs[:LATE], refs[LATE : 2 * LATE], refs[2 * LATE : 3 * LATE], refs[-1]
+    first = 0
+    for part, y, z in zip(rest, ys, zs):
+        store_result(out_ref, first, part[...] + y[...] + z[...], plan)
+        first += part.shape[0] // plan.packed
 
 
 def call(kernel, scalars, operands, outs, selected=(), chunk=None, after=None, update=None):
@@ -373,7 +430,8 @@
     if update is not None:
         specs[0] = pl.BlockSpec(memory_space=pl.ANY)
         out_specs = [
-            pl.BlockSpec((CHUNK,) + o[1:], lambda i, s, c=update: (c, 0, 0)) for o in outs
+            pl.BlockSpec((update,) + o[1:], lambda i, s, c=o[0] // update - 1: (c, 0, 0))
+            for o in outs
         ]
         aliases = {1: 0}
     return pl.pallas_call(
@@ -390,11 +448,26 @@
     )(scalars, *operands)
 
 
+def send(block, k, parts):
+    return lax.ppermute(block, "grid", [(i, i ^ k) for i in range(parts)])
+
+
 def exchange(blocks, parts):
-    return [blocks[0]] + [
-        lax.ppermute(blocks[k], "grid", [(i, i ^ k) for i in range(parts)])
-        for k in range(1, parts)
-    ]
+    far = [send(blocks[k], k, parts) for k in range(2, parts)]
+    return [blocks[0], send(blocks[1], 1, parts), *far]
+
+
+def exchange_pieces(blocks, parts, count):
+    near = send(blocks[1], 1, parts)
+    far = [send(block, JOINED + i // count, parts) for i, block in enumerate(blocks[JOINED:])]
+    return [blocks[0], near, *far]
+
+
+PIECES = 3
+
+
+def pieces_of(planes):
+    return (planes // PIECES,) * PIECES
 
 
 def exchange_term(bands):
@@ -403,11 +476,11 @@
     own = bands[0]
     plan = Plan(*own.shape, parts)
     part = lax.axis_index("grid")
-    even = 1 - lax.axis_index("band") % 2
+    even = lax.axis_index("band") % 2
     scalars = jnp.stack([part, even]).astype(jnp.int32)
     swap = [(i, i ^ 1) for i in range(number)]
-    behind = [(i, (i - CYCLE) % number) for i in range(number)]
-    ahead = [(i, (i + CYCLE) % number) for i in range(number)]
+    behind = [(i, (i + CYCLE) % number) for i in range(number)]
+    ahead = [(i, (i - CYCLE) % number) for i in range(number)]
     tz = jnp.asarray(plan.table_z())
     ty_forward, ty_backward = (jnp.asarray(t) for t in plan.table_y())
     tx_forward, tx_backward = (jnp.asarray(t) for t in plan.table_x())
@@ -415,7 +488,8 @@
     chunks = plan.planes // CHUNK
     whole = own.shape
     packed = (CHUNK * plan.packed, LANES)
-    sizes = (plan.planes,)
+    sizes = (CHUNK, plan.planes - CHUNK)
+    pieces = pieces_of(plan.planes)
 
     (first,) = call(functools.partial(pack_kernel, plan), scalars, (own,), [packed], chunk=(own, 0))
     q, r = [], []
@@ -437,15 +511,7 @@
     own_in = exchange(blocks, parts)
     for c in range(1, chunks):
         shift(mine[c])
-    (screen,) = call(
-        functools.partial(screen_kernel, plan),
-        scalars,
-        (across, within),
-        [(plan.rows * plan.length, LANES)],
-        (within,),
-        after=blocks[0],
-    )
-    after = screen
+    after = blocks[0]
     pair_in = []
     for c in range(chunks):
         out = call(
@@ -458,37 +524,52 @@
         )
         after = out[0]
         pair_in.append(exchange(out, parts))
+    (screen,) = call(
+        functools.partial(screen_kernel, plan),
+        scalars,
+        (across, within),
+        [(plan.rows * plan.length, LANES)],
+        (within,),
+        after=after,
+    )
 
     def middle(ins, sizes_in, sizes_out, count, after):
-        out = call(
+        return call(
             functools.partial(middle_kernel, plan, sizes_in, sizes_out, count),
             scalars,
             (*[block for part in ins for block in part], screen, tx_forward, tx_backward),
-            [(count * plan.rows * size, LANES) for size in sizes_out] * parts,
+            shapes_of(plan, sizes_out, count),
             (tx_forward, tx_backward),
             after=after,
         )
-        return [out[i :: len(sizes_out)] for i in range(len(sizes_out))]
-
-    own_mid = middle([[b] for b in own_in], (plan.planes,), sizes, 1, after)
-    even_chunks = (CHUNK,) * chunks
+
+    own_mid = middle([[b] for b in own_in], (plan.planes,), sizes, 1, screen)
+    own_back = exchange_pieces(own_mid, parts, len(sizes))
     pair_mid = middle(
         [[pair_in[c][k] for c in range(chunks)] for k in range(parts)],
-        even_chunks,
-        even_chunks,
+        (CHUNK,) * chunks,
+        pieces,
         2,
-        own_mid[0][0],
-    )
-    pair_back = [exchange(blocks, parts) for blocks in pair_mid]
-    own_back = exchange(own_mid[0], parts)
-    after = pair_mid[0][0]
+        own_mid[0],
+    )
+    pair_back = exchange_pieces(pair_mid, parts, len(pieces))
+    after = pair_mid[0]
     totals, from_y, from_z = [], [], []
-    for c in range(chunks):
+    for c, size in enumerate(pieces):
+        piece = (size * plan.packed, LANES)
         total, y, z = call(
-            functools.partial(backward_pair_kernel, plan),
+            functools.partial(backward_pair_kernel, plan, pieces, c),
             scalars,
-            (*pair_back[c], mine[c], q[c], r[c], tz, ty_backward),
-            [packed] * 3,
+            (
+                *pair_back[:JOINED],
+                *pair_back[JOINED + c :: len(pieces)],
+                *mine,
+                *q,
+                *r,
+                tz,
+                ty_backward,
+            ),
+            [piece] * 3,
             (ty_backward,),
             after=after,
         )
@@ -496,27 +577,28 @@
         totals.append(total)
         from_z.append(lax.ppermute(z, "band", ahead))
         from_y.append(lax.ppermute(y, "band", swap))
-    partial, rest = call(
-        functools.partial(backward_own_kernel, plan),
+    ready = len(pieces) - LATE
+    partial, *rest = call(
+        functools.partial(backward_own_kernel, plan, sizes, pieces),
         scalars,
         (
             *own_back,
             *totals,
             *mine,
-            *[part[c] for c in range(chunks - 1) for part in (from_y, from_z)],
+            *[part[c] for c in range(ready) for part in (from_y, from_z)],
             tz,
             ty_backward,
         ),
-        [whole, packed],
+        [whole] + [(size * plan.packed, LANES) for size in pieces[ready:]],
         (ty_backward,),
         after=after,
     )
     (result,) = call(
         functools.partial(final_kernel, plan),
         scalars,
-        (partial, rest, from_y[-1], from_z[-1]),
+        (partial, *rest, *from_y[ready:], *from_z[ready:]),
         [whole],
-        update=chunks - 1,
+        update=sum(pieces[ready:]),
     )
     return result[None]
 

time: 112 us -> 110 us (0.982)
  starting transfers between devices: 37.1 us -> 34.3 us
    ppermute x3, waiting for transfers between devices: 1.95 us -> 5.18 us  [shift(): q.append(lax.ppermute(chunk, 'band', swap))]
    ppermute x3, starting transfers between devices: 5.33 us -> 2.64 us  [exchange_term(): from_z.append(lax.ppermute(z, 'band', ahead))]
    ppermute x3, waiting for transfers between devices: 6.41 us -> 3.83 us  [shift(): r.append(lax.ppermute(chunk, 'band', behind))]
    ppermute x24, waiting for transfers between devices: 31.8 us -> 29.8 us  [send(): return lax.ppermute(block, 'grid', [(i, i ^ k) for i in range(parts)])]
    ppermute x3, waiting for transfers between devices: 0.01 us -> 1.75 us  [exchange_term(): from_y.append(lax.ppermute(y, 'band', swap))]
    ppermute x3, starting transfers between devices: 3.55 us -> 5.09 us  [shift(): q.append(lax.ppermute(chunk, 'band', swap))]
  transfers between devices with their start and end apart: 36 -> 36, of which waited for: 18 -> 22; matrix products, arithmetic and copies ran while one was open for 0% -> 0% of each run, Pallas kernels for 14% -> 13%
where the time goes in v3:
time: 110 us; the launch traced here: 109 us
  waiting for transfers between devices  53.6 us (49%)
  starting transfers between devices  34.3 us (31%)
  Pallas kernels  19.9 us (18%)
  local copies, waits for them, and re-layouts  1.36 us (1%)
    ppermute x24, waiting for transfers between devices, send(): return lax.ppermute(block, 'grid', [(i, i ^ k) for i in range(parts)])  29.8 us
    pallas_call x13, Pallas kernels, call(): pl.pallas_call(kernel, grid_spec=pltpu.PrefetchScalarGridSpec(num_scalar_...  19.9 us
    ppermute x24, starting transfers between devices, send(): return lax.ppermute(block, 'grid', [(i, i ^ k) for i in range(parts)])  18.7 us
    ppermute x3, waiting for transfers between devices, exchange_term(): from_z.append(lax.ppermute(z, 'band', ahead))  13 us
    ppermute x3, starting transfers between devices, shift(): r.append(lax.ppermute(chunk, 'band', behind))  5.23 us
    ppermute x3, waiting for transfers between devices, shift(): q.append(lax.ppermute(chunk, 'band', swap))  5.18 us
    ppermute x3, starting transfers between devices, shift(): q.append(lax.ppermute(chunk, 'band', swap))  5.09 us
    ppermute x3, waiting for transfers between devices, shift(): r.append(lax.ppermute(chunk, 'band', behind))  3.83 us
  transfers between devices with their start and end apart: 36, of which 22 were waited for; matrix products, arithmetic and copies ran while one was open for 0% of the time, Pallas kernels for 13%

profile of v3, /device:TPU:0, one launch (start us, length us, event | category | flops | bytes accessed | tf_op | source)
XLA Modules:
  0.0 109.4 jit_solution(6654840488664551272)
XLA Ops:
  0.0 0.1 pad_add_fusion.scalars
  0.1 1.3 %copy-done.3 = f32[1,24,96,96]{3,2,1,0:T(8,128)S(1)} copy-done((f32[1,24,96,96]{3,2,1,0:T(8,128)S(1)}, f32[1,24,96,96]{3,2,1,0:T(8,128)}, u32[]{:S(2)}) %copy-start.3) | copy-done | bytes 884760
  1.4 0.7 shard_map.82.after_ref.p_ref.refs_4_.refs_9_
  2.1 1.8 %shard_map.83 = (f32[432,128]{1,0:T(8,128)S(1)}, f32[432,128]{1,0:T(8,128)S(1)}, f32[432,128]{1,0:T(8,128)S(1)}, f32[432,128]{1,0:T(8,128)S(1)}, f32[576,128]{1,0:T(8,128)S(1)}, /*index=5*/f32[576,128]{1,0:T(8,128)S(1)}) custom-call(s32[2]{0:T(128)S(1)} %pad_add_fusion.scalars, f32[24,96,96]{2,1,0:T(8,128)S(1)} %bitcast.5, bf16[256,256]{1,0:T(8,128)(2,1)S(1)} %copy-done, ...), custom_call_target="tpu_custom_call" | custom-call | tf_op jit(solution)/shard_map/pallas_call | solution.py:437
  4.0 3.1 %collective-permute-start.5 = (f32[576,128]{1,0:T(8,128)S(1)}, f32[576,128]{1,0:T(8,128)S(1)}, u32[]{:S(2)}, u32[]{:S(2)}) collective-permute-start(f32[576,128]{1,0:T(8,128)S(1)} %get-tuple-element.53.p_ref.refs_5_.refs_10_), channel_id=1, source_target_pairs={{0,4},{4,0},{8,12},{12,8},{16,20},{20,16},{24,28},{28,24},{1,5},{5... | collective-permute-start | bytes 884744 | tf_op jit(solution)/shard_map/ppermute | solution.py:498
  7.0 1.6 %collective-permute-start.6 = (f32[576,128]{1,0:T(8,128)S(1)}, f32[576,128]{1,0:T(8,128)S(1)}, u32[]{:S(2)}, u32[]{:S(2)}) collective-permute-start(f32[576,128]{1,0:T(8,128)S(1)} %get-tuple-element.53.p_ref.refs_5_.refs_10_), channel_id=1, source_target_pairs={{0,8},{4,12},{8,16},{12,20},{16,24},{20,28},{24,0},{28,4},{1,9},{5... | collective-permute-start | bytes 884744 | tf_op jit(solution)/shard_map/ppermute | solution.py:499
  8.6 0.5 collective-permute-start.7
  9.1 1.6 %collective-permute-start.8 = (f32[576,128]{1,0:T(8,128)S(1)}, f32[576,128]{1,0:T(8,128)S(1)}, u32[]{:S(2)}, u32[]{:S(2)}) collective-permute-start(f32[576,128]{1,0:T(8,128)S(1)} %shard_map.82.after_ref.p_ref.refs_4_.refs_9_), channel_id=1, source_target_pairs={{0,8},{4,12},{8,16},{12,20},{16,24},{20,28},{24,0},{28,4},{1,9},{5... | collective-permute-start | bytes 884744 | tf_op jit(solution)/shard_map/ppermute | solution.py:499
  10.7 1.5 %collective-permute-start.3 = (f32[576,128]{1,0:T(8,128)S(1)}, f32[576,128]{1,0:T(8,128)S(1)}, u32[]{:S(2)}, u32[]{:S(2)}) collective-permute-start(f32[576,128]{1,0:T(8,128)S(1)} %get-tuple-element.52.p_ref.refs_6_.refs_11_), channel_id=1, source_target_pairs={{0,4},{4,0},{8,12},{12,8},{16,20},{20,16},{24,28},{28,24},{1,5},{5... | collective-permute-start | bytes 884744 | tf_op jit(solution)/shard_map/ppermute | solution.py:498
  12.2 2.7 %collective-permute-done.5.q_ref.refs_8_ = f32[576,128]{1,0:T(8,128)S(1)} collective-permute-done((f32[576,128]{1,0:T(8,128)S(1)}, f32[576,128]{1,0:T(8,128)S(1)}, u32[]{:S(2)}, u32[]{:S(2)}) %collective-permute-start.5) | collective-permute-done | bytes 294944 | tf_op jit(solution)/shard_map/ppermute | solution.py:498
  14.9 2.1 %collective-permute-start.4 = (f32[576,128]{1,0:T(8,128)S(1)}, f32[576,128]{1,0:T(8,128)S(1)}, u32[]{:S(2)}, u32[]{:S(2)}) collective-permute-start(f32[576,128]{1,0:T(8,128)S(1)} %get-tuple-element.52.p_ref.refs_6_.refs_11_), channel_id=1, source_target_pairs={{0,8},{4,12},{8,16},{12,20},{16,24},{20,28},{24,0},{28,4},{1,9},{5... | collective-permute-start | bytes 884744 | tf_op jit(solution)/shard_map/ppermute | solution.py:499
  17.0 1.7 %collective-permute-done.6.r_ref.refs_11_ = f32[576,128]{1,0:T(8,128)S(1)} collective-permute-done((f32[576,128]{1,0:T(8,128)S(1)}, f32[576,128]{1,0:T(8,128)S(1)}, u32[]{:S(2)}, u32[]{:S(2)}) %collective-permute-start.6) | collective-permute-done | bytes 294944 | tf_op jit(solution)/shard_map/ppermute | solution.py:499
  18.7 2.5 %collective-permute-done.7.q_ref.refs_7_ = f32[576,128]{1,0:T(8,128)S(1)} collective-permute-done((f32[576,128]{1,0:T(8,128)S(1)}, f32[576,128]{1,0:T(8,128)S(1)}, u32[]{:S(2)}, u32[]{:S(2)}) %collective-permute-start.7) | collective-permute-done | bytes 294944 | tf_op jit(solution)/shard_map/ppermute | solution.py:498
  21.2 2.0 %collective-permute-start.1 = (f32[432,128]{1,0:T(8,128)S(1)}, f32[432,128]{1,0:T(8,128)S(1)}, u32[]{:S(2)}, u32[]{:S(2)}) collective-permute-start(f32[432,128]{1,0:T(8,128)S(1)} %get-tuple-element.50), channel_id=1, source_target_pairs={{0,2},{1,3},{2,0},{3,1},{4,6},{5,7},{6,4},{7,5},{8,10},{9,11},{10,... | collective-permute-start | bytes 663560 | tf_op jit(solution)/shard_map/ppermute | solution.py:452
  23.2 1.8 %collective-permute-done.8.r_ref.refs_10_ = f32[576,128]{1,0:T(8,128)S(1)} collective-permute-done((f32[576,128]{1,0:T(8,128)S(1)}, f32[576,128]{1,0:T(8,128)S(1)}, u32[]{:S(2)}, u32[]{:S(2)}) %collective-permute-start.8) | collective-permute-done | bytes 294944 | tf_op jit(solution)/shard_map/ppermute | solution.py:499
  25.0 1.5 %shard_map.84 = (f32[288,128]{1,0:T(8,128)S(1)}, f32[288,128]{1,0:T(8,128)S(1)}, f32[288,128]{1,0:T(8,128)S(1)}, f32[288,128]{1,0:T(8,128)S(1)}) custom-call(s32[2]{0:T(128)S(1)} %pad_add_fusion.scalars, f32[576,128]{1,0:T(8,128)S(1)} %shard_map.82.after_ref.p_ref.refs_4_.refs_9_, f32[576,128]{1,0:T(8,128)S(1)} %collective-permute-done.7.q_ref.refs_7_, ...), custom_call_target="tpu_custom_call" | custom-call | tf_op jit(solution)/shard_map/pallas_call | solution.py:437
  26.5 1.5 %shard_map.85 = (f32[288,128]{1,0:T(8,128)S(1)}, f32[288,128]{1,0:T(8,128)S(1)}, f32[288,128]{1,0:T(8,128)S(1)}, f32[288,128]{1,0:T(8,128)S(1)}) custom-call(s32[2]{0:T(128)S(1)} %pad_add_fusion.scalars, f32[576,128]{1,0:T(8,128)S(1)} %get-tuple-element.53.p_ref.refs_5_.refs_10_, f32[576,128]{1,0:T(8,128)S(1)} %collective-permute-done.5.q_ref.refs_8_, ...), custom_call_target="tpu_custom_call" | custom-call | tf_op jit(solution)/shard_map/pallas_call | solution.py:437
  28.0 1.7 %collective-permute-start.14 = (f32[288,128]{1,0:T(8,128)S(1)}, f32[288,128]{1,0:T(8,128)S(1)}, u32[]{:S(2)}, u32[]{:S(2)}) collective-permute-start(f32[288,128]{1,0:T(8,128)S(1)} %get-tuple-element.63), channel_id=1, source_target_pairs={{0,1},{1,0},{2,3},{3,2},{4,5},{5,4},{6,7},{7,6},{8,9},{9,8},{10,11... | collective-permute-start | bytes 442376 | tf_op jit(solution)/shard_map/ppermute | solution.py:452
  29.7 0.3 collective-permute-done.4.r_ref.refs_12_
  30.0 1.5 %shard_map.86 = (f32[288,128]{1,0:T(8,128)S(1)}, f32[288,128]{1,0:T(8,128)S(1)}, f32[288,128]{1,0:T(8,128)S(1)}, f32[288,128]{1,0:T(8,128)S(1)}) custom-call(s32[2]{0:T(128)S(1)} %pad_add_fusion.scalars, f32[576,128]{1,0:T(8,128)S(1)} %get-tuple-element.52.p_ref.refs_6_.refs_11_, f32[576,128]{1,0:T(8,128)S(1)} %collective-permute-done.3.q_ref.refs_9_, ...), custom_call_target="tpu_custom_call" | custom-call | tf_op jit(solution)/shard_map/pallas_call | solution.py:437
  31.5 0.6 collective-permute-start.16
  32.1 1.5 %collective-permute-start.17 = (f32[288,128]{1,0:T(8,128)S(1)}, f32[288,128]{1,0:T(8,128)S(1)}, u32[]{:S(2)}, u32[]{:S(2)}) collective-permute-start(f32[288,128]{1,0:T(8,128)S(1)} %get-tuple-element.66), channel_id=1, source_target_pairs={{0,2},{1,3},{2,0},{3,1},{4,6},{5,7},{6,4},{7,5},{8,10},{9,11},{10,... | collective-permute-start | bytes 442376 | tf_op jit(solution)/shard_map/ppermute | solution.py:452
  33.6 0.5 collective-permute-start.18
  34.1 1.5 %collective-permute-start.19 = (f32[288,128]{1,0:T(8,128)S(1)}, f32[288,128]{1,0:T(8,128)S(1)}, u32[]{:S(2)}, u32[]{:S(2)}) collective-permute-start(f32[288,128]{1,0:T(8,128)S(1)} %get-tuple-element.68), channel_id=1, source_target_pairs={{0,2},{1,3},{2,0},{3,1},{4,6},{5,7},{6,4},{7,5},{8,10},{9,11},{10,... | collective-permute-start | bytes 442376 | tf_op jit(solution)/shard_map/ppermute | solution.py:452
  35.6 1.7 %collective-permute-start.21 = (f32[288,128]{1,0:T(8,128)S(1)}, f32[288,128]{1,0:T(8,128)S(1)}, u32[]{:S(2)}, u32[]{:S(2)}) collective-permute-start(f32[288,128]{1,0:T(8,128)S(1)} %get-tuple-element.70), channel_id=1, source_target_pairs={{0,3},{1,2},{2,1},{3,0},{4,7},{5,6},{6,5},{7,4},{8,11},{9,10},{10,... | collective-permute-start | bytes 442376 | tf_op jit(solution)/shard_map/ppermute | solution.py:452
  37.4 1.4 %collective-permute-done.17.refs_6_ = f32[288,128]{1,0:T(8,128)S(1)} collective-permute-done((f32[288,128]{1,0:T(8,128)S(1)}, f32[288,128]{1,0:T(8,128)S(1)}, u32[]{:S(2)}, u32[]{:S(2)}) %collective-permute-start.17) | collective-permute-done | bytes 147488 | tf_op jit(solution)/shard_map/ppermute | solution.py:452
  38.8 0.9 shard_map.87.refs_4_.refs_7_.refs_12_
  39.7 1.4 %shard_map.88 = (f32[432,128]{1,0:T(8,128)S(1)}, f32[432,128]{1,0:T(8,128)S(1)}, f32[144,128]{1,0:T(8,128)S(1)}, f32[288,128]{1,0:T(8,128)S(1)}, f32[144,128]{1,0:T(8,128)S(1)}, /*index=5*/f32[288,128]{1,0:T(8,128)S(1)}) custom-call(s32[2]{0:T(128)S(1)} %pad_add_fusion.scalars, f32[432,128]{1,0:T(8,128)S(1)} %get-tuple-element.48.after_ref.refs_0_, ...), custom_call_target="tpu_custom_call" | custom-call | tf_op jit(solution)/shard_map/pallas_call | solution.py:437
  41.1 0.9 collective-permute-done.18.refs_7_
  42.0 3.2 %collective-permute-done.19.refs_8_ = f32[288,128]{1,0:T(8,128)S(1)} collective-permute-done((f32[288,128]{1,0:T(8,128)S(1)}, f32[288,128]{1,0:T(8,128)S(1)}, u32[]{:S(2)}, u32[]{:S(2)}) %collective-permute-start.19) | collective-permute-done | bytes 147488 | tf_op jit(solution)/shard_map/ppermute | solution.py:452
  45.1 2.2 %collective-permute-done.20.refs_9_ = f32[288,128]{1,0:T(8,128)S(1)} collective-permute-done((f32[288,128]{1,0:T(8,128)S(1)}, f32[288,128]{1,0:T(8,128)S(1)}, u32[]{:S(2)}, u32[]{:S(2)}) %collective-permute-start.20) | collective-permute-done | bytes 147488 | tf_op jit(solution)/shard_map/ppermute | solution.py:452
  47.3 3.2 %collective-permute-done.21.refs_10_ = f32[288,128]{1,0:T(8,128)S(1)} collective-permute-done((f32[288,128]{1,0:T(8,128)S(1)}, f32[288,128]{1,0:T(8,128)S(1)}, u32[]{:S(2)}, u32[]{:S(2)}) %collective-permute-start.21) | collective-permute-done | bytes 147488 | tf_op jit(solution)/shard_map/ppermute | solution.py:452
  50.4 2.4 %collective-permute-done.22.refs_11_ = f32[288,128]{1,0:T(8,128)S(1)} collective-permute-done((f32[288,128]{1,0:T(8,128)S(1)}, f32[288,128]{1,0:T(8,128)S(1)}, u32[]{:S(2)}, u32[]{:S(2)}) %collective-permute-start.22) | collective-permute-done | bytes 147488 | tf_op jit(solution)/shard_map/ppermute | solution.py:452
  52.8 1.9 %shard_map.89 = (f32[864,128]{1,0:T(8,128)S(1)}, f32[864,128]{1,0:T(8,128)S(1)}, f32[288,128]{1,0:T(8,128)S(1)}, f32[288,128]{1,0:T(8,128)S(1)}, f32[288,128]{1,...) custom-call(s32[2]{0:T(128)S(1)} %pad_add_fusion.scalars, ...), custom_call_target="tpu_custom_call" | custom-call | tf_op jit(solution)/shard_map/pallas_call | solution.py:437
  54.7 0.8 collective-permute-start.23
  55.5 1.5 %collective-permute-start.24 = (f32[288,128]{1,0:T(8,128)S(1)}, f32[288,128]{1,0:T(8,128)S(1)}, u32[]{:S(2)}, u32[]{:S(2)}) collective-permute-start(f32[288,128]{1,0:T(8,128)S(1)} %get-tuple-element.74), channel_id=1, source_target_pairs={{0,2},{1,3},{2,0},{3,1},{4,6},{5,7},{6,4},{7,5},{8,10},{9,11},{10,... | collective-permute-start | bytes 442376 | tf_op jit(solution)/shard_map/ppermute | solution.py:452
  57.0 1.4 %collective-permute-start.26 = (f32[288,128]{1,0:T(8,128)S(1)}, f32[288,128]{1,0:T(8,128)S(1)}, u32[]{:S(2)}, u32[]{:S(2)}) collective-permute-start(f32[288,128]{1,0:T(8,128)S(1)} %get-tuple-element.77), channel_id=1, source_target_pairs={{0,2},{1,3},{2,0},{3,1},{4,6},{5,7},{6,4},{7,5},{8,10},{9,11},{10,... | collective-permute-start | bytes 442376 | tf_op jit(solution)/shard_map/ppermute | solution.py:452
  58.4 0.6 collective-permute-start.10
  59.0 3.2 %collective-permute-done.24.refs_2_ = f32[288,128]{1,0:T(8,128)S(1)} collective-permute-done((f32[288,128]{1,0:T(8,128)S(1)}, f32[288,128]{1,0:T(8,128)S(1)}, u32[]{:S(2)}, u32[]{:S(2)}) %collective-permute-start.24) | collective-permute-done | bytes 147488 | tf_op jit(solution)/shard_map/ppermute | solution.py:452
  62.2 2.2 %collective-permute-done.25.refs_3_ = f32[288,128]{1,0:T(8,128)S(1)} collective-permute-done((f32[288,128]{1,0:T(8,128)S(1)}, f32[288,128]{1,0:T(8,128)S(1)}, u32[]{:S(2)}, u32[]{:S(2)}) %collective-permute-start.25) | collective-permute-done | bytes 147488 | tf_op jit(solution)/shard_map/ppermute | solution.py:452
  64.4 0.7 collective-permute-start.28
  65.1 1.5 %shard_map.90 = (f32[576,128]{1,0:T(8,128)S(1)}, f32[576,128]{1,0:T(8,128)S(1)}, f32[576,128]{1,0:T(8,128)S(1)}) custom-call(s32[2]{0:T(128)S(1)} %pad_add_fusion.scalars, f32[864,128]{1,0:T(8,128)S(1)} %get-tuple-element.72.refs_0_.refs_15_, f32[864,128]{1,0:T(8,128)S(1)} %collective-permute-done.23.refs_1_, ...), custom_call_target="tpu_custom_call" | custom-call | tf_op jit(solution)/shard_map/pallas_call | solution.py:437
  66.6 0.6 collective-permute-start.30
  67.2 2.9 %collective-permute-done.10.refs_2_ = f32[144,128]{1,0:T(8,128)S(1)} collective-permute-done((f32[144,128]{1,0:T(8,128)S(1)}, f32[144,128]{1,0:T(8,128)S(1)}, u32[]{:S(2)}, u32[]{:S(2)}) %collective-permute-start.10) | collective-permute-done | bytes 73760 | tf_op jit(solution)/shard_map/ppermute | solution.py:452
  70.1 1.6 %collective-permute-start.9 = (f32[432,128]{1,0:T(8,128)S(1)}, f32[432,128]{1,0:T(8,128)S(1)}, u32[]{:S(2)}, u32[]{:S(2)}) collective-permute-start(f32[432,128]{1,0:T(8,128)S(1)} %get-tuple-element.58), channel_id=1, source_target_pairs={{0,1},{1,0},{2,3},{3,2},{4,5},{5,4},{6,7},{7,6},{8,9},{9,8},{10,11... | collective-permute-start | bytes 663560 | tf_op jit(solution)/shard_map/ppermute | solution.py:452
  71.7 0.6 collective-permute-done.27.refs_3_
  72.3 0.7 collective-permute-start.11
  73.0 3.4 %collective-permute-done.28.refs_2_ = f32[288,128]{1,0:T(8,128)S(1)} collective-permute-done((f32[288,128]{1,0:T(8,128)S(1)}, f32[288,128]{1,0:T(8,128)S(1)}, u32[]{:S(2)}, u32[]{:S(2)}) %collective-permute-start.28) | collective-permute-done | bytes 147488 | tf_op jit(solution)/shard_map/ppermute | solution.py:452
  76.4 2.2 %collective-permute-done.29.refs_3_ = f32[288,128]{1,0:T(8,128)S(1)} collective-permute-done((f32[288,128]{1,0:T(8,128)S(1)}, f32[288,128]{1,0:T(8,128)S(1)}, u32[]{:S(2)}, u32[]{:S(2)}) %collective-permute-start.29) | collective-permute-done | bytes 147488 | tf_op jit(solution)/shard_map/ppermute | solution.py:452
  78.6 1.9 %collective-permute-start.12 = (f32[144,128]{1,0:T(8,128)S(1)}, f32[144,128]{1,0:T(8,128)S(1)}, u32[]{:S(2)}, u32[]{:S(2)}) collective-permute-start(f32[144,128]{1,0:T(8,128)S(1)} %get-tuple-element.61), channel_id=1, source_target_pairs={{0,3},{1,2},{2,1},{3,0},{4,7},{5,6},{6,5},{7,4},{8,11},{9,10},{10,... | collective-permute-start | bytes 221192 | tf_op jit(solution)/shard_map/ppermute | solution.py:452
  80.5 1.5 %shard_map.91 = (f32[576,128]{1,0:T(8,128)S(1)}, f32[576,128]{1,0:T(8,128)S(1)}, f32[576,128]{1,0:T(8,128)S(1)}) custom-call(s32[2]{0:T(128)S(1)} %pad_add_fusion.scalars, f32[864,128]{1,0:T(8,128)S(1)} %get-tuple-element.72.refs_0_.refs_15_, f32[864,128]{1,0:T(8,128)S(1)} %collective-permute-done.23.refs_1_, ...), custom_call_target="tpu_custom_call" | custom-call | tf_op jit(solution)/shard_map/pallas_call | solution.py:437
  82.0 1.5 %shard_map.92 = (f32[576,128]{1,0:T(8,128)S(1)}, f32[576,128]{1,0:T(8,128)S(1)}, f32[576,128]{1,0:T(8,128)S(1)}) custom-call(s32[2]{0:T(128)S(1)} %pad_add_fusion.scalars, f32[864,128]{1,0:T(8,128)S(1)} %get-tuple-element.72.refs_0_.refs_15_, f32[864,128]{1,0:T(8,128)S(1)} %collective-permute-done.23.refs_1_, ...), custom_call_target="tpu_custom_call" | custom-call | tf_op jit(solution)/shard_map/pallas_call | solution.py:437
  83.6 2.1 %collective-permute-done.12.refs_4_ = f32[144,128]{1,0:T(8,128)S(1)} collective-permute-done((f32[144,128]{1,0:T(8,128)S(1)}, f32[144,128]{1,0:T(8,128)S(1)}, u32[]{:S(2)}, u32[]{:S(2)}) %collective-permute-start.12) | collective-permute-done | bytes 73760 | tf_op jit(solution)/shard_map/ppermute | solution.py:452
  85.7 1.7 %collective-permute-start.31 = (f32[576,128]{1,0:T(8,128)S(1)}, f32[576,128]{1,0:T(8,128)S(1)}, u32[]{:S(2)}, u32[]{:S(2)}) collective-permute-start(f32[576,128]{1,0:T(8,128)S(1)} %get-tuple-element.84), channel_id=1, source_target_pairs={{0,24},{4,28},{8,0},{12,4},{16,8},{20,12},{24,16},{28,20},{1,25},{... | collective-permute-start | bytes 884744 | tf_op jit(solution)/shard_map/ppermute | solution.py:578
  87.4 1.3 %collective-permute-start.32 = (f32[576,128]{1,0:T(8,128)S(1)}, f32[576,128]{1,0:T(8,128)S(1)}, u32[]{:S(2)}, u32[]{:S(2)}) collective-permute-start(f32[576,128]{1,0:T(8,128)S(1)} %get-tuple-element.85), channel_id=1, source_target_pairs={{0,4},{4,0},{8,12},{12,8},{16,20},{20,16},{24,28},{28,24},{1,5},{5... | collective-permute-start | bytes 884744 | tf_op jit(solution)/shard_map/ppermute | solution.py:579
  88.7 0.5 collective-permute-start.33
  89.2 0.7 collective-permute-start.34
  89.9 0.4 collective-permute-start.35
  90.4 5.2 %collective-permute-done.31.refs_13_ = f32[576,128]{1,0:T(8,128)S(1)} collective-permute-done((f32[576,128]{1,0:T(8,128)S(1)}, f32[576,128]{1,0:T(8,128)S(1)}, u32[]{:S(2)}, u32[]{:S(2)}) %collective-permute-start.31) | collective-permute-done | bytes 294944 | tf_op jit(solution)/shard_map/ppermute | solution.py:578
  95.6 1.7 %collective-permute-done.32.refs_14_ = f32[576,128]{1,0:T(8,128)S(1)} collective-permute-done((f32[576,128]{1,0:T(8,128)S(1)}, f32[576,128]{1,0:T(8,128)S(1)}, u32[]{:S(2)}, u32[]{:S(2)}) %collective-permute-start.32) | collective-permute-done | bytes 294944 | tf_op jit(solution)/shard_map/ppermute | solution.py:579
  97.3 4.6 %collective-permute-done.33.refs_15_ = f32[576,128]{1,0:T(8,128)S(1)} collective-permute-done((f32[576,128]{1,0:T(8,128)S(1)}, f32[576,128]{1,0:T(8,128)S(1)}, u32[]{:S(2)}, u32[]{:S(2)}) %collective-permute-start.33) | collective-permute-done | bytes 294944 | tf_op jit(solution)/shard_map/ppermute | solution.py:578
  101.9 2.8 %shard_map.93 = (f32[24,96,96]{2,1,0:T(8,128)}, f32[576,128]{1,0:T(8,128)S(1)}) custom-call(s32[2]{0:T(128)S(1)} %pad_add_fusion.scalars, f32[432,128]{1,0:T(8,128)S(1)} %get-tuple-element.57.refs_15_.refs_0_, f32[432,128]{1,0:T(8,128)S(1)} %collective-permute-done.9.refs_1_, f32[144,128]{1,0:T(8,128)S(1)} %collective-permute-done.10.refs_2_, ...), custom_call_target="tpu_custom_call" | custom-call | tf_op jit(solution)/shard_map/pallas_call | solution.py:437
  104.7 3.3 %collective-permute-done.35.refs_2_ = f32[576,128]{1,0:T(8,128)S(1)} collective-permute-done((f32[576,128]{1,0:T(8,128)S(1)}, f32[576,128]{1,0:T(8,128)S(1)}, u32[]{:S(2)}, u32[]{:S(2)}) %collective-permute-start.35) | collective-permute-done | bytes 294944 | tf_op jit(solution)/shard_map/ppermute | solution.py:578
  108.0 1.4 %shard_map.94 = f32[24,96,96]{2,1,0:T(8,128)} custom-call(s32[2]{0:T(128)S(1)} %pad_add_fusion.scalars, f32[24,96,96]{2,1,0:T(8,128)} %get-tuple-element.87.partial_ref, f32[576,128]{1,0:T(8,128)S(1)} %get-tuple-element.88.refs_0_, f32[576,128]{1,0:T(8,128)S(1)} %collective-permute-done.34.refs_1_, ...), custom_call_target="tpu_custom_call", output_to_operand_aliasing={{}: (1, {})} | custom-call | tf_op jit(solution)/shard_map/pallas_call | solution.py:437
  (38 shorter events, 0.1 us)
Async XLA Ops:
  0.0 2.1 %copy-start = (bf16[256,256]{1,0:T(8,128)(2,1)S(1)}, bf16[256,256]{1,0:T(8,128)(2,1)}, u32[]{:S(2)}) copy-start(bf16[256,256]{1,0:T(8,128)(2,1)} %constant.36.clone.tz_ref.refs_13_.refs_16_) | copy-start | bytes 393220
  0.0 2.1 %copy-start.1 = (bf16[4,256,192]{2,1,0:T(8,128)(2,1)S(1)}, bf16[4,256,192]{2,1,0:T(8,128)(2,1)}, u32[]{:S(2)}) copy-start(bf16[4,256,192]{2,1,0:T(8,128)(2,1)} %constant.37.clone.ty_ref) | copy-start | bytes 1179652
  0.1 1.3 %copy-start.3 = (f32[1,24,96,96]{3,2,1,0:T(8,128)S(1)}, f32[1,24,96,96]{3,2,1,0:T(8,128)}, u32[]{:S(2)}) copy-start(f32[1,24,96,96]{3,2,1,0:T(8,128)} %param.8) | copy-start | bytes 2654212
  4.0 10.9 %collective-permute-start.5 = (f32[576,128]{1,0:T(8,128)S(1)}, f32[576,128]{1,0:T(8,128)S(1)}, u32[]{:S(2)}, u32[]{:S(2)}) collective-permute-start(f32[576,128]{1,0:T(8,128)S(1)} %get-tuple-element.53.p_ref.refs_5_.refs_10_), channel_id=1, source_target_pairs={{0,4},{4,0},{8,12},{12,8},{16,20},{20,16},{24,28},{28,24},{1,5},{5... | collective-permute-start | bytes 884744 | tf_op jit(solution)/shard_map/ppermute | solution.py:498
  7.0 11.7 %collective-permute-start.6 = (f32[576,128]{1,0:T(8,128)S(1)}, f32[576,128]{1,0:T(8,128)S(1)}, u32[]{:S(2)}, u32[]{:S(2)}) collective-permute-start(f32[576,128]{1,0:T(8,128)S(1)} %get-tuple-element.53.p_ref.refs_5_.refs_10_), channel_id=1, source_target_pairs={{0,8},{4,12},{8,16},{12,20},{16,24},{20,28},{24,0},{28,4},{1,9},{5... | collective-permute-start | bytes 884744 | tf_op jit(solution)/shard_map/ppermute | solution.py:499
  8.6 12.6 %collective-permute-start.7 = (f32[576,128]{1,0:T(8,128)S(1)}, f32[576,128]{1,0:T(8,128)S(1)}, u32[]{:S(2)}, u32[]{:S(2)}) collective-permute-start(f32[576,128]{1,0:T(8,128)S(1)} %shard_map.82.after_ref.p_ref.refs_4_.refs_9_), channel_id=1, source_target_pairs={{0,4},{4,0},{8,12},{12,8},{16,20},{20,16},{24,28},{28,24},{1,5},{5... | collective-permute-start | bytes 884744 | tf_op jit(solution)/shard_map/ppermute | solution.py:498
  9.1 15.9 %collective-permute-start.8 = (f32[576,128]{1,0:T(8,128)S(1)}, f32[576,128]{1,0:T(8,128)S(1)}, u32[]{:S(2)}, u32[]{:S(2)}) collective-permute-start(f32[576,128]{1,0:T(8,128)S(1)} %shard_map.82.after_ref.p_ref.refs_4_.refs_9_), channel_id=1, source_target_pairs={{0,8},{4,12},{8,16},{12,20},{16,24},{20,28},{24,0},{28,4},{1,9},{5... | collective-permute-start | bytes 884744 | tf_op jit(solution)/shard_map/ppermute | solution.py:499
  10.7 17.4 %collective-permute-start.3 = (f32[576,128]{1,0:T(8,128)S(1)}, f32[576,128]{1,0:T(8,128)S(1)}, u32[]{:S(2)}, u32[]{:S(2)}) collective-permute-start(f32[576,128]{1,0:T(8,128)S(1)} %get-tuple-element.52.p_ref.refs_6_.refs_11_), channel_id=1, source_target_pairs={{0,4},{4,0},{8,12},{12,8},{16,20},{20,16},{24,28},{28,24},{1,5},{5... | collective-permute-start | bytes 884744 | tf_op jit(solution)/shard_map/ppermute | solution.py:498
  14.9 15.1 %collective-permute-start.4 = (f32[576,128]{1,0:T(8,128)S(1)}, f32[576,128]{1,0:T(8,128)S(1)}, u32[]{:S(2)}, u32[]{:S(2)}) collective-permute-start(f32[576,128]{1,0:T(8,128)S(1)} %get-tuple-element.52.p_ref.refs_6_.refs_11_), channel_id=1, source_target_pairs={{0,8},{4,12},{8,16},{12,20},{16,24},{20,28},{24,0},{28,4},{1,9},{5... | collective-permute-start | bytes 884744 | tf_op jit(solution)/shard_map/ppermute | solution.py:499
  18.7 12.8 %collective-permute-start = (f32[432,128]{1,0:T(8,128)S(1)}, f32[432,128]{1,0:T(8,128)S(1)}, u32[]{:S(2)}, u32[]{:S(2)}) collective-permute-start(f32[432,128]{1,0:T(8,128)S(1)} %get-tuple-element.49), channel_id=1, source_target_pairs={{0,1},{1,0},{2,3},{3,2},{4,5},{5,4},{6,7},{7,6},{8,9},{9,8},{10,11... | collective-permute-start | bytes 663560 | tf_op jit(solution)/shard_map/ppermute | solution.py:452
  21.2 10.9 %collective-permute-start.1 = (f32[432,128]{1,0:T(8,128)S(1)}, f32[432,128]{1,0:T(8,128)S(1)}, u32[]{:S(2)}, u32[]{:S(2)}) collective-permute-start(f32[432,128]{1,0:T(8,128)S(1)} %get-tuple-element.50), channel_id=1, source_target_pairs={{0,2},{1,3},{2,0},{3,1},{4,6},{5,7},{6,4},{7,5},{8,10},{9,11},{10,... | collective-permute-start | bytes 663560 | tf_op jit(solution)/shard_map/ppermute | solution.py:452
  25.0 8.5 %collective-permute-start.2 = (f32[432,128]{1,0:T(8,128)S(1)}, f32[432,128]{1,0:T(8,128)S(1)}, u32[]{:S(2)}, u32[]{:S(2)}) collective-permute-start(f32[432,128]{1,0:T(8,128)S(1)} %get-tuple-element.51), channel_id=1, source_target_pairs={{0,3},{1,2},{2,1},{3,0},{4,7},{5,6},{6,5},{7,4},{8,11},{9,10},{10,... | collective-permute-start | bytes 663560 | tf_op jit(solution)/shard_map/ppermute | solution.py:452
  28.0 10.8 %copy-start.6 = (f32[96,128]{1,0:T(8,128)S(1)}, f32[96,128]{1,0:T(8,128)}, u32[]{:S(2)}) copy-start(f32[96,128]{1,0:T(8,128)} %constant.41.clone.across_ref) | copy-start | bytes 147460
  28.0 10.8 %copy-start.7 = (f32[4,24,128]{2,1,0:T(8,128)S(1)}, f32[4,24,128]{2,1,0:T(8,128)}, u32[]{:S(2)}) copy-start(f32[4,24,128]{2,1,0:T(8,128)} %constant.42.clone.within_ref) | copy-start | bytes 147460
  28.0 6.1 %collective-permute-start.14 = (f32[288,128]{1,0:T(8,128)S(1)}, f32[288,128]{1,0:T(8,128)S(1)}, u32[]{:S(2)}, u32[]{:S(2)}) collective-permute-start(f32[288,128]{1,0:T(8,128)S(1)} %get-tuple-element.63), channel_id=1, source_target_pairs={{0,1},{1,0},{2,3},{3,2},{4,5},{5,4},{6,7},{7,6},{8,9},{9,8},{10,11... | collective-permute-start | bytes 442376 | tf_op jit(solution)/shard_map/ppermute | solution.py:452
  30.0 5.6 %collective-permute-start.15 = (f32[288,128]{1,0:T(8,128)S(1)}, f32[288,128]{1,0:T(8,128)S(1)}, u32[]{:S(2)}, u32[]{:S(2)}) collective-permute-start(f32[288,128]{1,0:T(8,128)S(1)} %get-tuple-element.64), channel_id=1, source_target_pairs={{0,1},{1,0},{2,3},{3,2},{4,5},{5,4},{6,7},{7,6},{8,9},{9,8},{10,11... | collective-permute-start | bytes 442376 | tf_op jit(solution)/shard_map/ppermute | solution.py:452
  30.0 9.7 %copy-start.4 = (bf16[4,192,192]{2,1,0:T(8,128)(2,1)S(1)}, bf16[4,192,192]{2,1,0:T(8,128)(2,1)}, u32[]{:S(2)}) copy-start(bf16[4,192,192]{2,1,0:T(8,128)(2,1)} %constant.39.clone.refs_5_.refs_13_) | copy-start | bytes 884740
  30.0 9.7 %copy-start.5 = (bf16[4,192,192]{2,1,0:T(8,128)(2,1)S(1)}, bf16[4,192,192]{2,1,0:T(8,128)(2,1)}, u32[]{:S(2)}) copy-start(bf16[4,192,192]{2,1,0:T(8,128)(2,1)} %constant.40.clone.refs_6_.refs_14_) | copy-start | bytes 884740
  31.5 4.1 %collective-permute-start.16 = (f32[288,128]{1,0:T(8,128)S(1)}, f32[288,128]{1,0:T(8,128)S(1)}, u32[]{:S(2)}, u32[]{:S(2)}) collective-permute-start(f32[288,128]{1,0:T(8,128)S(1)} %get-tuple-element.65), channel_id=1, source_target_pairs={{0,1},{1,0},{2,3},{3,2},{4,5},{5,4},{6,7},{7,6},{8,9},{9,8},{10,11... | collective-permute-start | bytes 442376 | tf_op jit(solution)/shard_map/ppermute | solution.py:452
  32.1 6.7 %collective-permute-start.17 = (f32[288,128]{1,0:T(8,128)S(1)}, f32[288,128]{1,0:T(8,128)S(1)}, u32[]{:S(2)}, u32[]{:S(2)}) collective-permute-start(f32[288,128]{1,0:T(8,128)S(1)} %get-tuple-element.66), channel_id=1, source_target_pairs={{0,2},{1,3},{2,0},{3,1},{4,6},{5,7},{6,4},{7,5},{8,10},{9,11},{10,... | collective-permute-start | bytes 442376 | tf_op jit(solution)/shard_map/ppermute | solution.py:452
  33.6 8.4 %collective-permute-start.18 = (f32[288,128]{1,0:T(8,128)S(1)}, f32[288,128]{1,0:T(8,128)S(1)}, u32[]{:S(2)}, u32[]{:S(2)}) collective-permute-start(f32[288,128]{1,0:T(8,128)S(1)} %get-tuple-element.67), channel_id=1, source_target_pairs={{0,2},{1,3},{2,0},{3,1},{4,6},{5,7},{6,4},{7,5},{8,10},{9,11},{10,... | collective-permute-start | bytes 442376 | tf_op jit(solution)/shard_map/ppermute | solution.py:452
  34.1 11.0 %collective-permute-start.19 = (f32[288,128]{1,0:T(8,128)S(1)}, f32[288,128]{1,0:T(8,128)S(1)}, u32[]{:S(2)}, u32[]{:S(2)}) collective-permute-start(f32[288,128]{1,0:T(8,128)S(1)} %get-tuple-element.68), channel_id=1, source_target_pairs={{0,2},{1,3},{2,0},{3,1},{4,6},{5,7},{6,4},{7,5},{8,10},{9,11},{10,... | collective-permute-start | bytes 442376 | tf_op jit(solution)/shard_map/ppermute | solution.py:452
  35.6 11.7 %collective-permute-start.20 = (f32[288,128]{1,0:T(8,128)S(1)}, f32[288,128]{1,0:T(8,128)S(1)}, u32[]{:S(2)}, u32[]{:S(2)}) collective-permute-start(f32[288,128]{1,0:T(8,128)S(1)} %get-tuple-element.69), channel_id=1, source_target_pairs={{0,3},{1,2},{2,1},{3,0},{4,7},{5,6},{6,5},{7,4},{8,11},{9,10},{10,... | collective-permute-start | bytes 442376 | tf_op jit(solution)/shard_map/ppermute | solution.py:452
  35.6 14.8 %collective-permute-start.21 = (f32[288,128]{1,0:T(8,128)S(1)}, f32[288,128]{1,0:T(8,128)S(1)}, u32[]{:S(2)}, u32[]{:S(2)}) collective-permute-start(f32[288,128]{1,0:T(8,128)S(1)} %get-tuple-element.70), channel_id=1, source_target_pairs={{0,3},{1,2},{2,1},{3,0},{4,7},{5,6},{6,5},{7,4},{8,11},{9,10},{10,... | collective-permute-start | bytes 442376 | tf_op jit(solution)/shard_map/ppermute | solution.py:452
  38.8 14.0 %collective-permute-start.22 = (f32[288,128]{1,0:T(8,128)S(1)}, f32[288,128]{1,0:T(8,128)S(1)}, u32[]{:S(2)}, u32[]{:S(2)}) collective-permute-start(f32[288,128]{1,0:T(8,128)S(1)} %get-tuple-element.71), channel_id=1, source_target_pairs={{0,3},{1,2},{2,1},{3,0},{4,7},{5,6},{6,5},{7,4},{8,11},{9,10},{10,... | collective-permute-start | bytes 442376 | tf_op jit(solution)/shard_map/ppermute | solution.py:452
  52.8 12.2 %copy-start.2 = (bf16[4,192,256]{2,1,0:T(8,128)(2,1)S(1)}, bf16[4,192,256]{2,1,0:T(8,128)(2,1)}, u32[]{:S(2)}) copy-start(bf16[4,192,256]{2,1,0:T(8,128)(2,1)} %constant.38.clone.refs_14_.refs_17_) | copy-start | bytes 1179652
  54.7 10.4 %collective-permute-start.23 = (f32[864,128]{1,0:T(8,128)S(1)}, f32[864,128]{1,0:T(8,128)S(1)}, u32[]{:S(2)}, u32[]{:S(2)}) collective-permute-start(f32[864,128]{1,0:T(8,128)S(1)} %get-tuple-element.73), channel_id=1, source_target_pairs={{0,1},{1,0},{2,3},{3,2},{4,5},{5,4},{6,7},{7,6},{8,9},{9,8},{10,11... | collective-permute-start | bytes 1327112 | tf_op jit(solution)/shard_map/ppermute | solution.py:452
  55.5 6.7 %collective-permute-start.24 = (f32[288,128]{1,0:T(8,128)S(1)}, f32[288,128]{1,0:T(8,128)S(1)}, u32[]{:S(2)}, u32[]{:S(2)}) collective-permute-start(f32[288,128]{1,0:T(8,128)S(1)} %get-tuple-element.74), channel_id=1, source_target_pairs={{0,2},{1,3},{2,0},{3,1},{4,6},{5,7},{6,4},{7,5},{8,10},{9,11},{10,... | collective-permute-start | bytes 442376 | tf_op jit(solution)/shard_map/ppermute | solution.py:452
  57.0 7.4 %collective-permute-start.25 = (f32[288,128]{1,0:T(8,128)S(1)}, f32[288,128]{1,0:T(8,128)S(1)}, u32[]{:S(2)}, u32[]{:S(2)}) collective-permute-start(f32[288,128]{1,0:T(8,128)S(1)} %get-tuple-element.75), channel_id=1, source_target_pairs={{0,3},{1,2},{2,1},{3,0},{4,7},{5,6},{6,5},{7,4},{8,11},{9,10},{10,... | collective-permute-start | bytes 442376 | tf_op jit(solution)/shard_map/ppermute | solution.py:452
  57.0 13.1 %collective-permute-start.26 = (f32[288,128]{1,0:T(8,128)S(1)}, f32[288,128]{1,0:T(8,128)S(1)}, u32[]{:S(2)}, u32[]{:S(2)}) collective-permute-start(f32[288,128]{1,0:T(8,128)S(1)} %get-tuple-element.77), channel_id=1, source_target_pairs={{0,2},{1,3},{2,0},{3,1},{4,6},{5,7},{6,4},{7,5},{8,10},{9,11},{10,... | collective-permute-start | bytes 442376 | tf_op jit(solution)/shard_map/ppermute | solution.py:452
  58.4 11.7 %collective-permute-start.10 = (f32[144,128]{1,0:T(8,128)S(1)}, f32[144,128]{1,0:T(8,128)S(1)}, u32[]{:S(2)}, u32[]{:S(2)}) collective-permute-start(f32[144,128]{1,0:T(8,128)S(1)} %get-tuple-element.59), channel_id=1, source_target_pairs={{0,2},{1,3},{2,0},{3,1},{4,6},{5,7},{6,4},{7,5},{8,10},{9,11},{10,... | collective-permute-start | bytes 221192 | tf_op jit(solution)/shard_map/ppermute | solution.py:452
  62.2 10.1 %collective-permute-start.27 = (f32[288,128]{1,0:T(8,128)S(1)}, f32[288,128]{1,0:T(8,128)S(1)}, u32[]{:S(2)}, u32[]{:S(2)}) collective-permute-start(f32[288,128]{1,0:T(8,128)S(1)} %get-tuple-element.78), channel_id=1, source_target_pairs={{0,3},{1,2},{2,1},{3,0},{4,7},{5,6},{6,5},{7,4},{8,11},{9,10},{10,... | collective-permute-start | bytes 442376 | tf_op jit(solution)/shard_map/ppermute | solution.py:452
  64.4 12.0 %collective-permute-start.28 = (f32[288,128]{1,0:T(8,128)S(1)}, f32[288,128]{1,0:T(8,128)S(1)}, u32[]{:S(2)}, u32[]{:S(2)}) collective-permute-start(f32[288,128]{1,0:T(8,128)S(1)} %get-tuple-element.80), channel_id=1, source_target_pairs={{0,2},{1,3},{2,0},{3,1},{4,6},{5,7},{6,4},{7,5},{8,10},{9,11},{10,... | collective-permute-start | bytes 442376 | tf_op jit(solution)/shard_map/ppermute | solution.py:452
  66.6 23.3 %collective-permute-start.30 = (f32[576,128]{1,0:T(8,128)S(1)}, f32[576,128]{1,0:T(8,128)S(1)}, u32[]{:S(2)}, u32[]{:S(2)}) collective-permute-start(f32[576,128]{1,0:T(8,128)S(1)} %get-tuple-element.83), channel_id=1, source_target_pairs={{0,4},{4,0},{8,12},{12,8},{16,20},{20,16},{24,28},{28,24},{1,5},{5... | collective-permute-start | bytes 884744 | tf_op jit(solution)/shard_map/ppermute | solution.py:579
  70.1 8.5 %collective-permute-start.29 = (f32[288,128]{1,0:T(8,128)S(1)}, f32[288,128]{1,0:T(8,128)S(1)}, u32[]{:S(2)}, u32[]{:S(2)}) collective-permute-start(f32[288,128]{1,0:T(8,128)S(1)} %get-tuple-element.81), channel_id=1, source_target_pairs={{0,3},{1,2},{2,1},{3,0},{4,7},{5,6},{6,5},{7,4},{8,11},{9,10},{10,... | collective-permute-start | bytes 442376 | tf_op jit(solution)/shard_map/ppermute | solution.py:452
  70.1 19.1 %collective-permute-start.9 = (f32[432,128]{1,0:T(8,128)S(1)}, f32[432,128]{1,0:T(8,128)S(1)}, u32[]{:S(2)}, u32[]{:S(2)}) collective-permute-start(f32[432,128]{1,0:T(8,128)S(1)} %get-tuple-element.58), channel_id=1, source_target_pairs={{0,1},{1,0},{2,3},{3,2},{4,5},{5,4},{6,7},{7,6},{8,9},{9,8},{10,11... | collective-permute-start | bytes 663560 | tf_op jit(solution)/shard_map/ppermute | solution.py:452
  72.3 15.2 %collective-permute-start.11 = (f32[288,128]{1,0:T(8,128)S(1)}, f32[288,128]{1,0:T(8,128)S(1)}, u32[]{:S(2)}, u32[]{:S(2)}) collective-permute-start(f32[288,128]{1,0:T(8,128)S(1)} %get-tuple-element.60), channel_id=1, source_target_pairs={{0,2},{1,3},{2,0},{3,1},{4,6},{5,7},{6,4},{7,5},{8,10},{9,11},{10,... | collective-permute-start | bytes 442376 | tf_op jit(solution)/shard_map/ppermute | solution.py:452
  76.4 12.3 %collective-permute-start.13 = (f32[288,128]{1,0:T(8,128)S(1)}, f32[288,128]{1,0:T(8,128)S(1)}, u32[]{:S(2)}, u32[]{:S(2)}) collective-permute-start(f32[288,128]{1,0:T(8,128)S(1)} %get-tuple-element.62), channel_id=1, source_target_pairs={{0,3},{1,2},{2,1},{3,0},{4,7},{5,6},{6,5},{7,4},{8,11},{9,10},{10,... | collective-permute-start | bytes 442376 | tf_op jit(solution)/shard_map/ppermute | solution.py:452
  78.6 7.1 %collective-permute-start.12 = (f32[144,128]{1,0:T(8,128)S(1)}, f32[144,128]{1,0:T(8,128)S(1)}, u32[]{:S(2)}, u32[]{:S(2)}) collective-permute-start(f32[144,128]{1,0:T(8,128)S(1)} %get-tuple-element.61), channel_id=1, source_target_pairs={{0,3},{1,2},{2,1},{3,0},{4,7},{5,6},{6,5},{7,4},{8,11},{9,10},{10,... | collective-permute-start | bytes 221192 | tf_op jit(solution)/shard_map/ppermute | solution.py:452
  85.7 9.9 %collective-permute-start.31 = (f32[576,128]{1,0:T(8,128)S(1)}, f32[576,128]{1,0:T(8,128)S(1)}, u32[]{:S(2)}, u32[]{:S(2)}) collective-permute-start(f32[576,128]{1,0:T(8,128)S(1)} %get-tuple-element.84), channel_id=1, source_target_pairs={{0,24},{4,28},{8,0},{12,4},{16,8},{20,12},{24,16},{28,20},{1,25},{... | collective-permute-start | bytes 884744 | tf_op jit(solution)/shard_map/ppermute | solution.py:578
  87.4 9.9 %collective-permute-start.32 = (f32[576,128]{1,0:T(8,128)S(1)}, f32[576,128]{1,0:T(8,128)S(1)}, u32[]{:S(2)}, u32[]{:S(2)}) collective-permute-start(f32[576,128]{1,0:T(8,128)S(1)} %get-tuple-element.85), channel_id=1, source_target_pairs={{0,4},{4,0},{8,12},{12,8},{16,20},{20,16},{24,28},{28,24},{1,5},{5... | collective-permute-start | bytes 884744 | tf_op jit(solution)/shard_map/ppermute | solution.py:579
  88.7 13.1 %collective-permute-start.33 = (f32[576,128]{1,0:T(8,128)S(1)}, f32[576,128]{1,0:T(8,128)S(1)}, u32[]{:S(2)}, u32[]{:S(2)}) collective-permute-start(f32[576,128]{1,0:T(8,128)S(1)} %get-tuple-element.86), channel_id=1, source_target_pairs={{0,24},{4,28},{8,0},{12,4},{16,8},{20,12},{24,16},{28,20},{1,25},{... | collective-permute-start | bytes 884744 | tf_op jit(solution)/shard_map/ppermute | solution.py:578
  89.2 15.5 %collective-permute-start.34 = (f32[576,128]{1,0:T(8,128)S(1)}, f32[576,128]{1,0:T(8,128)S(1)}, u32[]{:S(2)}, u32[]{:S(2)}) collective-permute-start(f32[576,128]{1,0:T(8,128)S(1)} %get-tuple-element.89), channel_id=1, source_target_pairs={{0,4},{4,0},{8,12},{12,8},{16,20},{20,16},{24,28},{28,24},{1,5},{5... | collective-permute-start | bytes 884744 | tf_op jit(solution)/shard_map/ppermute | solution.py:579
  89.9 18.0 %collective-permute-start.35 = (f32[576,128]{1,0:T(8,128)S(1)}, f32[576,128]{1,0:T(8,128)S(1)}, u32[]{:S(2)}, u32[]{:S(2)}) collective-permute-start(f32[576,128]{1,0:T(8,128)S(1)} %get-tuple-element.90), channel_id=1, source_target_pairs={{0,24},{4,28},{8,0},{12,4},{16,8},{20,12},{24,16},{28,20},{1,25},{... | collective-permute-start | bytes 884744 | tf_op jit(solution)/shard_map/ppermute | solution.py:578

commit v4 on v3

--- a/solution.py
+++ b/solution.py
@@ -1,4 +1,5 @@
 import functools
+from typing import NamedTuple
 
 import jax
 import jax.numpy as jnp
@@ -197,12 +198,11 @@
     for first in range(0, len(planes), 2):
         two = []
         for plane in planes[first : first + 2]:
-            ins, stride, offset = place(plane)
             rows, tails = [], []
-            for ref, base in ins:
+            for ref, stride, offset in place(plane):
                 parts = []
                 for t in range(3):
-                    at = base + t * e * stride + offset
+                    at = t * e * stride + offset
                     part = ref[pl.ds(at, e, stride=stride), :]
                     parts.append(jnp.concatenate([part, jnp.zeros((8 - e, LANES), F32)], axis=0))
                 rows += parts
@@ -214,11 +214,13 @@
 
 
 CHUNK = 8
-
-
-def pack_kernel(plan, scalars, own_ref, out):
+PIECES = 3
+LATE = 1
+
+
+def pack_kernel(plan, scalars, ins, outs):
     for i in range(CHUNK):
-        out[i * plan.packed : (i + 1) * plan.packed, :] = pack(widen(own_ref[i]), plan)
+        outs[0][i * plan.packed : (i + 1) * plan.packed, :] = pack(widen(ins[0][i]), plan)
 
 
 def unpack_chunk(value, plan):
@@ -245,7 +247,8 @@
     return jnp.concatenate(parts, axis=0)
 
 
-def forward_own_kernel(plan, scalars, own_ref, tz_ref, ty_ref, after_ref, *outs):
+def forward_own_kernel(plan, scalars, ins, outs):
+    own_ref, tz_ref, ty_ref = ins
     blocks, later = outs[: plan.parts], outs[plan.parts :]
     for c in range(plan.planes // CHUNK):
         here = slice(c * CHUNK, (c + 1) * CHUNK)
@@ -257,16 +260,20 @@
         )
 
 
-def forward_pair_kernel(plan, scalars, p_ref, q_ref, r_ref, tz_ref, ty_ref, after_ref, *outs):
+def forward_pair_kernel(plan, scalars, ins, outs):
+    p_ref, q_ref, r_ref, tz_ref, ty_ref = ins
     even = scalars[1] == 1
     p, r = p_ref[...], r_ref[...]
     tz, ty = tz_ref[...], ty_ref[0]
-    store_spectrum(plan, unpack_chunk(p * r, plan), tz, ty, outs, 0, CHUNK, 0)
+    apart = len(outs) > plan.parts
+    blocks, base = (outs[plan.parts :], 0) if apart else (outs, plan.rows * CHUNK)
     mixed = q_ref[...] * jnp.where(even, r, p)
-    store_spectrum(plan, unpack_chunk(mixed, plan), tz, ty, outs, plan.rows * CHUNK, CHUNK, 0)
-
-
-def screen_kernel(plan, scalars, across_ref, within_ref, after_ref, out_ref):
+    store_spectrum(plan, unpack_chunk(mixed, plan), tz, ty, blocks, base, CHUNK, 0)
+    store_spectrum(plan, unpack_chunk(p * r, plan), tz, ty, outs[: plan.parts], 0, CHUNK, 0)
+
+
+def screen_kernel(plan, scalars, ins, outs):
+    across_ref, within_ref = ins
     cells = plan.length * plan.height * plan.breadth
     limit = 4.0 * np.pi / plan.length
     rate = 1.0 / (4.0 * limit * limit)
@@ -274,87 +281,68 @@
         wave_sq = across_ref[...] + within_ref[0, row : row + 1, :]
         guarded = jnp.where(wave_sq > 0, wave_sq, 1.0)
         screened = (-0.2 * 4.0 * np.pi / cells) / guarded * (1.0 - jnp.exp(guarded * -rate))
-        out_ref[row * plan.length : (row + 1) * plan.length, :] = jnp.where(
+        outs[0][row * plan.length : (row + 1) * plan.length, :] = jnp.where(
             wave_sq > 0, screened, 0.0
         )
 
 
-JOINED = 2
-
-
-def places(refs, plan, sizes, count):
-    joined, cut = refs[:JOINED], refs[JOINED:]
-    result, row = [], 0
-    for i, size in enumerate(sizes):
-        result.append([(ref, row) for ref in joined] + [(ref, 0) for ref in cut[i :: len(sizes)]])
-        row += count * plan.rows * size
-    return result
-
-
-def shapes_of(plan, sizes, count):
-    rows = [count * plan.rows * size for size in sizes]
-    return [(sum(rows), LANES)] * JOINED + [(n, LANES) for n in rows] * (plan.parts - JOINED)
-
-
-def middle_kernel(plan, sizes_in, sizes_out, count, scalars, *refs):
-    n = plan.parts
-    ins = [refs[k * len(sizes_in) : (k + 1) * len(sizes_in)] for k in range(n)]
-    refs = refs[n * len(sizes_in) :]
-    screen_ref, tf_ref, tb_ref, after_ref, *refs = refs
-    outs = places(refs, plan, sizes_out, count)
-    length = plan.length
+def middle_kernel(plan, chunks, sizes, scalars, ins, outs):
+    n, length = plan.parts, plan.length
+    blocks = [ins[k * len(chunks) : (k + 1) * len(chunks)] for k in range(n)]
+    screen_ref, tf_ref, tb_ref = ins[n * len(chunks) :]
+    cut = [outs[2 + i * len(sizes) : 2 + (i + 1) * len(sizes)] for i in range(n - 2)]
     for pair in range(plan.rows // 2):
-        for solve in range(count):
-            columns = []
-            for i in range(2):
-                row = pair * 2 + i
-                parts = []
-                for k in range(n):
-                    for ref, size in zip(ins[k], sizes_in):
-                        first = (solve * plan.rows + row) * size
-                        parts.append(ref[first : first + size, :])
-                columns.append(jnp.concatenate(parts, axis=0))
-            spectrum = along_rows(tf_ref[0], jnp.concatenate(columns, axis=1))
-            screen = jnp.concatenate(
-                [
-                    screen_ref[(pair * 2 + i) * length : (pair * 2 + i + 1) * length, :]
-                    for i in range(2)
-                ],
-                axis=1,
-            )
-            back = along_rows(tb_ref[0], spectrum * screen)
-            for i in range(2):
-                row = pair * 2 + i
-                at = 0
-                for out, size in zip(outs, sizes_out):
-                    for k, (ref, base) in enumerate(out):
-                        first = base + (solve * plan.rows + row) * size
-                        ref[first : first + size, :] = back[
-                            k * plan.planes + at : k * plan.planes + at + size,
-                            i * LANES : (i + 1) * LANES,
-                        ]
+        columns = []
+        for row in (pair * 2, pair * 2 + 1):
+            parts = []
+            for part in blocks:
+                for ref, (size, base) in zip(part, chunks):
+                    parts.append(ref[base + row * size : base + (row + 1) * size, :])
+            columns.append(jnp.concatenate(parts, axis=0))
+        spectrum = along_rows(tf_ref[0], jnp.concatenate(columns, axis=1))
+        screen = jnp.concatenate(
+            [
+                screen_ref[row * length : (row + 1) * length, :]
+                for row in (pair * 2, pair * 2 + 1)
+            ],
+            axis=1,
+        )
+        back = along_rows(tb_ref[0], spectrum * screen)
+        for i in range(2):
+            row, lane = pair * 2 + i, slice(i * LANES, (i + 1) * LANES)
+            for k in range(n):
+                at = k * plan.planes
+                refs = cut[k - 2] if k >= 2 else outs[k : k + 1]
+                for ref, size in zip(refs, sizes if k >= 2 else (plan.planes,)):
+                    ref[row * size : (row + 1) * size, :] = back[at : at + size, lane]
                     at += size
 
 
-def backward_pair_kernel(plan, pieces, piece, scalars, *refs):
-    n = plan.parts
-    ins, refs = refs[:n], refs[n:]
+def backward_pair_kernel(plan, pieces, piece, scalars, ins, outs):
+    far = plan.parts - 2
+    whole, ins = ins[:4], ins[4:]
+    apart = piece == 0
+    blocks, ins = ins[: far * (1 + apart)], ins[far * (1 + apart) :]
+    chunks = plan.planes // CHUNK
     first, size = sum(pieces[:piece]), pieces[piece]
-    skipped = 2 * plan.rows * first
-    chunks = plan.planes // CHUNK
-    fields = [planes_of(refs[i * chunks : (i + 1) * chunks], first, size, plan) for i in range(3)]
-    tz_ref, ty_ref, _, total_ref, y_ref, z_ref = refs[3 * chunks :]
+    p, q, r = (
+        planes_of(ins[i * chunks : (i + 1) * chunks], first, size, plan) for i in range(3)
+    )
+    tz, ty = ins[3 * chunks][...], ins[3 * chunks + 1][0]
     even = scalars[1] == 1
-    tz, ty = tz_ref[...], ty_ref[0]
 
     def solved(which):
-        base = which * plan.rows * size
-        found = [(ref, base + (skipped if k < JOINED else 0)) for k, ref in enumerate(ins)]
-        wide = load_potential(plan, lambda i: (found, size, i), range(size), tz, ty)
-        return pack_chunk(wide, plan)
-
-    visit, mixed = solved(0), solved(1)
-    p, q, r = fields
+        base = 0 if apart else which * plan.rows * size
+        refs = blocks[which * far : (which + 1) * far] if apart else blocks
+
+        def place(i):
+            near = [(ref, plan.planes, first + i) for ref in whole[2 * which : 2 * which + 2]]
+            return near + [(ref, size, base + i) for ref in refs]
+
+        return pack_chunk(load_potential(plan, place, range(size), tz, ty), plan)
+
+    mixed, visit = solved(0), solved(1)
+    total_ref, y_ref, z_ref = outs
     other = mixed * q
     zero = jnp.zeros_like(other)
     y_ref[...] = mixed * jnp.where(even, r, p)
@@ -368,25 +356,17 @@
         out_ref[first + i] = wide[:, : plan.breadth]
 
 
-LATE = 1
-
-
-def backward_own_kernel(plan, sizes, pieces, scalars, *refs):
-    used = JOINED + (plan.parts - JOINED) * len(sizes)
-    ins, refs = places(refs[:used], plan, sizes, 1), refs[used:]
-    count, chunks = len(pieces), plan.planes // CHUNK
+def backward_own_kernel(plan, pieces, scalars, ins, outs):
+    n, count, chunks = plan.parts, len(pieces), plan.planes // CHUNK
     ready = count - LATE
-    totals, refs = refs[:count], refs[count:]
-    owns, refs = refs[:chunks], refs[chunks:]
-    returned, refs = refs[: 2 * ready], refs[2 * ready :]
-    tz_ref, ty_ref, after_ref, out_ref, *rest = refs
+    blocks, ins = ins[:n], ins[n:]
+    totals, ins = ins[:count], ins[count:]
+    owns, ins = ins[:chunks], ins[chunks:]
+    returned, (tz_ref, ty_ref) = ins[: 2 * ready], ins[2 * ready :]
+    out_ref, *rest = outs
 
     def place(plane):
-        which = 0
-        while plane >= sizes[which]:
-            plane -= sizes[which]
-            which += 1
-        return ins[which], sizes[which], plane
+        return [(ref, plan.planes, plane) for ref in blocks]
 
     first = 0
     for c, size in enumerate(pieces):
@@ -400,70 +380,75 @@
         first += size
 
 
-def final_kernel(plan, scalars, partial_ref, *refs):
-    rest, ys, zs, out_ref = refs[:LATE], refs[LATE : 2 * LATE], refs[2 * LATE : 3 * LATE], refs[-1]
+def final_kernel(plan, scalars, ins, outs):
+    rest, ys, zs = ins[:LATE], ins[LATE : 2 * LATE], ins[2 * LATE :]
     first = 0
     for part, y, z in zip(rest, ys, zs):
-        store_result(out_ref, first, part[...] + y[...] + z[...], plan)
+        store_result(outs[0], first, part[...] + y[...] + z[...], plan)
         first += part.shape[0] // plan.packed
 
 
-def call(kernel, scalars, operands, outs, selected=(), chunk=None, after=None, update=None):
+class Block(NamedTuple):
+    shape: tuple
+    rows: int
+    index: int
+    array: jax.Array | None = None
+
+
+def call(kernel, scalars, operands, outs, selected=(), chunk=None, after=None):
     specs = []
     for operand in operands:
         if any(operand is s for s in selected):
             specs.append(pl.BlockSpec((1,) + operand.shape[1:], lambda i, s: (s[0], 0, 0)))
         elif chunk is not None and operand is chunk[0]:
             specs.append(
-                pl.BlockSpec(
-                    (CHUNK,) + operand.shape[1:], lambda i, s, c=chunk[1]: (c, 0, 0)
-                )
+                pl.BlockSpec((CHUNK,) + operand.shape[1:], lambda i, s, c=chunk[1]: (c, 0, 0))
             )
         else:
             zeros = (0,) * operand.ndim
             specs.append(pl.BlockSpec(operand.shape, lambda i, s, zeros=zeros: zeros))
-    if after is not None:
-        operands = (*operands, after)
-        specs.append(pl.BlockSpec(memory_space=pl.ANY))
-    out_specs = [pl.BlockSpec(o, lambda i, s, zeros=(0,) * len(o): zeros) for o in outs]
-    aliases = {}
-    if update is not None:
-        specs[0] = pl.BlockSpec(memory_space=pl.ANY)
-        out_specs = [
-            pl.BlockSpec((update,) + o[1:], lambda i, s, c=o[0] // update - 1: (c, 0, 0))
-            for o in outs
-        ]
-        aliases = {1: 0}
+    count = len(operands)
+    extras = [] if after is None else [after]
+    out_specs, shapes, aliases = [], [], {}
+    for i, out in enumerate(outs):
+        if not isinstance(out, Block):
+            out = Block(out, out[0], 0)
+        if out.array is not None:
+            extras.append(out.array)
+            aliases[count + len(extras)] = i
+        shapes.append(jax.ShapeDtypeStruct(out.shape, F32))
+        at = (out.index,) + (0,) * (len(out.shape) - 1)
+        out_specs.append(pl.BlockSpec((out.rows,) + out.shape[1:], lambda i, s, at=at: at))
+    seen = count + len(extras)
+
+    def body(scalars, *refs):
+        kernel(scalars, refs[:count], refs[seen:])
+
     return pl.pallas_call(
-        kernel,
+        body,
         grid_spec=pltpu.PrefetchScalarGridSpec(
             num_scalar_prefetch=1,
             grid=(1,),
-            in_specs=specs,
+            in_specs=specs + [pl.BlockSpec(memory_space=pl.ANY)] * len(extras),
             out_specs=out_specs,
         ),
         input_output_aliases=aliases,
-        out_shape=[jax.ShapeDtypeStruct(o, F32) for o in outs],
+        out_shape=shapes,
         compiler_params=pltpu.CompilerParams(vmem_limit_bytes=48 * 1024 * 1024),
-    )(scalars, *operands)
+    )(scalars, *operands, *extras)
 
 
 def send(block, k, parts):
     return lax.ppermute(block, "grid", [(i, i ^ k) for i in range(parts)])
 
 
+def send_far(blocks, parts):
+    return [send(block, k, parts) for k, block in zip(range(2, parts), blocks)]
+
+
 def exchange(blocks, parts):
-    far = [send(blocks[k], k, parts) for k in range(2, parts)]
+    far = send_far(blocks[2:], parts)
     return [blocks[0], send(blocks[1], 1, parts), *far]
-
-
-def exchange_pieces(blocks, parts, count):
-    near = send(blocks[1], 1, parts)
-    far = [send(block, JOINED + i // count, parts) for i, block in enumerate(blocks[JOINED:])]
-    return [blocks[0], near, *far]
-
-
-PIECES = 3
 
 
 def pieces_of(planes):
@@ -488,7 +473,6 @@
     chunks = plan.planes // CHUNK
     whole = own.shape
     packed = (CHUNK * plan.packed, LANES)
-    sizes = (CHUNK, plan.planes - CHUNK)
     pieces = pieces_of(plan.planes)
 
     (first,) = call(functools.partial(pack_kernel, plan), scalars, (own,), [packed], chunk=(own, 0))
@@ -512,18 +496,24 @@
     for c in range(1, chunks):
         shift(mine[c])
     after = blocks[0]
+    rows = plan.rows * CHUNK
     pair_in = []
     for c in range(chunks):
+        last = c == chunks - 1
         out = call(
             functools.partial(forward_pair_kernel, plan),
             scalars,
             (mine[c], q[c], r[c], tz, ty_forward),
-            [(2 * plan.rows * CHUNK, LANES)] * parts,
+            [(rows, LANES)] * (2 * parts) if last else [(2 * rows, LANES)] * parts,
             (ty_forward,),
             after=after,
         )
         after = out[0]
-        pair_in.append(exchange(out, parts))
+        if last:
+            visit_last = exchange(out[:parts], parts)
+            mixed_last = exchange(out[parts:], parts)
+        else:
+            pair_in.append(exchange(out, parts))
     (screen,) = call(
         functools.partial(screen_kernel, plan),
         scalars,
@@ -533,27 +523,56 @@
         after=after,
     )
 
-    def middle(ins, sizes_in, sizes_out, count, after):
+    def middle(ins, places, sizes, outs, after):
         return call(
-            functools.partial(middle_kernel, plan, sizes_in, sizes_out, count),
+            functools.partial(middle_kernel, plan, places, sizes),
             scalars,
             (*[block for part in ins for block in part], screen, tx_forward, tx_backward),
-            shapes_of(plan, sizes_out, count),
+            [(plan.block, LANES)] * 2 + outs,
             (tx_forward, tx_backward),
             after=after,
         )
 
-    own_mid = middle([[b] for b in own_in], (plan.planes,), sizes, 1, screen)
-    own_back = exchange_pieces(own_mid, parts, len(sizes))
-    pair_mid = middle(
-        [[pair_in[c][k] for c in range(chunks)] for k in range(parts)],
-        (CHUNK,) * chunks,
-        pieces,
-        2,
-        own_mid[0],
-    )
-    pair_back = exchange_pieces(pair_mid, parts, len(pieces))
-    after = pair_mid[0]
+    own_mid = middle(
+        [[b] for b in own_in],
+        ((plan.planes, 0),),
+        (plan.planes,),
+        [(plan.block, LANES)] * (parts - 2),
+        screen,
+    )
+
+    def middle_of(last, half, arrays, after):
+        base = plan.rows * CHUNK if half == 0 else 0
+        outs = []
+        for i in range(parts - 2):
+            for c, size in enumerate(pieces):
+                n = plan.rows * size
+                if c == 0:
+                    outs.append((n, LANES))
+                else:
+                    array = None if arrays is None else arrays[i * len(pieces) + c]
+                    outs.append(Block((2 * n, LANES), n, half, array))
+        return middle(
+            [[*(pair_in[c][k] for c in range(chunks - 1)), last[k]] for k in range(parts)],
+            ((CHUNK, base),) * (chunks - 1) + ((CHUNK, 0),),
+            pieces,
+            outs,
+            after,
+        )
+
+    mixed_mid = middle_of(mixed_last, 0, None, own_mid[0])
+    mixed_far = mixed_mid[2:]
+    mixed_first = send_far(mixed_far[:: len(pieces)], parts)
+    mixed_near = send(mixed_mid[1], 1, parts)
+    visit_mid = middle_of(visit_last, 1, mixed_far, mixed_mid[0])
+    visit_far = visit_mid[2:]
+    visit_first = send_far(visit_far[:: len(pieces)], parts)
+    visit_near = send(visit_mid[1], 1, parts)
+    far = [[*mixed_first, *visit_first]]
+    for c in range(1, len(pieces)):
+        far.append(send_far(visit_far[c :: len(pieces)], parts))
+    own_back = exchange(own_mid, parts)
+    after = visit_mid[0]
     totals, from_y, from_z = [], [], []
     for c, size in enumerate(pieces):
         piece = (size * plan.packed, LANES)
@@ -561,8 +580,11 @@
             functools.partial(backward_pair_kernel, plan, pieces, c),
             scalars,
             (
-                *pair_back[:JOINED],
-                *pair_back[JOINED + c :: len(pieces)],
+                mixed_mid[0],
+                mixed_near,
+                visit_mid[0],
+                visit_near,
+                *far[c],
                 *mine,
                 *q,
                 *r,
@@ -579,7 +601,7 @@
         from_y.append(lax.ppermute(y, "band", swap))
     ready = len(pieces) - LATE
     partial, *rest = call(
-        functools.partial(backward_own_kernel, plan, sizes, pieces),
+        functools.partial(backward_own_kernel, plan, pieces),
         scalars,
         (
             *own_back,
@@ -593,12 +615,12 @@
         (ty_backward,),
         after=after,
     )
+    late = sum(pieces[ready:])
     (result,) = call(
         functools.partial(final_kernel, plan),
         scalars,
-        (partial, *rest, *from_y[ready:], *from_z[ready:]),
-        [whole],
-        update=sum(pieces[ready:]),
+        (*rest, *from_y[ready:], *from_z[ready:]),
+        [Block(whole, late, whole[0] // late - 1, partial)],
     )
     return result[None]
 

time: 110 us -> 107 us (0.973)
  waiting for transfers between devices: 53.6 us -> 48.7 us
  starting transfers between devices: 34.3 us -> 35.7 us
    ppermute x3, waiting for transfers between devices: 13 us -> 7.41 us  [exchange_term(): from_z.append(lax.ppermute(z, 'band', ahead))]
    ppermute x3, waiting for transfers between devices: 5.18 us -> 0.01 us  [shift(): q.append(lax.ppermute(chunk, 'band', swap))]
    ppermute x3, waiting for transfers between devices: 3.83 us -> 8.1 us  [shift(): r.append(lax.ppermute(chunk, 'band', behind))]
    ppermute x3, waiting for transfers between devices: 1.75 us -> 4.28 us  [exchange_term(): from_y.append(lax.ppermute(y, 'band', swap))]
    ppermute x3, starting transfers between devices: 2.59 us -> 4.26 us  [exchange_term(): from_y.append(lax.ppermute(y, 'band', swap))]
    ppermute x3, starting transfers between devices: 5.09 us -> 3.77 us  [shift(): q.append(lax.ppermute(chunk, 'band', swap))]
    ppermute x24 -> x28, starting transfers between devices: 18.7 us -> 17.8 us  [send(): return lax.ppermute(block, 'grid', [(i, i ^ k) for i in range(parts)])]
    ppermute x24 -> x28, waiting for transfers between devices: 29.8 us -> 28.9 us  [send(): return lax.ppermute(block, 'grid', [(i, i ^ k) for i in range(parts)])]
  transfers between devices with their start and end apart: 36 -> 40, of which waited for: 22 -> 23; matrix products, arithmetic and copies ran while one was open for 0% -> 0% of each run, Pallas kernels for 13% -> 16%
where the time goes in v4:
time: 107 us
  waiting for transfers between devices  48.7 us (46%)
  starting transfers between devices  35.7 us (33%)
  Pallas kernels  20.8 us (19%)
  local copies, waits for them, and re-layouts  1.37 us (1%)
    ppermute x28, waiting for transfers between devices, send(): return lax.ppermute(block, 'grid', [(i, i ^ k) for i in range(parts)])  28.9 us
    pallas_call x14, Pallas kernels, call(): pl.pallas_call(body, grid_spec=pltpu.PrefetchScalarGridSpec(num_scalar_pr...  20.8 us
    ppermute x28, starting transfers between devices, send(): return lax.ppermute(block, 'grid', [(i, i ^ k) for i in range(parts)])  17.8 us
    ppermute x3, waiting for transfers between devices, shift(): r.append(lax.ppermute(chunk, 'band', behind))  8.1 us
    ppermute x3, waiting for transfers between devices, exchange_term(): from_z.append(lax.ppermute(z, 'band', ahead))  7.41 us
    ppermute x3, starting transfers between devices, shift(): r.append(lax.ppermute(chunk, 'band', behind))  6.31 us
    ppermute x3, waiting for transfers between devices, exchange_term(): from_y.append(lax.ppermute(y, 'band', swap))  4.28 us
    ppermute x3, starting transfers between devices, exchange_term(): from_y.append(lax.ppermute(y, 'band', swap))  4.26 us
  transfers between devices with their start and end apart: 40, of which 23 were waited for; matrix products, arithmetic and copies ran while one was open for 0% of the time, Pallas kernels for 16%

profile of v4, /device:TPU:0, one launch (start us, length us, event | category | flops | bytes accessed | tf_op | source)
XLA Modules:
  0.0 106.8 jit_solution(9247865543293289977)
XLA Ops:
  0.1 1.3 %copy-done.3 = f32[1,24,96,96]{3,2,1,0:T(8,128)S(1)} copy-done((f32[1,24,96,96]{3,2,1,0:T(8,128)S(1)}, f32[1,24,96,96]{3,2,1,0:T(8,128)}, u32[]{:S(2)}) %copy-start.3) | copy-done | bytes 884760
  1.4 0.7 shard_map.82.refs_3_.refs_0_.refs_8_.refs_6_.refs_7_
  2.1 3.1 %collective-permute-start.8 = (f32[576,128]{1,0:T(8,128)S(1)}, f32[576,128]{1,0:T(8,128)S(1)}, u32[]{:S(2)}, u32[]{:S(2)}) collective-permute-start(f32[576,128]{1,0:T(8,128)S(1)} %shard_map.82.refs_3_.refs_0_.refs_8_.refs_6_.refs_7_), channel_id=1, source_target_pairs={{0,8},{4,12},{8,16},{12,20},{16,24},{20,28},{24,0},{28,4},{1,9},{5... | collective-permute-start | bytes 884744 | tf_op jit(solution)/shard_map/ppermute | solution.py:483
  5.2 1.5 %collective-permute-start.7 = (f32[576,128]{1,0:T(8,128)S(1)}, f32[576,128]{1,0:T(8,128)S(1)}, u32[]{:S(2)}, u32[]{:S(2)}) collective-permute-start(f32[576,128]{1,0:T(8,128)S(1)} %shard_map.82.refs_3_.refs_0_.refs_8_.refs_6_.refs_7_), channel_id=1, source_target_pairs={{0,4},{4,0},{8,12},{12,8},{16,20},{20,16},{24,28},{28,24},{1,5},{5... | collective-permute-start | bytes 884744 | tf_op jit(solution)/shard_map/ppermute | solution.py:482
  6.7 1.8 %shard_map.83 = (f32[432,128]{1,0:T(8,128)S(1)}, f32[432,128]{1,0:T(8,128)S(1)}, f32[432,128]{1,0:T(8,128)S(1)}, f32[432,128]{1,0:T(8,128)S(1)}, f32[576,128]{1,0:T(8,128)S(1)}, /*index=5*/f32[576,128]{1,0:T(8,128)S(1)}) custom-call(s32[2]{0:T(128)S(1)} %pad_add_fusion.scalars, f32[24,96,96]{2,1,0:T(8,128)S(1)} %bitcast.5, bf16[256,256]{1,0:T(8,128)(2,1)S(1)} %copy-done, ...), custom_call_target="tpu_custom_call" | custom-call | tf_op jit(solution)/shard_map/pallas_call | solution.py:427
  8.6 1.6 %collective-permute-start.6 = (f32[576,128]{1,0:T(8,128)S(1)}, f32[576,128]{1,0:T(8,128)S(1)}, u32[]{:S(2)}, u32[]{:S(2)}) collective-permute-start(f32[576,128]{1,0:T(8,128)S(1)} %get-tuple-element.63.refs_0_.refs_9_.refs_7_.refs_8_), channel_id=1, source_target_pairs={{0,8},{4,12},{8,16},{12,20},{16,24},{20,28},{24,0},{28,4},{1,9},{5... | collective-permute-start | bytes 884744 | tf_op jit(solution)/shard_map/ppermute | solution.py:483
  10.2 0.5 collective-permute-start.5
  10.7 1.6 %collective-permute-start.4 = (f32[576,128]{1,0:T(8,128)S(1)}, f32[576,128]{1,0:T(8,128)S(1)}, u32[]{:S(2)}, u32[]{:S(2)}) collective-permute-start(f32[576,128]{1,0:T(8,128)S(1)} %get-tuple-element.62.refs_0_.refs_10_.refs_8_.refs_9_), channel_id=1, source_target_pairs={{0,8},{4,12},{8,16},{12,20},{16,24},{20,28},{24,0},{28,4},{1,9},{5... | collective-permute-start | bytes 884744 | tf_op jit(solution)/shard_map/ppermute | solution.py:483
  12.3 2.8 %collective-permute-done.8.refs_2_.refs_14_.refs_12_ = f32[576,128]{1,0:T(8,128)S(1)} collective-permute-done((f32[576,128]{1,0:T(8,128)S(1)}, f32[576,128]{1,0:T(8,128)S(1)}, u32[]{:S(2)}, u32[]{:S(2)}) %collective-permute-start.8) | collective-permute-done | bytes 294944 | tf_op jit(solution)/shard_map/ppermute | solution.py:483
  15.1 1.7 %collective-permute-start.3 = (f32[576,128]{1,0:T(8,128)S(1)}, f32[576,128]{1,0:T(8,128)S(1)}, u32[]{:S(2)}, u32[]{:S(2)}) collective-permute-start(f32[576,128]{1,0:T(8,128)S(1)} %get-tuple-element.62.refs_0_.refs_10_.refs_8_.refs_9_), channel_id=1, source_target_pairs={{0,4},{4,0},{8,12},{12,8},{16,20},{20,16},{24,28},{28,24},{1,5},{5... | collective-permute-start | bytes 884744 | tf_op jit(solution)/shard_map/ppermute | solution.py:482
  16.8 4.6 %collective-permute-done.6.refs_2_.refs_15_.refs_13_ = f32[576,128]{1,0:T(8,128)S(1)} collective-permute-done((f32[576,128]{1,0:T(8,128)S(1)}, f32[576,128]{1,0:T(8,128)S(1)}, u32[]{:S(2)}, u32[]{:S(2)}) %collective-permute-start.6) | collective-permute-done | bytes 294944 | tf_op jit(solution)/shard_map/ppermute | solution.py:483
  21.4 1.7 %collective-permute-start.1 = (f32[432,128]{1,0:T(8,128)S(1)}, f32[432,128]{1,0:T(8,128)S(1)}, u32[]{:S(2)}, u32[]{:S(2)}) collective-permute-start(f32[432,128]{1,0:T(8,128)S(1)} %get-tuple-element.60), channel_id=1, source_target_pairs={{0,2},{1,3},{2,0},{3,1},{4,6},{5,7},{6,4},{7,5},{8,10},{9,11},{10,... | collective-permute-start | bytes 663560 | tf_op jit(solution)/shard_map/ppermute | solution.py:442
  23.1 1.5 %shard_map.84 = (f32[288,128]{1,0:T(8,128)S(1)}, f32[288,128]{1,0:T(8,128)S(1)}, f32[288,128]{1,0:T(8,128)S(1)}, f32[288,128]{1,0:T(8,128)S(1)}) custom-call(s32[2]{0:T(128)S(1)} %pad_add_fusion.scalars, f32[576,128]{1,0:T(8,128)S(1)} %shard_map.82.refs_3_.refs_0_.refs_8_.refs_6_.refs_7_, f32[576,128]{1,0:T(8,128)S(1)} %collective-permute-done.7.refs_1_.refs_11_.refs_9_, ...), custom_call_target="tpu_custom_call" | custom-call | tf_op jit(solution)/shard_map/pallas_call | solution.py:427
  24.6 1.5 %shard_map.85 = (f32[288,128]{1,0:T(8,128)S(1)}, f32[288,128]{1,0:T(8,128)S(1)}, f32[288,128]{1,0:T(8,128)S(1)}, f32[288,128]{1,0:T(8,128)S(1)}) custom-call(s32[2]{0:T(128)S(1)} %pad_add_fusion.scalars, f32[576,128]{1,0:T(8,128)S(1)} %get-tuple-element.63.refs_0_.refs_9_.refs_7_.refs_8_, f32[576,128]{1,0:T(8,128)S(1)} %collective-permute-done.5.refs_1_.refs_12_.refs_10_, ...), custom_call_target="tpu_custom_call" | custom-call | tf_op jit(solution)/shard_map/pallas_call | solution.py:427
  26.2 0.7 collective-permute-done.4.refs_2_.refs_16_.refs_14_
  26.9 1.5 %shard_map.86 = (f32[144,128]{1,0:T(8,128)S(1)}, f32[144,128]{1,0:T(8,128)S(1)}, f32[144,128]{1,0:T(8,128)S(1)}, f32[144,128]{1,0:T(8,128)S(1)}, f32[144,128]{1,...) custom-call(s32[2]{0:T(128)S(1)} %pad_add_fusion.scalars, ...), custom_call_target="tpu_custom_call" | custom-call | tf_op jit(solution)/shard_map/pallas_call | solution.py:427
  28.4 0.6 collective-permute-start.14
  29.0 1.5 %collective-permute-start.17 = (f32[144,128]{1,0:T(8,128)S(1)}, f32[144,128]{1,0:T(8,128)S(1)}, u32[]{:S(2)}, u32[]{:S(2)}) collective-permute-start(f32[144,128]{1,0:T(8,128)S(1)} %get-tuple-element.77), channel_id=1, source_target_pairs={{0,2},{1,3},{2,0},{3,1},{4,6},{5,7},{6,4},{7,5},{8,10},{9,11},{10,... | collective-permute-start | bytes 221192 | tf_op jit(solution)/shard_map/ppermute | solution.py:442
  30.5 1.0 collective-permute-done.2.refs_3_
  31.5 0.6 collective-permute-start.15
  32.1 1.6 %collective-permute-start.18 = (f32[288,128]{1,0:T(8,128)S(1)}, f32[288,128]{1,0:T(8,128)S(1)}, u32[]{:S(2)}, u32[]{:S(2)}) collective-permute-start(f32[288,128]{1,0:T(8,128)S(1)} %get-tuple-element.78), channel_id=1, source_target_pairs={{0,3},{1,2},{2,1},{3,0},{4,7},{5,6},{6,5},{7,4},{8,11},{9,10},{10,... | collective-permute-start | bytes 442376 | tf_op jit(solution)/shard_map/ppermute | solution.py:442
  33.9 1.2 %collective-permute-done.20.refs_11_ = f32[144,128]{1,0:T(8,128)S(1)} collective-permute-done((f32[144,128]{1,0:T(8,128)S(1)}, f32[144,128]{1,0:T(8,128)S(1)}, u32[]{:S(2)}, u32[]{:S(2)}) %collective-permute-start.20) | collective-permute-done | bytes 73760 | tf_op jit(solution)/shard_map/ppermute | solution.py:442
  35.0 1.2 %collective-permute-start.16 = (f32[288,128]{1,0:T(8,128)S(1)}, f32[288,128]{1,0:T(8,128)S(1)}, u32[]{:S(2)}, u32[]{:S(2)}) collective-permute-start(f32[288,128]{1,0:T(8,128)S(1)} %get-tuple-element.76), channel_id=1, source_target_pairs={{0,2},{1,3},{2,0},{3,1},{4,6},{5,7},{6,4},{7,5},{8,10},{9,11},{10,... | collective-permute-start | bytes 442376 | tf_op jit(solution)/shard_map/ppermute | solution.py:442
  36.2 0.4 collective-permute-start.19
  36.6 2.0 %collective-permute-done.15.refs_6_ = f32[288,128]{1,0:T(8,128)S(1)} collective-permute-done((f32[288,128]{1,0:T(8,128)S(1)}, f32[288,128]{1,0:T(8,128)S(1)}, u32[]{:S(2)}, u32[]{:S(2)}) %collective-permute-start.15) | collective-permute-done | bytes 147488 | tf_op jit(solution)/shard_map/ppermute | solution.py:442
  38.6 2.7 %collective-permute-done.18.refs_9_ = f32[288,128]{1,0:T(8,128)S(1)} collective-permute-done((f32[288,128]{1,0:T(8,128)S(1)}, f32[288,128]{1,0:T(8,128)S(1)}, u32[]{:S(2)}, u32[]{:S(2)}) %collective-permute-start.18) | collective-permute-done | bytes 147488 | tf_op jit(solution)/shard_map/ppermute | solution.py:442
  41.3 1.3 %collective-permute-start.23 = (f32[144,128]{1,0:T(8,128)S(1)}, f32[144,128]{1,0:T(8,128)S(1)}, u32[]{:S(2)}, u32[]{:S(2)}) collective-permute-start(f32[144,128]{1,0:T(8,128)S(1)} %get-tuple-element.84), channel_id=1, source_target_pairs={{0,2},{1,3},{2,0},{3,1},{4,6},{5,7},{6,4},{7,5},{8,10},{9,11},{10,... | collective-permute-start | bytes 221192 | tf_op jit(solution)/shard_map/ppermute | solution.py:442
  42.9 0.9 shard_map.87.refs_4_.refs_7_.refs_12_
  43.8 1.4 %shard_map.88 = (f32[432,128]{1,0:T(8,128)S(1)}, f32[432,128]{1,0:T(8,128)S(1)}, f32[432,128]{1,0:T(8,128)S(1)}, f32[432,128]{1,0:T(8,128)S(1)}) custom-call(s32[2]{0:T(128)S(1)} %pad_add_fusion.scalars, f32[432,128]{1,0:T(8,128)S(1)} %get-tuple-element.58.refs_5_.refs_0_, f32[432,128]{1,0:T(8,128)S(1)} %collective-permute-done.refs_1_, ...), custom_call_target="tpu_custom_call" | custom-call | tf_op jit(solution)/shard_map/pallas_call | solution.py:427
  45.2 2.4 %collective-permute-done.19.refs_10_ = f32[288,128]{1,0:T(8,128)S(1)} collective-permute-done((f32[288,128]{1,0:T(8,128)S(1)}, f32[288,128]{1,0:T(8,128)S(1)}, u32[]{:S(2)}, u32[]{:S(2)}) %collective-permute-start.19) | collective-permute-done | bytes 147488 | tf_op jit(solution)/shard_map/ppermute | solution.py:442
  47.7 1.4 %shard_map.89 = (f32[432,128]{1,0:T(8,128)S(1)}, f32[432,128]{1,0:T(8,128)S(1)}, f32[144,128]{1,0:T(8,128)S(1)}, f32[288,128]{1,0:T(8,128)S(1)}, f32[288,128]{1,...) custom-call(s32[2]{0:T(128)S(1)} %pad_add_fusion.scalars, ...), custom_call_target="tpu_custom_call" | custom-call | tf_op jit(solution)/shard_map/pallas_call | solution.py:427
  49.0 0.6 collective-permute-done.23.refs_8_
  49.7 1.2 %collective-permute-done.24.refs_11_ = f32[144,128]{1,0:T(8,128)S(1)} collective-permute-done((f32[144,128]{1,0:T(8,128)S(1)}, f32[144,128]{1,0:T(8,128)S(1)}, u32[]{:S(2)}, u32[]{:S(2)}) %collective-permute-start.24) | collective-permute-done | bytes 73760 | tf_op jit(solution)/shard_map/ppermute | solution.py:442
  50.8 1.4 %shard_map.90 = (f32[432,128]{1,0:T(8,128)S(1)}, f32[432,128]{1,0:T(8,128)S(1)}, f32[144,128]{1,0:T(8,128)S(1)}, f32[288,128]{1,0:T(8,128)S(1)}, f32[288,128]{1,...) custom-call(s32[2]{0:T(128)S(1)} %pad_add_fusion.scalars, ...), custom_call_target="tpu_custom_call", output_to_operand_aliasing={{3}: (17, {}), {4}: (18, {}), {6}: (19, {}), {7}: (20, {})} | custom-call | tf_op jit(solution)/shard_map/pallas_call | solution.py:427
  52.4 0.4 collective-permute-start.21
  52.8 1.3 %collective-permute-start.28 = (f32[144,128]{1,0:T(8,128)S(1)}, f32[144,128]{1,0:T(8,128)S(1)}, u32[]{:S(2)}, u32[]{:S(2)}) collective-permute-start(f32[144,128]{1,0:T(8,128)S(1)} %get-tuple-element.94), channel_id=1, source_target_pairs={{0,2},{1,3},{2,0},{3,1},{4,6},{5,7},{6,4},{7,5},{8,10},{9,11},{10,... | collective-permute-start | bytes 221192 | tf_op jit(solution)/shard_map/ppermute | solution.py:442
  54.2 1.4 %collective-permute-start.26 = (f32[144,128]{1,0:T(8,128)S(1)}, f32[144,128]{1,0:T(8,128)S(1)}, u32[]{:S(2)}, u32[]{:S(2)}) collective-permute-start(f32[144,128]{1,0:T(8,128)S(1)} %get-tuple-element.92), channel_id=1, source_target_pairs={{0,2},{1,3},{2,0},{3,1},{4,6},{5,7},{6,4},{7,5},{8,10},{9,11},{10,... | collective-permute-start | bytes 221192 | tf_op jit(solution)/shard_map/ppermute | solution.py:442
  55.6 1.5 %collective-permute-done.28.refs_6_ = f32[144,128]{1,0:T(8,128)S(1)} collective-permute-done((f32[144,128]{1,0:T(8,128)S(1)}, f32[144,128]{1,0:T(8,128)S(1)}, u32[]{:S(2)}, u32[]{:S(2)}) %collective-permute-start.28) | collective-permute-done | bytes 73760 | tf_op jit(solution)/shard_map/ppermute | solution.py:442
  57.2 1.5 %collective-permute-done.29.refs_7_ = f32[144,128]{1,0:T(8,128)S(1)} collective-permute-done((f32[144,128]{1,0:T(8,128)S(1)}, f32[144,128]{1,0:T(8,128)S(1)}, u32[]{:S(2)}, u32[]{:S(2)}) %collective-permute-start.29) | collective-permute-done | bytes 73760 | tf_op jit(solution)/shard_map/ppermute | solution.py:442
  58.7 0.7 collective-permute-start.30
  59.4 1.0 collective-permute-done.26.refs_4_
  60.3 0.3 collective-permute-start.31
  60.7 0.8 collective-permute-done.27.refs_5_
  61.5 2.0 %collective-permute-start.32 = (f32[288,128]{1,0:T(8,128)S(1)}, f32[288,128]{1,0:T(8,128)S(1)}, u32[]{:S(2)}, u32[]{:S(2)}) collective-permute-start(f32[288,128]{1,0:T(8,128)S(1)} %get-tuple-element.100), channel_id=1, source_target_pairs={{0,2},{1,3},{2,0},{3,1},{4,6},{5,7},{6,4},{7,5},{8,10},{9,11},{10,... | collective-permute-start | bytes 442376 | tf_op jit(solution)/shard_map/ppermute | solution.py:442
  63.5 1.6 %shard_map.91 = (f32[576,128]{1,0:T(8,128)S(1)}, f32[576,128]{1,0:T(8,128)S(1)}, f32[576,128]{1,0:T(8,128)S(1)}) custom-call(s32[2]{0:T(128)S(1)} %pad_add_fusion.scalars, f32[432,128]{1,0:T(8,128)S(1)} %get-tuple-element.81.refs_15_.refs_0_, f32[432,128]{1,0:T(8,128)S(1)} %collective-permute-done.21.refs_1_, ...), custom_call_target="tpu_custom_call" | custom-call | tf_op jit(solution)/shard_map/pallas_call | solution.py:427
  65.0 2.1 %collective-permute-start.34 = (f32[576,128]{1,0:T(8,128)S(1)}, f32[576,128]{1,0:T(8,128)S(1)}, u32[]{:S(2)}, u32[]{:S(2)}) collective-permute-start(f32[576,128]{1,0:T(8,128)S(1)} %get-tuple-element.103), channel_id=1, source_target_pairs={{0,4},{4,0},{8,12},{12,8},{16,20},{20,16},{24,28},{28,24},{1,5},{5... | collective-permute-start | bytes 884744 | tf_op jit(solution)/shard_map/ppermute | solution.py:601
  67.2 0.7 collective-permute-done.31.refs_5_
  67.8 1.2 %collective-permute-start.11 = (f32[432,128]{1,0:T(8,128)S(1)}, f32[432,128]{1,0:T(8,128)S(1)}, u32[]{:S(2)}, u32[]{:S(2)}) collective-permute-start(f32[432,128]{1,0:T(8,128)S(1)} %get-tuple-element.70), channel_id=1, source_target_pairs={{0,3},{1,2},{2,1},{3,0},{4,7},{5,6},{6,5},{7,4},{8,11},{9,10},{10,... | collective-permute-start | bytes 663560 | tf_op jit(solution)/shard_map/ppermute | solution.py:442
  69.0 2.7 %collective-permute-done.32.refs_4_ = f32[288,128]{1,0:T(8,128)S(1)} collective-permute-done((f32[288,128]{1,0:T(8,128)S(1)}, f32[288,128]{1,0:T(8,128)S(1)}, u32[]{:S(2)}, u32[]{:S(2)}) %collective-permute-start.32) | collective-permute-done | bytes 147488 | tf_op jit(solution)/shard_map/ppermute | solution.py:442
  71.7 0.9 collective-permute-start.33
  72.7 1.5 %shard_map.92 = (f32[576,128]{1,0:T(8,128)S(1)}, f32[576,128]{1,0:T(8,128)S(1)}, f32[576,128]{1,0:T(8,128)S(1)}) custom-call(s32[2]{0:T(128)S(1)} %pad_add_fusion.scalars, f32[432,128]{1,0:T(8,128)S(1)} %get-tuple-element.81.refs_15_.refs_0_, f32[432,128]{1,0:T(8,128)S(1)} %collective-permute-done.21.refs_1_, ...), custom_call_target="tpu_custom_call" | custom-call | tf_op jit(solution)/shard_map/pallas_call | solution.py:427
  74.2 9.4 %collective-permute-done.33.refs_5_ = f32[288,128]{1,0:T(8,128)S(1)} collective-permute-done((f32[288,128]{1,0:T(8,128)S(1)}, f32[288,128]{1,0:T(8,128)S(1)}, u32[]{:S(2)}, u32[]{:S(2)}) %collective-permute-start.33) | collective-permute-done | bytes 147488 | tf_op jit(solution)/shard_map/ppermute | solution.py:442
  83.6 2.5 %collective-permute-start.35 = (f32[576,128]{1,0:T(8,128)S(1)}, f32[576,128]{1,0:T(8,128)S(1)}, u32[]{:S(2)}, u32[]{:S(2)}) collective-permute-start(f32[576,128]{1,0:T(8,128)S(1)} %get-tuple-element.104), channel_id=1, source_target_pairs={{0,24},{4,28},{8,0},{12,4},{16,8},{20,12},{24,16},{28,20},{1,25},{... | collective-permute-start | bytes 884744 | tf_op jit(solution)/shard_map/ppermute | solution.py:600
  86.1 1.5 %shard_map.93 = (f32[576,128]{1,0:T(8,128)S(1)}, f32[576,128]{1,0:T(8,128)S(1)}, f32[576,128]{1,0:T(8,128)S(1)}) custom-call(s32[2]{0:T(128)S(1)} %pad_add_fusion.scalars, f32[432,128]{1,0:T(8,128)S(1)} %get-tuple-element.81.refs_15_.refs_0_, f32[432,128]{1,0:T(8,128)S(1)} %collective-permute-done.21.refs_1_, ...), custom_call_target="tpu_custom_call" | custom-call | tf_op jit(solution)/shard_map/pallas_call | solution.py:427
  87.6 1.6 %collective-permute-start.36 = (f32[576,128]{1,0:T(8,128)S(1)}, f32[576,128]{1,0:T(8,128)S(1)}, u32[]{:S(2)}, u32[]{:S(2)}) collective-permute-start(f32[576,128]{1,0:T(8,128)S(1)} %get-tuple-element.105), channel_id=1, source_target_pairs={{0,4},{4,0},{8,12},{12,8},{16,20},{20,16},{24,28},{28,24},{1,5},{5... | collective-permute-start | bytes 884744 | tf_op jit(solution)/shard_map/ppermute | solution.py:601
  89.2 0.7 collective-permute-start.37
  90.0 0.6 collective-permute-start.38
  90.5 0.4 collective-permute-start.39
  90.9 2.6 %collective-permute-done.35.refs_11_ = f32[576,128]{1,0:T(8,128)S(1)} collective-permute-done((f32[576,128]{1,0:T(8,128)S(1)}, f32[576,128]{1,0:T(8,128)S(1)}, u32[]{:S(2)}, u32[]{:S(2)}) %collective-permute-start.35) | collective-permute-done | bytes 294944 | tf_op jit(solution)/shard_map/ppermute | solution.py:600
  93.5 4.1 %collective-permute-done.36.refs_12_ = f32[576,128]{1,0:T(8,128)S(1)} collective-permute-done((f32[576,128]{1,0:T(8,128)S(1)}, f32[576,128]{1,0:T(8,128)S(1)}, u32[]{:S(2)}, u32[]{:S(2)}) %collective-permute-start.36) | collective-permute-done | bytes 294944 | tf_op jit(solution)/shard_map/ppermute | solution.py:601
  97.6 2.2 %collective-permute-done.37.refs_13_ = f32[576,128]{1,0:T(8,128)S(1)} collective-permute-done((f32[576,128]{1,0:T(8,128)S(1)}, f32[576,128]{1,0:T(8,128)S(1)}, u32[]{:S(2)}, u32[]{:S(2)}) %collective-permute-start.37) | collective-permute-done | bytes 294944 | tf_op jit(solution)/shard_map/ppermute | solution.py:600
  99.8 2.7 %shard_map.94 = (f32[24,96,96]{2,1,0:T(8,128)}, f32[576,128]{1,0:T(8,128)S(1)}) custom-call(s32[2]{0:T(128)S(1)} %pad_add_fusion.scalars, f32[432,128]{1,0:T(8,128)S(1)} %get-tuple-element.67.refs_15_.refs_0_, f32[432,128]{1,0:T(8,128)S(1)} %collective-permute-done.9.refs_1_, f32[432,128]{1,0:T(8,128)S(1)} %collective-permute-done.10.refs_2_, ...), custom_call_target="tpu_custom_call" | custom-call | tf_op jit(solution)/shard_map/pallas_call | solution.py:427
  102.8 2.6 %collective-permute-done.39.refs_2_ = f32[576,128]{1,0:T(8,128)S(1)} collective-permute-done((f32[576,128]{1,0:T(8,128)S(1)}, f32[576,128]{1,0:T(8,128)S(1)}, u32[]{:S(2)}, u32[]{:S(2)}) %collective-permute-start.39) | collective-permute-done | bytes 294944 | tf_op jit(solution)/shard_map/ppermute | solution.py:600
  105.4 1.4 %shard_map.95 = f32[24,96,96]{2,1,0:T(8,128)} custom-call(s32[2]{0:T(128)S(1)} %pad_add_fusion.scalars, f32[576,128]{1,0:T(8,128)S(1)} %get-tuple-element.107.refs_0_, f32[576,128]{1,0:T(8,128)S(1)} %collective-permute-done.38.refs_1_, f32[576,128]{1,0:T(8,128)S(1)} %collective-permute-done.39.refs_2_, ...), custom_call_target="tpu_custom_call", output_to_operand_aliasing={{}: (4, {})} | custom-call | tf_op jit(solution)/shard_map/pallas_call | solution.py:427
  (47 shorter events, 1.2 us)
Async XLA Ops:
  0.0 6.7 %copy-start = (bf16[256,256]{1,0:T(8,128)(2,1)S(1)}, bf16[256,256]{1,0:T(8,128)(2,1)}, u32[]{:S(2)}) copy-start(bf16[256,256]{1,0:T(8,128)(2,1)} %constant.36.clone.refs_1_.refs_3_.refs_17_.refs_15_.refs_14_) | copy-start | bytes 393220
  0.0 6.7 %copy-start.1 = (bf16[4,256,192]{2,1,0:T(8,128)(2,1)S(1)}, bf16[4,256,192]{2,1,0:T(8,128)(2,1)}, u32[]{:S(2)}) copy-start(bf16[4,256,192]{2,1,0:T(8,128)(2,1)} %constant.37.clone.refs_2_.refs_4_) | copy-start | bytes 1179652
  0.1 1.3 %copy-start.3 = (f32[1,24,96,96]{3,2,1,0:T(8,128)S(1)}, f32[1,24,96,96]{3,2,1,0:T(8,128)}, u32[]{:S(2)}) copy-start(f32[1,24,96,96]{3,2,1,0:T(8,128)} %param.8) | copy-start | bytes 2654212
  2.1 13.0 %collective-permute-start.8 = (f32[576,128]{1,0:T(8,128)S(1)}, f32[576,128]{1,0:T(8,128)S(1)}, u32[]{:S(2)}, u32[]{:S(2)}) collective-permute-start(f32[576,128]{1,0:T(8,128)S(1)} %shard_map.82.refs_3_.refs_0_.refs_8_.refs_6_.refs_7_), channel_id=1, source_target_pairs={{0,8},{4,12},{8,16},{12,20},{16,24},{20,28},{24,0},{28,4},{1,9},{5... | collective-permute-start | bytes 884744 | tf_op jit(solution)/shard_map/ppermute | solution.py:483
  5.2 11.6 %collective-permute-start.7 = (f32[576,128]{1,0:T(8,128)S(1)}, f32[576,128]{1,0:T(8,128)S(1)}, u32[]{:S(2)}, u32[]{:S(2)}) collective-permute-start(f32[576,128]{1,0:T(8,128)S(1)} %shard_map.82.refs_3_.refs_0_.refs_8_.refs_6_.refs_7_), channel_id=1, source_target_pairs={{0,4},{4,0},{8,12},{12,8},{16,20},{20,16},{24,28},{28,24},{1,5},{5... | collective-permute-start | bytes 884744 | tf_op jit(solution)/shard_map/ppermute | solution.py:482
  8.6 12.8 %collective-permute-start.6 = (f32[576,128]{1,0:T(8,128)S(1)}, f32[576,128]{1,0:T(8,128)S(1)}, u32[]{:S(2)}, u32[]{:S(2)}) collective-permute-start(f32[576,128]{1,0:T(8,128)S(1)} %get-tuple-element.63.refs_0_.refs_9_.refs_7_.refs_8_), channel_id=1, source_target_pairs={{0,8},{4,12},{8,16},{12,20},{16,24},{20,28},{24,0},{28,4},{1,9},{5... | collective-permute-start | bytes 884744 | tf_op jit(solution)/shard_map/ppermute | solution.py:483
  10.2 12.9 %collective-permute-start.5 = (f32[576,128]{1,0:T(8,128)S(1)}, f32[576,128]{1,0:T(8,128)S(1)}, u32[]{:S(2)}, u32[]{:S(2)}) collective-permute-start(f32[576,128]{1,0:T(8,128)S(1)} %get-tuple-element.63.refs_0_.refs_9_.refs_7_.refs_8_), channel_id=1, source_target_pairs={{0,4},{4,0},{8,12},{12,8},{16,20},{20,16},{24,28},{28,24},{1,5},{5... | collective-permute-start | bytes 884744 | tf_op jit(solution)/shard_map/ppermute | solution.py:482
  10.7 16.2 %collective-permute-start.4 = (f32[576,128]{1,0:T(8,128)S(1)}, f32[576,128]{1,0:T(8,128)S(1)}, u32[]{:S(2)}, u32[]{:S(2)}) collective-permute-start(f32[576,128]{1,0:T(8,128)S(1)} %get-tuple-element.62.refs_0_.refs_10_.refs_8_.refs_9_), channel_id=1, source_target_pairs={{0,8},{4,12},{8,16},{12,20},{16,24},{20,28},{24,0},{28,4},{1,9},{5... | collective-permute-start | bytes 884744 | tf_op jit(solution)/shard_map/ppermute | solution.py:483
  15.1 11.8 %collective-permute-start.3 = (f32[576,128]{1,0:T(8,128)S(1)}, f32[576,128]{1,0:T(8,128)S(1)}, u32[]{:S(2)}, u32[]{:S(2)}) collective-permute-start(f32[576,128]{1,0:T(8,128)S(1)} %get-tuple-element.62.refs_0_.refs_10_.refs_8_.refs_9_), channel_id=1, source_target_pairs={{0,4},{4,0},{8,12},{12,8},{16,20},{20,16},{24,28},{28,24},{1,5},{5... | collective-permute-start | bytes 884744 | tf_op jit(solution)/shard_map/ppermute | solution.py:482
  16.8 12.1 %collective-permute-start = (f32[432,128]{1,0:T(8,128)S(1)}, f32[432,128]{1,0:T(8,128)S(1)}, u32[]{:S(2)}, u32[]{:S(2)}) collective-permute-start(f32[432,128]{1,0:T(8,128)S(1)} %get-tuple-element.59), channel_id=1, source_target_pairs={{0,1},{1,0},{2,3},{3,2},{4,5},{5,4},{6,7},{7,6},{8,9},{9,8},{10,11... | collective-permute-start | bytes 663560 | tf_op jit(solution)/shard_map/ppermute | solution.py:442
  21.4 9.1 %collective-permute-start.1 = (f32[432,128]{1,0:T(8,128)S(1)}, f32[432,128]{1,0:T(8,128)S(1)}, u32[]{:S(2)}, u32[]{:S(2)}) collective-permute-start(f32[432,128]{1,0:T(8,128)S(1)} %get-tuple-element.60), channel_id=1, source_target_pairs={{0,2},{1,3},{2,0},{3,1},{4,6},{5,7},{6,4},{7,5},{8,10},{9,11},{10,... | collective-permute-start | bytes 663560 | tf_op jit(solution)/shard_map/ppermute | solution.py:442
  23.1 8.3 %collective-permute-start.2 = (f32[432,128]{1,0:T(8,128)S(1)}, f32[432,128]{1,0:T(8,128)S(1)}, u32[]{:S(2)}, u32[]{:S(2)}) collective-permute-start(f32[432,128]{1,0:T(8,128)S(1)} %get-tuple-element.61), channel_id=1, source_target_pairs={{0,3},{1,2},{2,1},{3,0},{4,7},{5,6},{6,5},{7,4},{8,11},{9,10},{10,... | collective-permute-start | bytes 663560 | tf_op jit(solution)/shard_map/ppermute | solution.py:442
  26.1 16.8 %copy-start.6 = (f32[4,24,128]{2,1,0:T(8,128)S(1)}, f32[4,24,128]{2,1,0:T(8,128)}, u32[]{:S(2)}) copy-start(f32[4,24,128]{2,1,0:T(8,128)} %constant.42.clone.refs_1_) | copy-start | bytes 147460
  26.1 16.8 %copy-start.7 = (f32[96,128]{1,0:T(8,128)S(1)}, f32[96,128]{1,0:T(8,128)}, u32[]{:S(2)}) copy-start(f32[96,128]{1,0:T(8,128)} %constant.41.clone.refs_0_) | copy-start | bytes 147460
  26.9 9.3 %collective-permute-start.12 = (f32[288,128]{1,0:T(8,128)S(1)}, f32[288,128]{1,0:T(8,128)S(1)}, u32[]{:S(2)}, u32[]{:S(2)}) collective-permute-start(f32[288,128]{1,0:T(8,128)S(1)} %get-tuple-element.72), channel_id=1, source_target_pairs={{0,1},{1,0},{2,3},{3,2},{4,5},{5,4},{6,7},{7,6},{8,9},{9,8},{10,11... | collective-permute-start | bytes 442376 | tf_op jit(solution)/shard_map/ppermute | solution.py:442
  26.9 16.9 %copy-start.4 = (bf16[4,192,192]{2,1,0:T(8,128)(2,1)S(1)}, bf16[4,192,192]{2,1,0:T(8,128)(2,1)}, u32[]{:S(2)}) copy-start(bf16[4,192,192]{2,1,0:T(8,128)(2,1)} %constant.40.clone.refs_6_.refs_14_) | copy-start | bytes 884740
  26.9 16.9 %copy-start.5 = (bf16[4,192,192]{2,1,0:T(8,128)(2,1)S(1)}, bf16[4,192,192]{2,1,0:T(8,128)(2,1)}, u32[]{:S(2)}) copy-start(bf16[4,192,192]{2,1,0:T(8,128)(2,1)} %constant.39.clone.refs_5_.refs_13_) | copy-start | bytes 884740
  28.4 3.7 %collective-permute-start.14 = (f32[144,128]{1,0:T(8,128)S(1)}, f32[144,128]{1,0:T(8,128)S(1)}, u32[]{:S(2)}, u32[]{:S(2)}) collective-permute-start(f32[144,128]{1,0:T(8,128)S(1)} %get-tuple-element.74), channel_id=1, source_target_pairs={{0,1},{1,0},{2,3},{3,2},{4,5},{5,4},{6,7},{7,6},{8,9},{9,8},{10,11... | collective-permute-start | bytes 221192 | tf_op jit(solution)/shard_map/ppermute | solution.py:442
  29.0 4.9 %collective-permute-start.17 = (f32[144,128]{1,0:T(8,128)S(1)}, f32[144,128]{1,0:T(8,128)S(1)}, u32[]{:S(2)}, u32[]{:S(2)}) collective-permute-start(f32[144,128]{1,0:T(8,128)S(1)} %get-tuple-element.77), channel_id=1, source_target_pairs={{0,2},{1,3},{2,0},{3,1},{4,6},{5,7},{6,4},{7,5},{8,10},{9,11},{10,... | collective-permute-start | bytes 221192 | tf_op jit(solution)/shard_map/ppermute | solution.py:442
  30.5 4.6 %collective-permute-start.20 = (f32[144,128]{1,0:T(8,128)S(1)}, f32[144,128]{1,0:T(8,128)S(1)}, u32[]{:S(2)}, u32[]{:S(2)}) collective-permute-start(f32[144,128]{1,0:T(8,128)S(1)} %get-tuple-element.80), channel_id=1, source_target_pairs={{0,3},{1,2},{2,1},{3,0},{4,7},{5,6},{6,5},{7,4},{8,11},{9,10},{10,... | collective-permute-start | bytes 221192 | tf_op jit(solution)/shard_map/ppermute | solution.py:442
  31.5 7.2 %collective-permute-start.15 = (f32[288,128]{1,0:T(8,128)S(1)}, f32[288,128]{1,0:T(8,128)S(1)}, u32[]{:S(2)}, u32[]{:S(2)}) collective-permute-start(f32[288,128]{1,0:T(8,128)S(1)} %get-tuple-element.75), channel_id=1, source_target_pairs={{0,2},{1,3},{2,0},{3,1},{4,6},{5,7},{6,4},{7,5},{8,10},{9,11},{10,... | collective-permute-start | bytes 442376 | tf_op jit(solution)/shard_map/ppermute | solution.py:442
  32.1 9.3 %collective-permute-start.18 = (f32[288,128]{1,0:T(8,128)S(1)}, f32[288,128]{1,0:T(8,128)S(1)}, u32[]{:S(2)}, u32[]{:S(2)}) collective-permute-start(f32[288,128]{1,0:T(8,128)S(1)} %get-tuple-element.78), channel_id=1, source_target_pairs={{0,3},{1,2},{2,1},{3,0},{4,7},{5,6},{6,5},{7,4},{8,11},{9,10},{10,... | collective-permute-start | bytes 442376 | tf_op jit(solution)/shard_map/ppermute | solution.py:442
  33.9 8.8 %collective-permute-start.13 = (f32[288,128]{1,0:T(8,128)S(1)}, f32[288,128]{1,0:T(8,128)S(1)}, u32[]{:S(2)}, u32[]{:S(2)}) collective-permute-start(f32[288,128]{1,0:T(8,128)S(1)} %get-tuple-element.73), channel_id=1, source_target_pairs={{0,1},{1,0},{2,3},{3,2},{4,5},{5,4},{6,7},{7,6},{8,9},{9,8},{10,11... | collective-permute-start | bytes 442376 | tf_op jit(solution)/shard_map/ppermute | solution.py:442
  35.0 10.2 %collective-permute-start.16 = (f32[288,128]{1,0:T(8,128)S(1)}, f32[288,128]{1,0:T(8,128)S(1)}, u32[]{:S(2)}, u32[]{:S(2)}) collective-permute-start(f32[288,128]{1,0:T(8,128)S(1)} %get-tuple-element.76), channel_id=1, source_target_pairs={{0,2},{1,3},{2,0},{3,1},{4,6},{5,7},{6,4},{7,5},{8,10},{9,11},{10,... | collective-permute-start | bytes 442376 | tf_op jit(solution)/shard_map/ppermute | solution.py:442
  36.2 11.4 %collective-permute-start.19 = (f32[288,128]{1,0:T(8,128)S(1)}, f32[288,128]{1,0:T(8,128)S(1)}, u32[]{:S(2)}, u32[]{:S(2)}) collective-permute-start(f32[288,128]{1,0:T(8,128)S(1)} %get-tuple-element.79), channel_id=1, source_target_pairs={{0,3},{1,2},{2,1},{3,0},{4,7},{5,6},{6,5},{7,4},{8,11},{9,10},{10,... | collective-permute-start | bytes 442376 | tf_op jit(solution)/shard_map/ppermute | solution.py:442
  38.6 10.4 %collective-permute-start.22 = (f32[144,128]{1,0:T(8,128)S(1)}, f32[144,128]{1,0:T(8,128)S(1)}, u32[]{:S(2)}, u32[]{:S(2)}) collective-permute-start(f32[144,128]{1,0:T(8,128)S(1)} %get-tuple-element.83), channel_id=1, source_target_pairs={{0,1},{1,0},{2,3},{3,2},{4,5},{5,4},{6,7},{7,6},{8,9},{9,8},{10,11... | collective-permute-start | bytes 221192 | tf_op jit(solution)/shard_map/ppermute | solution.py:442
  41.3 8.3 %collective-permute-start.23 = (f32[144,128]{1,0:T(8,128)S(1)}, f32[144,128]{1,0:T(8,128)S(1)}, u32[]{:S(2)}, u32[]{:S(2)}) collective-permute-start(f32[144,128]{1,0:T(8,128)S(1)} %get-tuple-element.84), channel_id=1, source_target_pairs={{0,2},{1,3},{2,0},{3,1},{4,6},{5,7},{6,4},{7,5},{8,10},{9,11},{10,... | collective-permute-start | bytes 221192 | tf_op jit(solution)/shard_map/ppermute | solution.py:442
  42.7 8.2 %collective-permute-start.24 = (f32[144,128]{1,0:T(8,128)S(1)}, f32[144,128]{1,0:T(8,128)S(1)}, u32[]{:S(2)}, u32[]{:S(2)}) collective-permute-start(f32[144,128]{1,0:T(8,128)S(1)} %get-tuple-element.85), channel_id=1, source_target_pairs={{0,3},{1,2},{2,1},{3,0},{4,7},{5,6},{6,5},{7,4},{8,11},{9,10},{10,... | collective-permute-start | bytes 221192 | tf_op jit(solution)/shard_map/ppermute | solution.py:442
  50.8 12.6 %copy-start.2 = (bf16[4,192,256]{2,1,0:T(8,128)(2,1)S(1)}, bf16[4,192,256]{2,1,0:T(8,128)(2,1)}, u32[]{:S(2)}) copy-start(bf16[4,192,256]{2,1,0:T(8,128)(2,1)} %constant.38.clone.refs_18_.refs_16_.refs_15_) | copy-start | bytes 1179652
  52.2 11.3 %collective-permute-start.25 = (f32[432,128]{1,0:T(8,128)S(1)}, f32[432,128]{1,0:T(8,128)S(1)}, u32[]{:S(2)}, u32[]{:S(2)}) collective-permute-start(f32[432,128]{1,0:T(8,128)S(1)} %get-tuple-element.91), channel_id=1, source_target_pairs={{0,1},{1,0},{2,3},{3,2},{4,5},{5,4},{6,7},{7,6},{8,9},{9,8},{10,11... | collective-permute-start | bytes 663560 | tf_op jit(solution)/shard_map/ppermute | solution.py:442
  52.4 11.1 %collective-permute-start.21 = (f32[432,128]{1,0:T(8,128)S(1)}, f32[432,128]{1,0:T(8,128)S(1)}, u32[]{:S(2)}, u32[]{:S(2)}) collective-permute-start(f32[432,128]{1,0:T(8,128)S(1)} %get-tuple-element.82), channel_id=1, source_target_pairs={{0,1},{1,0},{2,3},{3,2},{4,5},{5,4},{6,7},{7,6},{8,9},{9,8},{10,11... | collective-permute-start | bytes 663560 | tf_op jit(solution)/shard_map/ppermute | solution.py:442
  52.8 4.4 %collective-permute-start.28 = (f32[144,128]{1,0:T(8,128)S(1)}, f32[144,128]{1,0:T(8,128)S(1)}, u32[]{:S(2)}, u32[]{:S(2)}) collective-permute-start(f32[144,128]{1,0:T(8,128)S(1)} %get-tuple-element.94), channel_id=1, source_target_pairs={{0,2},{1,3},{2,0},{3,1},{4,6},{5,7},{6,4},{7,5},{8,10},{9,11},{10,... | collective-permute-start | bytes 221192 | tf_op jit(solution)/shard_map/ppermute | solution.py:442
  54.1 4.6 %collective-permute-start.29 = (f32[144,128]{1,0:T(8,128)S(1)}, f32[144,128]{1,0:T(8,128)S(1)}, u32[]{:S(2)}, u32[]{:S(2)}) collective-permute-start(f32[144,128]{1,0:T(8,128)S(1)} %get-tuple-element.95), channel_id=1, source_target_pairs={{0,3},{1,2},{2,1},{3,0},{4,7},{5,6},{6,5},{7,4},{8,11},{9,10},{10,... | collective-permute-start | bytes 221192 | tf_op jit(solution)/shard_map/ppermute | solution.py:442
  54.2 6.1 %collective-permute-start.26 = (f32[144,128]{1,0:T(8,128)S(1)}, f32[144,128]{1,0:T(8,128)S(1)}, u32[]{:S(2)}, u32[]{:S(2)}) collective-permute-start(f32[144,128]{1,0:T(8,128)S(1)} %get-tuple-element.92), channel_id=1, source_target_pairs={{0,2},{1,3},{2,0},{3,1},{4,6},{5,7},{6,4},{7,5},{8,10},{9,11},{10,... | collective-permute-start | bytes 221192 | tf_op jit(solution)/shard_map/ppermute | solution.py:442
  57.2 4.3 %collective-permute-start.27 = (f32[144,128]{1,0:T(8,128)S(1)}, f32[144,128]{1,0:T(8,128)S(1)}, u32[]{:S(2)}, u32[]{:S(2)}) collective-permute-start(f32[144,128]{1,0:T(8,128)S(1)} %get-tuple-element.93), channel_id=1, source_target_pairs={{0,3},{1,2},{2,1},{3,0},{4,7},{5,6},{6,5},{7,4},{8,11},{9,10},{10,... | collective-permute-start | bytes 221192 | tf_op jit(solution)/shard_map/ppermute | solution.py:442
  58.7 8.5 %collective-permute-start.30 = (f32[288,128]{1,0:T(8,128)S(1)}, f32[288,128]{1,0:T(8,128)S(1)}, u32[]{:S(2)}, u32[]{:S(2)}) collective-permute-start(f32[288,128]{1,0:T(8,128)S(1)} %get-tuple-element.97), channel_id=1, source_target_pairs={{0,2},{1,3},{2,0},{3,1},{4,6},{5,7},{6,4},{7,5},{8,10},{9,11},{10,... | collective-permute-start | bytes 442376 | tf_op jit(solution)/shard_map/ppermute | solution.py:442
  60.3 7.5 %collective-permute-start.31 = (f32[288,128]{1,0:T(8,128)S(1)}, f32[288,128]{1,0:T(8,128)S(1)}, u32[]{:S(2)}, u32[]{:S(2)}) collective-permute-start(f32[288,128]{1,0:T(8,128)S(1)} %get-tuple-element.98), channel_id=1, source_target_pairs={{0,3},{1,2},{2,1},{3,0},{4,7},{5,6},{6,5},{7,4},{8,11},{9,10},{10,... | collective-permute-start | bytes 442376 | tf_op jit(solution)/shard_map/ppermute | solution.py:442
  61.5 10.2 %collective-permute-start.32 = (f32[288,128]{1,0:T(8,128)S(1)}, f32[288,128]{1,0:T(8,128)S(1)}, u32[]{:S(2)}, u32[]{:S(2)}) collective-permute-start(f32[288,128]{1,0:T(8,128)S(1)} %get-tuple-element.100), channel_id=1, source_target_pairs={{0,2},{1,3},{2,0},{3,1},{4,6},{5,7},{6,4},{7,5},{8,10},{9,11},{10,... | collective-permute-start | bytes 442376 | tf_op jit(solution)/shard_map/ppermute | solution.py:442
  65.0 25.5 %collective-permute-start.34 = (f32[576,128]{1,0:T(8,128)S(1)}, f32[576,128]{1,0:T(8,128)S(1)}, u32[]{:S(2)}, u32[]{:S(2)}) collective-permute-start(f32[576,128]{1,0:T(8,128)S(1)} %get-tuple-element.103), channel_id=1, source_target_pairs={{0,4},{4,0},{8,12},{12,8},{16,20},{20,16},{24,28},{28,24},{1,5},{5... | collective-permute-start | bytes 884744 | tf_op jit(solution)/shard_map/ppermute | solution.py:601
  67.2 20.5 %collective-permute-start.9 = (f32[432,128]{1,0:T(8,128)S(1)}, f32[432,128]{1,0:T(8,128)S(1)}, u32[]{:S(2)}, u32[]{:S(2)}) collective-permute-start(f32[432,128]{1,0:T(8,128)S(1)} %get-tuple-element.68), channel_id=1, source_target_pairs={{0,1},{1,0},{2,3},{3,2},{4,5},{5,4},{6,7},{7,6},{8,9},{9,8},{10,11... | collective-permute-start | bytes 663560 | tf_op jit(solution)/shard_map/ppermute | solution.py:442
  67.2 22.1 %collective-permute-start.10 = (f32[432,128]{1,0:T(8,128)S(1)}, f32[432,128]{1,0:T(8,128)S(1)}, u32[]{:S(2)}, u32[]{:S(2)}) collective-permute-start(f32[432,128]{1,0:T(8,128)S(1)} %get-tuple-element.69), channel_id=1, source_target_pairs={{0,2},{1,3},{2,0},{3,1},{4,6},{5,7},{6,4},{7,5},{8,10},{9,11},{10,... | collective-permute-start | bytes 663560 | tf_op jit(solution)/shard_map/ppermute | solution.py:442
  67.8 22.1 %collective-permute-start.11 = (f32[432,128]{1,0:T(8,128)S(1)}, f32[432,128]{1,0:T(8,128)S(1)}, u32[]{:S(2)}, u32[]{:S(2)}) collective-permute-start(f32[432,128]{1,0:T(8,128)S(1)} %get-tuple-element.70), channel_id=1, source_target_pairs={{0,3},{1,2},{2,1},{3,0},{4,7},{5,6},{6,5},{7,4},{8,11},{9,10},{10,... | collective-permute-start | bytes 663560 | tf_op jit(solution)/shard_map/ppermute | solution.py:442
  71.7 11.9 %collective-permute-start.33 = (f32[288,128]{1,0:T(8,128)S(1)}, f32[288,128]{1,0:T(8,128)S(1)}, u32[]{:S(2)}, u32[]{:S(2)}) collective-permute-start(f32[288,128]{1,0:T(8,128)S(1)} %get-tuple-element.101), channel_id=1, source_target_pairs={{0,3},{1,2},{2,1},{3,0},{4,7},{5,6},{6,5},{7,4},{8,11},{9,10},{10,... | collective-permute-start | bytes 442376 | tf_op jit(solution)/shard_map/ppermute | solution.py:442
  83.6 9.9 %collective-permute-start.35 = (f32[576,128]{1,0:T(8,128)S(1)}, f32[576,128]{1,0:T(8,128)S(1)}, u32[]{:S(2)}, u32[]{:S(2)}) collective-permute-start(f32[576,128]{1,0:T(8,128)S(1)} %get-tuple-element.104), channel_id=1, source_target_pairs={{0,24},{4,28},{8,0},{12,4},{16,8},{20,12},{24,16},{28,20},{1,25},{... | collective-permute-start | bytes 884744 | tf_op jit(solution)/shard_map/ppermute | solution.py:600
  87.6 9.9 %collective-permute-start.36 = (f32[576,128]{1,0:T(8,128)S(1)}, f32[576,128]{1,0:T(8,128)S(1)}, u32[]{:S(2)}, u32[]{:S(2)}) collective-permute-start(f32[576,128]{1,0:T(8,128)S(1)} %get-tuple-element.105), channel_id=1, source_target_pairs={{0,4},{4,0},{8,12},{12,8},{16,20},{20,16},{24,28},{28,24},{1,5},{5... | collective-permute-start | bytes 884744 | tf_op jit(solution)/shard_map/ppermute | solution.py:601
  89.2 10.6 %collective-permute-start.37 = (f32[576,128]{1,0:T(8,128)S(1)}, f32[576,128]{1,0:T(8,128)S(1)}, u32[]{:S(2)}, u32[]{:S(2)}) collective-permute-start(f32[576,128]{1,0:T(8,128)S(1)} %get-tuple-element.106), channel_id=1, source_target_pairs={{0,24},{4,28},{8,0},{12,4},{16,8},{20,12},{24,16},{28,20},{1,25},{... | collective-permute-start | bytes 884744 | tf_op jit(solution)/shard_map/ppermute | solution.py:600
  90.0 12.8 %collective-permute-start.38 = (f32[576,128]{1,0:T(8,128)S(1)}, f32[576,128]{1,0:T(8,128)S(1)}, u32[]{:S(2)}, u32[]{:S(2)}) collective-permute-start(f32[576,128]{1,0:T(8,128)S(1)} %get-tuple-element.108), channel_id=1, source_target_pairs={{0,4},{4,0},{8,12},{12,8},{16,20},{20,16},{24,28},{28,24},{1,5},{5... | collective-permute-start | bytes 884744 | tf_op jit(solution)/shard_map/ppermute | solution.py:601
  90.5 14.8 %collective-permute-start.39 = (f32[576,128]{1,0:T(8,128)S(1)}, f32[576,128]{1,0:T(8,128)S(1)}, u32[]{:S(2)}, u32[]{:S(2)}) collective-permute-start(f32[576,128]{1,0:T(8,128)S(1)} %get-tuple-element.109), channel_id=1, source_target_pairs={{0,24},{4,28},{8,0},{12,4},{16,8},{20,12},{24,16},{28,20},{1,25},{... | collective-permute-start | bytes 884744 | tf_op jit(solution)/shard_map/ppermute | solution.py:600

commit v5 on v4

--- a/solution.py
+++ b/solution.py
@@ -218,7 +218,7 @@
 LATE = 1
 
 
-def pack_kernel(plan, scalars, ins, outs):
+def pack_kernel(plan, ins, outs):
     for i in range(CHUNK):
         outs[0][i * plan.packed : (i + 1) * plan.packed, :] = pack(widen(ins[0][i]), plan)
 
@@ -247,7 +247,7 @@
     return jnp.concatenate(parts, axis=0)
 
 
-def forward_own_kernel(plan, scalars, ins, outs):
+def forward_own_kernel(plan, ins, outs):
     own_ref, tz_ref, ty_ref = ins
     blocks, later = outs[: plan.parts], outs[plan.parts :]
     for c in range(plan.planes // CHUNK):
@@ -256,15 +256,15 @@
         if c:
             later[c - 1][...] = pack_chunk(wide, plan)
         store_spectrum(
-            plan, wide * wide, tz_ref[...], ty_ref[0], blocks, 0, plan.planes, c * CHUNK
-        )
-
-
-def forward_pair_kernel(plan, scalars, ins, outs):
+            plan, wide * wide, tz_ref[...], ty_ref[lax.axis_index("grid")], blocks, 0, plan.planes, c * CHUNK
+        )
+
+
+def forward_pair_kernel(plan, ins, outs):
     p_ref, q_ref, r_ref, tz_ref, ty_ref = ins
-    even = scalars[1] == 1
+    even = lax.axis_index("band") % 2 == 1
     p, r = p_ref[...], r_ref[...]
-    tz, ty = tz_ref[...], ty_ref[0]
+    tz, ty = tz_ref[...], ty_ref[lax.axis_index("grid")]
     apart = len(outs) > plan.parts
     blocks, base = (outs[plan.parts :], 0) if apart else (outs, plan.rows * CHUNK)
     mixed = q_ref[...] * jnp.where(even, r, p)
@@ -272,13 +272,14 @@
     store_spectrum(plan, unpack_chunk(p * r, plan), tz, ty, outs[: plan.parts], 0, CHUNK, 0)
 
 
-def screen_kernel(plan, scalars, ins, outs):
+def screen_kernel(plan, ins, outs):
     across_ref, within_ref = ins
+    part = lax.axis_index("grid")
     cells = plan.length * plan.height * plan.breadth
     limit = 4.0 * np.pi / plan.length
     rate = 1.0 / (4.0 * limit * limit)
     for row in range(plan.rows):
-        wave_sq = across_ref[...] + within_ref[0, row : row + 1, :]
+        wave_sq = across_ref[...] + within_ref[part, row : row + 1, :]
         guarded = jnp.where(wave_sq > 0, wave_sq, 1.0)
         screened = (-0.2 * 4.0 * np.pi / cells) / guarded * (1.0 - jnp.exp(guarded * -rate))
         outs[0][row * plan.length : (row + 1) * plan.length, :] = jnp.where(
@@ -286,20 +287,22 @@
         )
 
 
-def middle_kernel(plan, chunks, sizes, scalars, ins, outs):
+def middle_kernel(plan, chunks, sizes, ins, outs):
     n, length = plan.parts, plan.length
     blocks = [ins[k * len(chunks) : (k + 1) * len(chunks)] for k in range(n)]
     screen_ref, tf_ref, tb_ref = ins[n * len(chunks) :]
+    part = lax.axis_index("grid")
+    tf, tb = tf_ref[part], tb_ref[part]
     cut = [outs[2 + i * len(sizes) : 2 + (i + 1) * len(sizes)] for i in range(n - 2)]
     for pair in range(plan.rows // 2):
         columns = []
         for row in (pair * 2, pair * 2 + 1):
             parts = []
-            for part in blocks:
-                for ref, (size, base) in zip(part, chunks):
+            for block in blocks:
+                for ref, (size, base) in zip(block, chunks):
                     parts.append(ref[base + row * size : base + (row + 1) * size, :])
             columns.append(jnp.concatenate(parts, axis=0))
-        spectrum = along_rows(tf_ref[0], jnp.concatenate(columns, axis=1))
+        spectrum = along_rows(tf, jnp.concatenate(columns, axis=1))
         screen = jnp.concatenate(
             [
                 screen_ref[row * length : (row + 1) * length, :]
@@ -307,7 +310,7 @@
             ],
             axis=1,
         )
-        back = along_rows(tb_ref[0], spectrum * screen)
+        back = along_rows(tb, spectrum * screen)
         for i in range(2):
             row, lane = pair * 2 + i, slice(i * LANES, (i + 1) * LANES)
             for k in range(n):
@@ -318,7 +321,7 @@
                     at += size
 
 
-def backward_pair_kernel(plan, pieces, piece, scalars, ins, outs):
+def backward_pair_kernel(plan, pieces, piece, ins, outs):
     far = plan.parts - 2
     whole, ins = ins[:4], ins[4:]
     apart = piece == 0
@@ -328,8 +331,8 @@
     p, q, r = (
         planes_of(ins[i * chunks : (i + 1) * chunks], first, size, plan) for i in range(3)
     )
-    tz, ty = ins[3 * chunks][...], ins[3 * chunks + 1][0]
-    even = scalars[1] == 1
+    tz, ty = ins[3 * chunks][...], ins[3 * chunks + 1][lax.axis_index("grid")]
+    even = lax.axis_index("band") % 2 == 1
 
     def solved(which):
         base = 0 if apart else which * plan.rows * size
@@ -356,7 +359,7 @@
         out_ref[first + i] = wide[:, : plan.breadth]
 
 
-def backward_own_kernel(plan, pieces, scalars, ins, outs):
+def backward_own_kernel(plan, pieces, ins, outs):
     n, count, chunks = plan.parts, len(pieces), plan.planes // CHUNK
     ready = count - LATE
     blocks, ins = ins[:n], ins[n:]
@@ -370,7 +373,7 @@
 
     first = 0
     for c, size in enumerate(pieces):
-        value = load_potential(plan, place, range(first, first + size), tz_ref[...], ty_ref[0])
+        value = load_potential(plan, place, range(first, first + size), tz_ref[...], ty_ref[lax.axis_index("grid")])
         value = pack_chunk(value, plan) * planes_of(owns, first, size, plan) + totals[c][...]
         if c < ready:
             value = value + returned[2 * c][...] + returned[2 * c + 1][...]
@@ -380,7 +383,7 @@
         first += size
 
 
-def final_kernel(plan, scalars, ins, outs):
+def final_kernel(plan, ins, outs):
     rest, ys, zs = ins[:LATE], ins[LATE : 2 * LATE], ins[2 * LATE :]
     first = 0
     for part, y, z in zip(rest, ys, zs):
@@ -395,18 +398,14 @@
     array: jax.Array | None = None
 
 
-def call(kernel, scalars, operands, outs, selected=(), chunk=None, after=None):
+def call(kernel, operands, outs, chunk=None, after=None):
     specs = []
     for operand in operands:
-        if any(operand is s for s in selected):
-            specs.append(pl.BlockSpec((1,) + operand.shape[1:], lambda i, s: (s[0], 0, 0)))
-        elif chunk is not None and operand is chunk[0]:
-            specs.append(
-                pl.BlockSpec((CHUNK,) + operand.shape[1:], lambda i, s, c=chunk[1]: (c, 0, 0))
-            )
-        else:
-            zeros = (0,) * operand.ndim
-            specs.append(pl.BlockSpec(operand.shape, lambda i, s, zeros=zeros: zeros))
+        shape, first = operand.shape, 0
+        if chunk is not None and operand is chunk[0]:
+            shape, first = (CHUNK,) + shape[1:], chunk[1]
+        at = (first,) + (0,) * (operand.ndim - 1)
+        specs.append(pl.BlockSpec(shape, lambda i, at=at: at))
     count = len(operands)
     extras = [] if after is None else [after]
     out_specs, shapes, aliases = [], [], {}
@@ -414,28 +413,25 @@
         if not isinstance(out, Block):
             out = Block(out, out[0], 0)
         if out.array is not None:
+            aliases[count + len(extras)] = i
             extras.append(out.array)
-            aliases[count + len(extras)] = i
         shapes.append(jax.ShapeDtypeStruct(out.shape, F32))
         at = (out.index,) + (0,) * (len(out.shape) - 1)
-        out_specs.append(pl.BlockSpec((out.rows,) + out.shape[1:], lambda i, s, at=at: at))
+        out_specs.append(pl.BlockSpec((out.rows,) + out.shape[1:], lambda i, at=at: at))
     seen = count + len(extras)
 
-    def body(scalars, *refs):
-        kernel(scalars, refs[:count], refs[seen:])
+    def body(*refs):
+        kernel(refs[:count], refs[seen:])
 
     return pl.pallas_call(
         body,
-        grid_spec=pltpu.PrefetchScalarGridSpec(
-            num_scalar_prefetch=1,
-            grid=(1,),
-            in_specs=specs + [pl.BlockSpec(memory_space=pl.ANY)] * len(extras),
-            out_specs=out_specs,
-        ),
+        grid=(1,),
+        in_specs=specs + [pl.BlockSpec(memory_space=pl.ANY)] * len(extras),
+        out_specs=out_specs,
         input_output_aliases=aliases,
         out_shape=shapes,
         compiler_params=pltpu.CompilerParams(vmem_limit_bytes=48 * 1024 * 1024),
-    )(scalars, *operands, *extras)
+    )(*operands, *extras)
 
 
 def send(block, k, parts):
@@ -460,9 +456,6 @@
     number = lax.axis_size("band")
     own = bands[0]
     plan = Plan(*own.shape, parts)
-    part = lax.axis_index("grid")
-    even = lax.axis_index("band") % 2
-    scalars = jnp.stack([part, even]).astype(jnp.int32)
     swap = [(i, i ^ 1) for i in range(number)]
     behind = [(i, (i + CYCLE) % number) for i in range(number)]
     ahead = [(i, (i - CYCLE) % number) for i in range(number)]
@@ -475,7 +468,7 @@
     packed = (CHUNK * plan.packed, LANES)
     pieces = pieces_of(plan.planes)
 
-    (first,) = call(functools.partial(pack_kernel, plan), scalars, (own,), [packed], chunk=(own, 0))
+    (first,) = call(functools.partial(pack_kernel, plan), (own,), [packed], chunk=(own, 0))
     q, r = [], []
 
     def shift(chunk):
@@ -485,10 +478,8 @@
     shift(first)
     out = call(
         functools.partial(forward_own_kernel, plan),
-        scalars,
         (own, tz, ty_forward),
         [(plan.block, LANES)] * parts + [packed] * (chunks - 1),
-        (ty_forward,),
         after=first,
     )
     blocks, mine = out[:parts], [first, *out[parts:]]
@@ -502,10 +493,8 @@
         last = c == chunks - 1
         out = call(
             functools.partial(forward_pair_kernel, plan),
-            scalars,
-            (mine[c], q[c], r[c], tz, ty_forward),
+                (mine[c], q[c], r[c], tz, ty_forward),
             [(rows, LANES)] * (2 * parts) if last else [(2 * rows, LANES)] * parts,
-            (ty_forward,),
             after=after,
         )
         after = out[0]
@@ -516,20 +505,16 @@
             pair_in.append(exchange(out, parts))
     (screen,) = call(
         functools.partial(screen_kernel, plan),
-        scalars,
         (across, within),
         [(plan.rows * plan.length, LANES)],
-        (within,),
         after=after,
     )
 
     def middle(ins, places, sizes, outs, after):
         return call(
             functools.partial(middle_kernel, plan, places, sizes),
-            scalars,
-            (*[block for part in ins for block in part], screen, tx_forward, tx_backward),
+                (*[block for part in ins for block in part], screen, tx_forward, tx_backward),
             [(plan.block, LANES)] * 2 + outs,
-            (tx_forward, tx_backward),
             after=after,
         )
 
@@ -578,8 +563,7 @@
         piece = (size * plan.packed, LANES)
         total, y, z = call(
             functools.partial(backward_pair_kernel, plan, pieces, c),
-            scalars,
-            (
+                (
                 mixed_mid[0],
                 mixed_near,
                 visit_mid[0],
@@ -592,7 +576,6 @@
                 ty_backward,
             ),
             [piece] * 3,
-            (ty_backward,),
             after=after,
         )
         after = total
@@ -602,7 +585,6 @@
     ready = len(pieces) - LATE
     partial, *rest = call(
         functools.partial(backward_own_kernel, plan, pieces),
-        scalars,
         (
             *own_back,
             *totals,
@@ -612,13 +594,11 @@
             ty_backward,
         ),
         [whole] + [(size * plan.packed, LANES) for size in pieces[ready:]],
-        (ty_backward,),
         after=after,
     )
     late = sum(pieces[ready:])
     (result,) = call(
         functools.partial(final_kernel, plan),
-        scalars,
         (*rest, *from_y[ready:], *from_z[ready:]),
         [Block(whole, late, whole[0] // late - 1, partial)],
     )

time: 107 us -> 106 us (level)
  Pallas kernels: 20.8 us -> 13.1 us
  waiting for transfers between devices: 48.7 us -> 55 us
    pallas_call x14, Pallas kernels: 20.8 us -> 13.1 us  [call(): pl.pallas_call(body, grid=(1,), in_specs=specs + [pl.BlockSpec(memory_spa...]
    ppermute x28, waiting for transfers between devices: 28.9 us -> 31.6 us  [send(): return lax.ppermute(block, 'grid', [(i, i ^ k) for i in range(parts)])]
    ppermute x3, waiting for transfers between devices: 7.41 us -> 9.96 us  [exchange_term(): from_z.append(lax.ppermute(z, 'band', ahead))]
    ppermute x3, waiting for transfers between devices: 8.1 us -> 9.73 us  [shift(): r.append(lax.ppermute(chunk, 'band', behind))]
    ppermute x28, starting transfers between devices: 17.8 us -> 19.3 us  [send(): return lax.ppermute(block, 'grid', [(i, i ^ k) for i in range(parts)])]
  transfers between devices with their start and end apart: 40 -> 40, of which waited for: 23 -> 24; matrix products, arithmetic and copies ran while one was open for 0% -> 0% of each run, Pallas kernels for 16% -> 11%
where the time goes in v5:
time: 106 us; the launch traced here: 105 us
  waiting for transfers between devices  55 us (52%)
  starting transfers between devices  35.8 us (34%)
  Pallas kernels  13.1 us (12%)
  local copies, waits for them, and re-layouts  1.37 us (1%)
    ppermute x28, waiting for transfers between devices, send(): return lax.ppermute(block, 'grid', [(i, i ^ k) for i in range(parts)])  31.6 us
    ppermute x28, starting transfers between devices, send(): return lax.ppermute(block, 'grid', [(i, i ^ k) for i in range(parts)])  19.3 us
    pallas_call x14, Pallas kernels, call(): pl.pallas_call(body, grid=(1,), in_specs=specs + [pl.BlockSpec(memory_spa...  13.1 us
    ppermute x3, waiting for transfers between devices, exchange_term(): from_z.append(lax.ppermute(z, 'band', ahead))  9.96 us
    ppermute x3, waiting for transfers between devices, shift(): r.append(lax.ppermute(chunk, 'band', behind))  9.73 us
    ppermute x3, starting transfers between devices, shift(): r.append(lax.ppermute(chunk, 'band', behind))  6.31 us
    ppermute x3, starting transfers between devices, shift(): q.append(lax.ppermute(chunk, 'band', swap))  3.76 us
    ppermute x3, starting transfers between devices, exchange_term(): from_y.append(lax.ppermute(y, 'band', swap))  3.7 us
  transfers between devices with their start and end apart: 40, of which 24 were waited for; matrix products, arithmetic and copies ran while one was open for 0% of the time, Pallas kernels for 11%

profile of v5, /device:TPU:0, one launch (start us, length us, event | category | flops | bytes accessed | tf_op | source)
XLA Modules:
  0.0 105.4 jit_solution(9795762686649226729)
XLA Ops:
  0.0 1.3 %copy-done.3 = f32[1,24,96,96]{3,2,1,0:T(8,128)S(1)} copy-done((f32[1,24,96,96]{3,2,1,0:T(8,128)S(1)}, f32[1,24,96,96]{3,2,1,0:T(8,128)}, u32[]{:S(2)}) %copy-start.3) | copy-done | bytes 884760
  1.5 3.1 %collective-permute-start.8 = (f32[576,128]{1,0:T(8,128)S(1)}, f32[576,128]{1,0:T(8,128)S(1)}, u32[]{:S(2)}, u32[]{:S(2)}) collective-permute-start(f32[576,128]{1,0:T(8,128)S(1)} %shard_map.82.refs_3_.refs_0_.refs_8_.refs_6_.refs_7_), channel_id=1, source_target_pairs={{0,8},{4,12},{8,16},{12,20},{16,24},{20,28},{24,0},{28,4},{1,9},{5... | collective-permute-start | bytes 884744 | tf_op jit(solution)/shard_map/ppermute | solution.py:476
  4.6 1.5 %collective-permute-start.7 = (f32[576,128]{1,0:T(8,128)S(1)}, f32[576,128]{1,0:T(8,128)S(1)}, u32[]{:S(2)}, u32[]{:S(2)}) collective-permute-start(f32[576,128]{1,0:T(8,128)S(1)} %shard_map.82.refs_3_.refs_0_.refs_8_.refs_6_.refs_7_), channel_id=1, source_target_pairs={{0,4},{4,0},{8,12},{12,8},{16,20},{20,16},{24,28},{28,24},{1,5},{5... | collective-permute-start | bytes 884744 | tf_op jit(solution)/shard_map/ppermute | solution.py:475
  6.1 1.3 %shard_map.83 = (f32[432,128]{1,0:T(8,128)S(1)}, f32[432,128]{1,0:T(8,128)S(1)}, f32[432,128]{1,0:T(8,128)S(1)}, f32[432,128]{1,0:T(8,128)S(1)}, f32[576,128]{1,0:T(8,128)S(1)}, /*index=5*/f32[576,128]{1,0:T(8,128)S(1)}) custom-call(f32[24,96,96]{2,1,0:T(8,128)S(1)} %bitcast.3, bf16[256,256]{1,0:T(8,128)(2,1)S(1)} %copy-done, ...), custom_call_target="tpu_custom_call" | custom-call | tf_op jit(solution)/shard_map/pallas_call | solution.py:426
  7.4 1.6 %collective-permute-start.6 = (f32[576,128]{1,0:T(8,128)S(1)}, f32[576,128]{1,0:T(8,128)S(1)}, u32[]{:S(2)}, u32[]{:S(2)}) collective-permute-start(f32[576,128]{1,0:T(8,128)S(1)} %get-tuple-element.63.refs_0_.refs_9_.refs_7_.refs_8_), channel_id=1, source_target_pairs={{0,8},{4,12},{8,16},{12,20},{16,24},{20,28},{24,0},{28,4},{1,9},{5... | collective-permute-start | bytes 884744 | tf_op jit(solution)/shard_map/ppermute | solution.py:476
  9.0 0.5 collective-permute-start.5
  9.6 1.6 %collective-permute-start.4 = (f32[576,128]{1,0:T(8,128)S(1)}, f32[576,128]{1,0:T(8,128)S(1)}, u32[]{:S(2)}, u32[]{:S(2)}) collective-permute-start(f32[576,128]{1,0:T(8,128)S(1)} %get-tuple-element.62.refs_0_.refs_10_.refs_8_.refs_9_), channel_id=1, source_target_pairs={{0,8},{4,12},{8,16},{12,20},{16,24},{20,28},{24,0},{28,4},{1,9},{5... | collective-permute-start | bytes 884744 | tf_op jit(solution)/shard_map/ppermute | solution.py:476
  11.1 3.3 %collective-permute-done.8.refs_2_.refs_14_.refs_12_ = f32[576,128]{1,0:T(8,128)S(1)} collective-permute-done((f32[576,128]{1,0:T(8,128)S(1)}, f32[576,128]{1,0:T(8,128)S(1)}, u32[]{:S(2)}, u32[]{:S(2)}) %collective-permute-start.8) | collective-permute-done | bytes 294944 | tf_op jit(solution)/shard_map/ppermute | solution.py:476
  14.5 1.7 %collective-permute-start.3 = (f32[576,128]{1,0:T(8,128)S(1)}, f32[576,128]{1,0:T(8,128)S(1)}, u32[]{:S(2)}, u32[]{:S(2)}) collective-permute-start(f32[576,128]{1,0:T(8,128)S(1)} %get-tuple-element.62.refs_0_.refs_10_.refs_8_.refs_9_), channel_id=1, source_target_pairs={{0,4},{4,0},{8,12},{12,8},{16,20},{20,16},{24,28},{28,24},{1,5},{5... | collective-permute-start | bytes 884744 | tf_op jit(solution)/shard_map/ppermute | solution.py:475
  16.2 4.6 %collective-permute-done.6.refs_2_.refs_15_.refs_13_ = f32[576,128]{1,0:T(8,128)S(1)} collective-permute-done((f32[576,128]{1,0:T(8,128)S(1)}, f32[576,128]{1,0:T(8,128)S(1)}, u32[]{:S(2)}, u32[]{:S(2)}) %collective-permute-start.6) | collective-permute-done | bytes 294944 | tf_op jit(solution)/shard_map/ppermute | solution.py:476
  20.8 1.7 %collective-permute-start.1 = (f32[432,128]{1,0:T(8,128)S(1)}, f32[432,128]{1,0:T(8,128)S(1)}, u32[]{:S(2)}, u32[]{:S(2)}) collective-permute-start(f32[432,128]{1,0:T(8,128)S(1)} %get-tuple-element.60), channel_id=1, source_target_pairs={{0,2},{1,3},{2,0},{3,1},{4,6},{5,7},{6,4},{7,5},{8,10},{9,11},{10,... | collective-permute-start | bytes 663560 | tf_op jit(solution)/shard_map/ppermute | solution.py:438
  22.5 0.9 shard_map.84
  23.5 1.0 shard_map.85
  24.5 1.8 %collective-permute-done.4.refs_2_.refs_16_.refs_14_ = f32[576,128]{1,0:T(8,128)S(1)} collective-permute-done((f32[576,128]{1,0:T(8,128)S(1)}, f32[576,128]{1,0:T(8,128)S(1)}, u32[]{:S(2)}, u32[]{:S(2)}) %collective-permute-start.4) | collective-permute-done | bytes 294944 | tf_op jit(solution)/shard_map/ppermute | solution.py:476
  26.3 1.0 shard_map.86
  27.2 0.6 collective-permute-start.14
  27.8 1.5 %collective-permute-start.17 = (f32[144,128]{1,0:T(8,128)S(1)}, f32[144,128]{1,0:T(8,128)S(1)}, u32[]{:S(2)}, u32[]{:S(2)}) collective-permute-start(f32[144,128]{1,0:T(8,128)S(1)} %get-tuple-element.77), channel_id=1, source_target_pairs={{0,2},{1,3},{2,0},{3,1},{4,6},{5,7},{6,4},{7,5},{8,10},{9,11},{10,... | collective-permute-start | bytes 221192 | tf_op jit(solution)/shard_map/ppermute | solution.py:438
  29.3 2.1 %collective-permute-done.2.refs_3_ = f32[432,128]{1,0:T(8,128)S(1)} collective-permute-done((f32[432,128]{1,0:T(8,128)S(1)}, f32[432,128]{1,0:T(8,128)S(1)}, u32[]{:S(2)}, u32[]{:S(2)}) %collective-permute-start.2) | collective-permute-done | bytes 221216 | tf_op jit(solution)/shard_map/ppermute | solution.py:438
  31.4 0.4 collective-permute-start.15
  31.8 1.8 %collective-permute-start.18 = (f32[288,128]{1,0:T(8,128)S(1)}, f32[288,128]{1,0:T(8,128)S(1)}, u32[]{:S(2)}, u32[]{:S(2)}) collective-permute-start(f32[288,128]{1,0:T(8,128)S(1)} %get-tuple-element.78), channel_id=1, source_target_pairs={{0,3},{1,2},{2,1},{3,0},{4,7},{5,6},{6,5},{7,4},{8,11},{9,10},{10,... | collective-permute-start | bytes 442376 | tf_op jit(solution)/shard_map/ppermute | solution.py:438
  33.6 0.2 collective-permute-done.17.refs_8_
  33.9 1.5 %collective-permute-start.16 = (f32[288,128]{1,0:T(8,128)S(1)}, f32[288,128]{1,0:T(8,128)S(1)}, u32[]{:S(2)}, u32[]{:S(2)}) collective-permute-start(f32[288,128]{1,0:T(8,128)S(1)} %get-tuple-element.76), channel_id=1, source_target_pairs={{0,2},{1,3},{2,0},{3,1},{4,6},{5,7},{6,4},{7,5},{8,10},{9,11},{10,... | collective-permute-start | bytes 442376 | tf_op jit(solution)/shard_map/ppermute | solution.py:438
  35.4 0.4 collective-permute-start.19
  35.8 2.3 %collective-permute-done.15.refs_6_ = f32[288,128]{1,0:T(8,128)S(1)} collective-permute-done((f32[288,128]{1,0:T(8,128)S(1)}, f32[288,128]{1,0:T(8,128)S(1)}, u32[]{:S(2)}, u32[]{:S(2)}) %collective-permute-start.15) | collective-permute-done | bytes 147488 | tf_op jit(solution)/shard_map/ppermute | solution.py:438
  38.1 2.9 %collective-permute-done.18.refs_9_ = f32[288,128]{1,0:T(8,128)S(1)} collective-permute-done((f32[288,128]{1,0:T(8,128)S(1)}, f32[288,128]{1,0:T(8,128)S(1)}, u32[]{:S(2)}, u32[]{:S(2)}) %collective-permute-start.18) | collective-permute-done | bytes 147488 | tf_op jit(solution)/shard_map/ppermute | solution.py:438
  41.0 1.9 %collective-permute-start.23 = (f32[144,128]{1,0:T(8,128)S(1)}, f32[144,128]{1,0:T(8,128)S(1)}, u32[]{:S(2)}, u32[]{:S(2)}) collective-permute-start(f32[144,128]{1,0:T(8,128)S(1)} %get-tuple-element.84), channel_id=1, source_target_pairs={{0,2},{1,3},{2,0},{3,1},{4,6},{5,7},{6,4},{7,5},{8,10},{9,11},{10,... | collective-permute-start | bytes 221192 | tf_op jit(solution)/shard_map/ppermute | solution.py:438
  42.9 0.3 shard_map.87.refs_4_.refs_7_.refs_12_
  43.3 0.8 shard_map.88
  44.1 0.3 collective-permute-done.16.refs_7_
  44.4 2.9 %collective-permute-done.19.refs_10_ = f32[288,128]{1,0:T(8,128)S(1)} collective-permute-done((f32[288,128]{1,0:T(8,128)S(1)}, f32[288,128]{1,0:T(8,128)S(1)}, u32[]{:S(2)}, u32[]{:S(2)}) %collective-permute-start.19) | collective-permute-done | bytes 147488 | tf_op jit(solution)/shard_map/ppermute | solution.py:438
  47.4 0.8 shard_map.89
  48.2 1.0 collective-permute-done.23.refs_8_
  49.2 1.3 %collective-permute-done.24.refs_11_ = f32[144,128]{1,0:T(8,128)S(1)} collective-permute-done((f32[144,128]{1,0:T(8,128)S(1)}, f32[144,128]{1,0:T(8,128)S(1)}, u32[]{:S(2)}, u32[]{:S(2)}) %collective-permute-start.24) | collective-permute-done | bytes 73760 | tf_op jit(solution)/shard_map/ppermute | solution.py:438
  50.5 0.8 shard_map.90
  51.5 0.4 collective-permute-start.21
  51.9 1.4 %collective-permute-start.28 = (f32[144,128]{1,0:T(8,128)S(1)}, f32[144,128]{1,0:T(8,128)S(1)}, u32[]{:S(2)}, u32[]{:S(2)}) collective-permute-start(f32[144,128]{1,0:T(8,128)S(1)} %get-tuple-element.94), channel_id=1, source_target_pairs={{0,2},{1,3},{2,0},{3,1},{4,6},{5,7},{6,4},{7,5},{8,10},{9,11},{10,... | collective-permute-start | bytes 221192 | tf_op jit(solution)/shard_map/ppermute | solution.py:438
  53.4 1.3 %collective-permute-start.26 = (f32[144,128]{1,0:T(8,128)S(1)}, f32[144,128]{1,0:T(8,128)S(1)}, u32[]{:S(2)}, u32[]{:S(2)}) collective-permute-start(f32[144,128]{1,0:T(8,128)S(1)} %get-tuple-element.92), channel_id=1, source_target_pairs={{0,2},{1,3},{2,0},{3,1},{4,6},{5,7},{6,4},{7,5},{8,10},{9,11},{10,... | collective-permute-start | bytes 221192 | tf_op jit(solution)/shard_map/ppermute | solution.py:438
  54.7 1.6 %collective-permute-done.28.refs_6_ = f32[144,128]{1,0:T(8,128)S(1)} collective-permute-done((f32[144,128]{1,0:T(8,128)S(1)}, f32[144,128]{1,0:T(8,128)S(1)}, u32[]{:S(2)}, u32[]{:S(2)}) %collective-permute-start.28) | collective-permute-done | bytes 73760 | tf_op jit(solution)/shard_map/ppermute | solution.py:438
  56.3 1.6 %collective-permute-done.29.refs_7_ = f32[144,128]{1,0:T(8,128)S(1)} collective-permute-done((f32[144,128]{1,0:T(8,128)S(1)}, f32[144,128]{1,0:T(8,128)S(1)}, u32[]{:S(2)}, u32[]{:S(2)}) %collective-permute-start.29) | collective-permute-done | bytes 73760 | tf_op jit(solution)/shard_map/ppermute | solution.py:438
  57.8 0.7 collective-permute-start.30
  58.5 0.9 collective-permute-done.26.refs_4_
  59.4 0.4 collective-permute-start.31
  59.8 0.7 collective-permute-done.27.refs_5_
  60.5 2.1 %collective-permute-start.32 = (f32[288,128]{1,0:T(8,128)S(1)}, f32[288,128]{1,0:T(8,128)S(1)}, u32[]{:S(2)}, u32[]{:S(2)}) collective-permute-start(f32[288,128]{1,0:T(8,128)S(1)} %get-tuple-element.100), channel_id=1, source_target_pairs={{0,2},{1,3},{2,0},{3,1},{4,6},{5,7},{6,4},{7,5},{8,10},{9,11},{10,... | collective-permute-start | bytes 442376 | tf_op jit(solution)/shard_map/ppermute | solution.py:438
  62.7 1.0 shard_map.91
  63.7 1.5 %collective-permute-start.34 = (f32[576,128]{1,0:T(8,128)S(1)}, f32[576,128]{1,0:T(8,128)S(1)}, u32[]{:S(2)}, u32[]{:S(2)}) collective-permute-start(f32[576,128]{1,0:T(8,128)S(1)} %get-tuple-element.103), channel_id=1, source_target_pairs={{0,4},{4,0},{8,12},{12,8},{16,20},{20,16},{24,28},{28,24},{1,5},{5... | collective-permute-start | bytes 884744 | tf_op jit(solution)/shard_map/ppermute | solution.py:584
  65.2 0.9 collective-permute-start.10
  66.1 0.9 collective-permute-done.31.refs_5_
  67.0 1.1 %collective-permute-start.11 = (f32[432,128]{1,0:T(8,128)S(1)}, f32[432,128]{1,0:T(8,128)S(1)}, u32[]{:S(2)}, u32[]{:S(2)}) collective-permute-start(f32[432,128]{1,0:T(8,128)S(1)} %get-tuple-element.70), channel_id=1, source_target_pairs={{0,3},{1,2},{2,1},{3,0},{4,7},{5,6},{6,5},{7,4},{8,11},{9,10},{10,... | collective-permute-start | bytes 663560 | tf_op jit(solution)/shard_map/ppermute | solution.py:438
  68.1 2.8 %collective-permute-done.32.refs_4_ = f32[288,128]{1,0:T(8,128)S(1)} collective-permute-done((f32[288,128]{1,0:T(8,128)S(1)}, f32[288,128]{1,0:T(8,128)S(1)}, u32[]{:S(2)}, u32[]{:S(2)}) %collective-permute-start.32) | collective-permute-done | bytes 147488 | tf_op jit(solution)/shard_map/ppermute | solution.py:438
  70.9 1.0 collective-permute-start.33
  71.9 1.0 shard_map.92
  72.9 9.9 %collective-permute-done.33.refs_5_ = f32[288,128]{1,0:T(8,128)S(1)} collective-permute-done((f32[288,128]{1,0:T(8,128)S(1)}, f32[288,128]{1,0:T(8,128)S(1)}, u32[]{:S(2)}, u32[]{:S(2)}) %collective-permute-start.33) | collective-permute-done | bytes 147488 | tf_op jit(solution)/shard_map/ppermute | solution.py:438
  82.8 2.4 %collective-permute-start.35 = (f32[576,128]{1,0:T(8,128)S(1)}, f32[576,128]{1,0:T(8,128)S(1)}, u32[]{:S(2)}, u32[]{:S(2)}) collective-permute-start(f32[576,128]{1,0:T(8,128)S(1)} %get-tuple-element.104), channel_id=1, source_target_pairs={{0,24},{4,28},{8,0},{12,4},{16,8},{20,12},{24,16},{28,20},{1,25},{... | collective-permute-start | bytes 884744 | tf_op jit(solution)/shard_map/ppermute | solution.py:583
  85.2 1.0 shard_map.93
  86.2 1.6 %collective-permute-start.36 = (f32[576,128]{1,0:T(8,128)S(1)}, f32[576,128]{1,0:T(8,128)S(1)}, u32[]{:S(2)}, u32[]{:S(2)}) collective-permute-start(f32[576,128]{1,0:T(8,128)S(1)} %get-tuple-element.105), channel_id=1, source_target_pairs={{0,4},{4,0},{8,12},{12,8},{16,20},{20,16},{24,28},{28,24},{1,5},{5... | collective-permute-start | bytes 884744 | tf_op jit(solution)/shard_map/ppermute | solution.py:584
  87.8 0.6 collective-permute-start.38
  88.4 0.3 collective-permute-start.39
  88.7 4.0 %collective-permute-done.35.refs_11_ = f32[576,128]{1,0:T(8,128)S(1)} collective-permute-done((f32[576,128]{1,0:T(8,128)S(1)}, f32[576,128]{1,0:T(8,128)S(1)}, u32[]{:S(2)}, u32[]{:S(2)}) %collective-permute-start.35) | collective-permute-done | bytes 294944 | tf_op jit(solution)/shard_map/ppermute | solution.py:583
  92.7 3.5 %collective-permute-done.36.refs_12_ = f32[576,128]{1,0:T(8,128)S(1)} collective-permute-done((f32[576,128]{1,0:T(8,128)S(1)}, f32[576,128]{1,0:T(8,128)S(1)}, u32[]{:S(2)}, u32[]{:S(2)}) %collective-permute-start.36) | collective-permute-done | bytes 294944 | tf_op jit(solution)/shard_map/ppermute | solution.py:584
  96.2 2.8 %collective-permute-done.37.refs_13_ = f32[576,128]{1,0:T(8,128)S(1)} collective-permute-done((f32[576,128]{1,0:T(8,128)S(1)}, f32[576,128]{1,0:T(8,128)S(1)}, u32[]{:S(2)}, u32[]{:S(2)}) %collective-permute-start.37) | collective-permute-done | bytes 294944 | tf_op jit(solution)/shard_map/ppermute | solution.py:583
  99.0 2.2 %shard_map.94 = (f32[24,96,96]{2,1,0:T(8,128)}, f32[576,128]{1,0:T(8,128)S(1)}) custom-call(f32[432,128]{1,0:T(8,128)S(1)} %get-tuple-element.67.refs_15_.refs_0_, f32[432,128]{1,0:T(8,128)S(1)} %collective-permute-done.9.refs_1_, f32[432,128]{1,0:T(8,128)S(1)} %collective-permute-done.10.refs_2_, f32[432,128]{1,0:T(8,128)S(1)} %collective-permute-done.11.refs_3_, ...), custom_call_target="tpu_custom_call" | custom-call | tf_op jit(solution)/shard_map/pallas_call | solution.py:426
  101.4 3.2 %collective-permute-done.39.refs_2_ = f32[576,128]{1,0:T(8,128)S(1)} collective-permute-done((f32[576,128]{1,0:T(8,128)S(1)}, f32[576,128]{1,0:T(8,128)S(1)}, u32[]{:S(2)}, u32[]{:S(2)}) %collective-permute-start.39) | collective-permute-done | bytes 294944 | tf_op jit(solution)/shard_map/ppermute | solution.py:583
  104.5 0.9 shard_map.95
  (46 shorter events, 0.8 us)
Async XLA Ops:
  0.0 6.1 %copy-start = (bf16[256,256]{1,0:T(8,128)(2,1)S(1)}, bf16[256,256]{1,0:T(8,128)(2,1)}, u32[]{:S(2)}) copy-start(bf16[256,256]{1,0:T(8,128)(2,1)} %constant.14.clone.refs_1_.refs_3_.refs_17_.refs_15_.refs_14_) | copy-start | bytes 393220
  0.0 6.1 %copy-start.1 = (bf16[4,256,192]{2,1,0:T(8,128)(2,1)S(1)}, bf16[4,256,192]{2,1,0:T(8,128)(2,1)}, u32[]{:S(2)}) copy-start(bf16[4,256,192]{2,1,0:T(8,128)(2,1)} %constant.15.clone.refs_2_.refs_4_) | copy-start | bytes 1179652
  0.0 1.3 %copy-start.3 = (f32[1,24,96,96]{3,2,1,0:T(8,128)S(1)}, f32[1,24,96,96]{3,2,1,0:T(8,128)}, u32[]{:S(2)}) copy-start(f32[1,24,96,96]{3,2,1,0:T(8,128)} %param.8) | copy-start | bytes 2654212
  1.5 13.0 %collective-permute-start.8 = (f32[576,128]{1,0:T(8,128)S(1)}, f32[576,128]{1,0:T(8,128)S(1)}, u32[]{:S(2)}, u32[]{:S(2)}) collective-permute-start(f32[576,128]{1,0:T(8,128)S(1)} %shard_map.82.refs_3_.refs_0_.refs_8_.refs_6_.refs_7_), channel_id=1, source_target_pairs={{0,8},{4,12},{8,16},{12,20},{16,24},{20,28},{24,0},{28,4},{1,9},{5... | collective-permute-start | bytes 884744 | tf_op jit(solution)/shard_map/ppermute | solution.py:476
  4.6 11.6 %collective-permute-start.7 = (f32[576,128]{1,0:T(8,128)S(1)}, f32[576,128]{1,0:T(8,128)S(1)}, u32[]{:S(2)}, u32[]{:S(2)}) collective-permute-start(f32[576,128]{1,0:T(8,128)S(1)} %shard_map.82.refs_3_.refs_0_.refs_8_.refs_6_.refs_7_), channel_id=1, source_target_pairs={{0,4},{4,0},{8,12},{12,8},{16,20},{20,16},{24,28},{28,24},{1,5},{5... | collective-permute-start | bytes 884744 | tf_op jit(solution)/shard_map/ppermute | solution.py:475
  7.4 13.4 %collective-permute-start.6 = (f32[576,128]{1,0:T(8,128)S(1)}, f32[576,128]{1,0:T(8,128)S(1)}, u32[]{:S(2)}, u32[]{:S(2)}) collective-permute-start(f32[576,128]{1,0:T(8,128)S(1)} %get-tuple-element.63.refs_0_.refs_9_.refs_7_.refs_8_), channel_id=1, source_target_pairs={{0,8},{4,12},{8,16},{12,20},{16,24},{20,28},{24,0},{28,4},{1,9},{5... | collective-permute-start | bytes 884744 | tf_op jit(solution)/shard_map/ppermute | solution.py:476
  9.0 13.5 %collective-permute-start.5 = (f32[576,128]{1,0:T(8,128)S(1)}, f32[576,128]{1,0:T(8,128)S(1)}, u32[]{:S(2)}, u32[]{:S(2)}) collective-permute-start(f32[576,128]{1,0:T(8,128)S(1)} %get-tuple-element.63.refs_0_.refs_9_.refs_7_.refs_8_), channel_id=1, source_target_pairs={{0,4},{4,0},{8,12},{12,8},{16,20},{20,16},{24,28},{28,24},{1,5},{5... | collective-permute-start | bytes 884744 | tf_op jit(solution)/shard_map/ppermute | solution.py:475
  9.6 16.7 %collective-permute-start.4 = (f32[576,128]{1,0:T(8,128)S(1)}, f32[576,128]{1,0:T(8,128)S(1)}, u32[]{:S(2)}, u32[]{:S(2)}) collective-permute-start(f32[576,128]{1,0:T(8,128)S(1)} %get-tuple-element.62.refs_0_.refs_10_.refs_8_.refs_9_), channel_id=1, source_target_pairs={{0,8},{4,12},{8,16},{12,20},{16,24},{20,28},{24,0},{28,4},{1,9},{5... | collective-permute-start | bytes 884744 | tf_op jit(solution)/shard_map/ppermute | solution.py:476
  14.5 11.8 %collective-permute-start.3 = (f32[576,128]{1,0:T(8,128)S(1)}, f32[576,128]{1,0:T(8,128)S(1)}, u32[]{:S(2)}, u32[]{:S(2)}) collective-permute-start(f32[576,128]{1,0:T(8,128)S(1)} %get-tuple-element.62.refs_0_.refs_10_.refs_8_.refs_9_), channel_id=1, source_target_pairs={{0,4},{4,0},{8,12},{12,8},{16,20},{20,16},{24,28},{28,24},{1,5},{5... | collective-permute-start | bytes 884744 | tf_op jit(solution)/shard_map/ppermute | solution.py:475
  16.2 11.6 %collective-permute-start = (f32[432,128]{1,0:T(8,128)S(1)}, f32[432,128]{1,0:T(8,128)S(1)}, u32[]{:S(2)}, u32[]{:S(2)}) collective-permute-start(f32[432,128]{1,0:T(8,128)S(1)} %get-tuple-element.59), channel_id=1, source_target_pairs={{0,1},{1,0},{2,3},{3,2},{4,5},{5,4},{6,7},{7,6},{8,9},{9,8},{10,11... | collective-permute-start | bytes 663560 | tf_op jit(solution)/shard_map/ppermute | solution.py:438
  20.8 8.5 %collective-permute-start.1 = (f32[432,128]{1,0:T(8,128)S(1)}, f32[432,128]{1,0:T(8,128)S(1)}, u32[]{:S(2)}, u32[]{:S(2)}) collective-permute-start(f32[432,128]{1,0:T(8,128)S(1)} %get-tuple-element.60), channel_id=1, source_target_pairs={{0,2},{1,3},{2,0},{3,1},{4,6},{5,7},{6,4},{7,5},{8,10},{9,11},{10,... | collective-permute-start | bytes 663560 | tf_op jit(solution)/shard_map/ppermute | solution.py:438
  22.5 8.9 %collective-permute-start.2 = (f32[432,128]{1,0:T(8,128)S(1)}, f32[432,128]{1,0:T(8,128)S(1)}, u32[]{:S(2)}, u32[]{:S(2)}) collective-permute-start(f32[432,128]{1,0:T(8,128)S(1)} %get-tuple-element.61), channel_id=1, source_target_pairs={{0,3},{1,2},{2,1},{3,0},{4,7},{5,6},{6,5},{7,4},{8,11},{9,10},{10,... | collective-permute-start | bytes 663560 | tf_op jit(solution)/shard_map/ppermute | solution.py:438
  24.4 18.5 %copy-start.6 = (f32[4,24,128]{2,1,0:T(8,128)S(1)}, f32[4,24,128]{2,1,0:T(8,128)}, u32[]{:S(2)}) copy-start(f32[4,24,128]{2,1,0:T(8,128)} %constant.20.clone.refs_1_) | copy-start | bytes 147460
  24.4 18.5 %copy-start.7 = (f32[96,128]{1,0:T(8,128)S(1)}, f32[96,128]{1,0:T(8,128)}, u32[]{:S(2)}) copy-start(f32[96,128]{1,0:T(8,128)} %constant.19.clone.refs_0_) | copy-start | bytes 147460
  26.3 9.2 %collective-permute-start.12 = (f32[288,128]{1,0:T(8,128)S(1)}, f32[288,128]{1,0:T(8,128)S(1)}, u32[]{:S(2)}, u32[]{:S(2)}) collective-permute-start(f32[288,128]{1,0:T(8,128)S(1)} %get-tuple-element.72), channel_id=1, source_target_pairs={{0,1},{1,0},{2,3},{3,2},{4,5},{5,4},{6,7},{7,6},{8,9},{9,8},{10,11... | collective-permute-start | bytes 442376 | tf_op jit(solution)/shard_map/ppermute | solution.py:438
  26.3 17.0 %copy-start.4 = (bf16[4,192,192]{2,1,0:T(8,128)(2,1)S(1)}, bf16[4,192,192]{2,1,0:T(8,128)(2,1)}, u32[]{:S(2)}) copy-start(bf16[4,192,192]{2,1,0:T(8,128)(2,1)} %constant.18.clone.refs_6_.refs_14_) | copy-start | bytes 884740
  26.3 17.0 %copy-start.5 = (bf16[4,192,192]{2,1,0:T(8,128)(2,1)S(1)}, bf16[4,192,192]{2,1,0:T(8,128)(2,1)}, u32[]{:S(2)}) copy-start(bf16[4,192,192]{2,1,0:T(8,128)(2,1)} %constant.17.clone.refs_5_.refs_13_) | copy-start | bytes 884740
  27.2 4.6 %collective-permute-start.14 = (f32[144,128]{1,0:T(8,128)S(1)}, f32[144,128]{1,0:T(8,128)S(1)}, u32[]{:S(2)}, u32[]{:S(2)}) collective-permute-start(f32[144,128]{1,0:T(8,128)S(1)} %get-tuple-element.74), channel_id=1, source_target_pairs={{0,1},{1,0},{2,3},{3,2},{4,5},{5,4},{6,7},{7,6},{8,9},{9,8},{10,11... | collective-permute-start | bytes 221192 | tf_op jit(solution)/shard_map/ppermute | solution.py:438
  27.8 6.0 %collective-permute-start.17 = (f32[144,128]{1,0:T(8,128)S(1)}, f32[144,128]{1,0:T(8,128)S(1)}, u32[]{:S(2)}, u32[]{:S(2)}) collective-permute-start(f32[144,128]{1,0:T(8,128)S(1)} %get-tuple-element.77), channel_id=1, source_target_pairs={{0,2},{1,3},{2,0},{3,1},{4,6},{5,7},{6,4},{7,5},{8,10},{9,11},{10,... | collective-permute-start | bytes 221192 | tf_op jit(solution)/shard_map/ppermute | solution.py:438
  29.3 4.6 %collective-permute-start.20 = (f32[144,128]{1,0:T(8,128)S(1)}, f32[144,128]{1,0:T(8,128)S(1)}, u32[]{:S(2)}, u32[]{:S(2)}) collective-permute-start(f32[144,128]{1,0:T(8,128)S(1)} %get-tuple-element.80), channel_id=1, source_target_pairs={{0,3},{1,2},{2,1},{3,0},{4,7},{5,6},{6,5},{7,4},{8,11},{9,10},{10,... | collective-permute-start | bytes 221192 | tf_op jit(solution)/shard_map/ppermute | solution.py:438
  31.4 6.7 %collective-permute-start.15 = (f32[288,128]{1,0:T(8,128)S(1)}, f32[288,128]{1,0:T(8,128)S(1)}, u32[]{:S(2)}, u32[]{:S(2)}) collective-permute-start(f32[288,128]{1,0:T(8,128)S(1)} %get-tuple-element.75), channel_id=1, source_target_pairs={{0,2},{1,3},{2,0},{3,1},{4,6},{5,7},{6,4},{7,5},{8,10},{9,11},{10,... | collective-permute-start | bytes 442376 | tf_op jit(solution)/shard_map/ppermute | solution.py:438
  31.8 9.2 %collective-permute-start.18 = (f32[288,128]{1,0:T(8,128)S(1)}, f32[288,128]{1,0:T(8,128)S(1)}, u32[]{:S(2)}, u32[]{:S(2)}) collective-permute-start(f32[288,128]{1,0:T(8,128)S(1)} %get-tuple-element.78), channel_id=1, source_target_pairs={{0,3},{1,2},{2,1},{3,0},{4,7},{5,6},{6,5},{7,4},{8,11},{9,10},{10,... | collective-permute-start | bytes 442376 | tf_op jit(solution)/shard_map/ppermute | solution.py:438
  33.8 9.1 %collective-permute-start.13 = (f32[288,128]{1,0:T(8,128)S(1)}, f32[288,128]{1,0:T(8,128)S(1)}, u32[]{:S(2)}, u32[]{:S(2)}) collective-permute-start(f32[288,128]{1,0:T(8,128)S(1)} %get-tuple-element.73), channel_id=1, source_target_pairs={{0,1},{1,0},{2,3},{3,2},{4,5},{5,4},{6,7},{7,6},{8,9},{9,8},{10,11... | collective-permute-start | bytes 442376 | tf_op jit(solution)/shard_map/ppermute | solution.py:438
  33.9 10.6 %collective-permute-start.16 = (f32[288,128]{1,0:T(8,128)S(1)}, f32[288,128]{1,0:T(8,128)S(1)}, u32[]{:S(2)}, u32[]{:S(2)}) collective-permute-start(f32[288,128]{1,0:T(8,128)S(1)} %get-tuple-element.76), channel_id=1, source_target_pairs={{0,2},{1,3},{2,0},{3,1},{4,6},{5,7},{6,4},{7,5},{8,10},{9,11},{10,... | collective-permute-start | bytes 442376 | tf_op jit(solution)/shard_map/ppermute | solution.py:438
  35.4 11.9 %collective-permute-start.19 = (f32[288,128]{1,0:T(8,128)S(1)}, f32[288,128]{1,0:T(8,128)S(1)}, u32[]{:S(2)}, u32[]{:S(2)}) collective-permute-start(f32[288,128]{1,0:T(8,128)S(1)} %get-tuple-element.79), channel_id=1, source_target_pairs={{0,3},{1,2},{2,1},{3,0},{4,7},{5,6},{6,5},{7,4},{8,11},{9,10},{10,... | collective-permute-start | bytes 442376 | tf_op jit(solution)/shard_map/ppermute | solution.py:438
  38.1 10.1 %collective-permute-start.22 = (f32[144,128]{1,0:T(8,128)S(1)}, f32[144,128]{1,0:T(8,128)S(1)}, u32[]{:S(2)}, u32[]{:S(2)}) collective-permute-start(f32[144,128]{1,0:T(8,128)S(1)} %get-tuple-element.83), channel_id=1, source_target_pairs={{0,1},{1,0},{2,3},{3,2},{4,5},{5,4},{6,7},{7,6},{8,9},{9,8},{10,11... | collective-permute-start | bytes 221192 | tf_op jit(solution)/shard_map/ppermute | solution.py:438
  41.0 8.1 %collective-permute-start.23 = (f32[144,128]{1,0:T(8,128)S(1)}, f32[144,128]{1,0:T(8,128)S(1)}, u32[]{:S(2)}, u32[]{:S(2)}) collective-permute-start(f32[144,128]{1,0:T(8,128)S(1)} %get-tuple-element.84), channel_id=1, source_target_pairs={{0,2},{1,3},{2,0},{3,1},{4,6},{5,7},{6,4},{7,5},{8,10},{9,11},{10,... | collective-permute-start | bytes 221192 | tf_op jit(solution)/shard_map/ppermute | solution.py:438
  42.9 7.6 %collective-permute-start.24 = (f32[144,128]{1,0:T(8,128)S(1)}, f32[144,128]{1,0:T(8,128)S(1)}, u32[]{:S(2)}, u32[]{:S(2)}) collective-permute-start(f32[144,128]{1,0:T(8,128)S(1)} %get-tuple-element.85), channel_id=1, source_target_pairs={{0,3},{1,2},{2,1},{3,0},{4,7},{5,6},{6,5},{7,4},{8,11},{9,10},{10,... | collective-permute-start | bytes 221192 | tf_op jit(solution)/shard_map/ppermute | solution.py:438
  50.5 12.2 %copy-start.2 = (bf16[4,192,256]{2,1,0:T(8,128)(2,1)S(1)}, bf16[4,192,256]{2,1,0:T(8,128)(2,1)}, u32[]{:S(2)}) copy-start(bf16[4,192,256]{2,1,0:T(8,128)(2,1)} %constant.16.clone.refs_18_.refs_16_.refs_15_) | copy-start | bytes 1179652
  51.3 11.4 %collective-permute-start.25 = (f32[432,128]{1,0:T(8,128)S(1)}, f32[432,128]{1,0:T(8,128)S(1)}, u32[]{:S(2)}, u32[]{:S(2)}) collective-permute-start(f32[432,128]{1,0:T(8,128)S(1)} %get-tuple-element.91), channel_id=1, source_target_pairs={{0,1},{1,0},{2,3},{3,2},{4,5},{5,4},{6,7},{7,6},{8,9},{9,8},{10,11... | collective-permute-start | bytes 663560 | tf_op jit(solution)/shard_map/ppermute | solution.py:438
  51.5 11.2 %collective-permute-start.21 = (f32[432,128]{1,0:T(8,128)S(1)}, f32[432,128]{1,0:T(8,128)S(1)}, u32[]{:S(2)}, u32[]{:S(2)}) collective-permute-start(f32[432,128]{1,0:T(8,128)S(1)} %get-tuple-element.82), channel_id=1, source_target_pairs={{0,1},{1,0},{2,3},{3,2},{4,5},{5,4},{6,7},{7,6},{8,9},{9,8},{10,11... | collective-permute-start | bytes 663560 | tf_op jit(solution)/shard_map/ppermute | solution.py:438
  51.9 4.4 %collective-permute-start.28 = (f32[144,128]{1,0:T(8,128)S(1)}, f32[144,128]{1,0:T(8,128)S(1)}, u32[]{:S(2)}, u32[]{:S(2)}) collective-permute-start(f32[144,128]{1,0:T(8,128)S(1)} %get-tuple-element.94), channel_id=1, source_target_pairs={{0,2},{1,3},{2,0},{3,1},{4,6},{5,7},{6,4},{7,5},{8,10},{9,11},{10,... | collective-permute-start | bytes 221192 | tf_op jit(solution)/shard_map/ppermute | solution.py:438
  53.3 4.6 %collective-permute-start.29 = (f32[144,128]{1,0:T(8,128)S(1)}, f32[144,128]{1,0:T(8,128)S(1)}, u32[]{:S(2)}, u32[]{:S(2)}) collective-permute-start(f32[144,128]{1,0:T(8,128)S(1)} %get-tuple-element.95), channel_id=1, source_target_pairs={{0,3},{1,2},{2,1},{3,0},{4,7},{5,6},{6,5},{7,4},{8,11},{9,10},{10,... | collective-permute-start | bytes 221192 | tf_op jit(solution)/shard_map/ppermute | solution.py:438
  53.4 6.0 %collective-permute-start.26 = (f32[144,128]{1,0:T(8,128)S(1)}, f32[144,128]{1,0:T(8,128)S(1)}, u32[]{:S(2)}, u32[]{:S(2)}) collective-permute-start(f32[144,128]{1,0:T(8,128)S(1)} %get-tuple-element.92), channel_id=1, source_target_pairs={{0,2},{1,3},{2,0},{3,1},{4,6},{5,7},{6,4},{7,5},{8,10},{9,11},{10,... | collective-permute-start | bytes 221192 | tf_op jit(solution)/shard_map/ppermute | solution.py:438
  56.3 4.3 %collective-permute-start.27 = (f32[144,128]{1,0:T(8,128)S(1)}, f32[144,128]{1,0:T(8,128)S(1)}, u32[]{:S(2)}, u32[]{:S(2)}) collective-permute-start(f32[144,128]{1,0:T(8,128)S(1)} %get-tuple-element.93), channel_id=1, source_target_pairs={{0,3},{1,2},{2,1},{3,0},{4,7},{5,6},{6,5},{7,4},{8,11},{9,10},{10,... | collective-permute-start | bytes 221192 | tf_op jit(solution)/shard_map/ppermute | solution.py:438
  57.8 7.4 %collective-permute-start.30 = (f32[288,128]{1,0:T(8,128)S(1)}, f32[288,128]{1,0:T(8,128)S(1)}, u32[]{:S(2)}, u32[]{:S(2)}) collective-permute-start(f32[288,128]{1,0:T(8,128)S(1)} %get-tuple-element.97), channel_id=1, source_target_pairs={{0,2},{1,3},{2,0},{3,1},{4,6},{5,7},{6,4},{7,5},{8,10},{9,11},{10,... | collective-permute-start | bytes 442376 | tf_op jit(solution)/shard_map/ppermute | solution.py:438
  59.4 7.6 %collective-permute-start.31 = (f32[288,128]{1,0:T(8,128)S(1)}, f32[288,128]{1,0:T(8,128)S(1)}, u32[]{:S(2)}, u32[]{:S(2)}) collective-permute-start(f32[288,128]{1,0:T(8,128)S(1)} %get-tuple-element.98), channel_id=1, source_target_pairs={{0,3},{1,2},{2,1},{3,0},{4,7},{5,6},{6,5},{7,4},{8,11},{9,10},{10,... | collective-permute-start | bytes 442376 | tf_op jit(solution)/shard_map/ppermute | solution.py:438
  60.5 10.3 %collective-permute-start.32 = (f32[288,128]{1,0:T(8,128)S(1)}, f32[288,128]{1,0:T(8,128)S(1)}, u32[]{:S(2)}, u32[]{:S(2)}) collective-permute-start(f32[288,128]{1,0:T(8,128)S(1)} %get-tuple-element.100), channel_id=1, source_target_pairs={{0,2},{1,3},{2,0},{3,1},{4,6},{5,7},{6,4},{7,5},{8,10},{9,11},{10,... | collective-permute-start | bytes 442376 | tf_op jit(solution)/shard_map/ppermute | solution.py:438
  63.7 24.7 %collective-permute-start.34 = (f32[576,128]{1,0:T(8,128)S(1)}, f32[576,128]{1,0:T(8,128)S(1)}, u32[]{:S(2)}, u32[]{:S(2)}) collective-permute-start(f32[576,128]{1,0:T(8,128)S(1)} %get-tuple-element.103), channel_id=1, source_target_pairs={{0,4},{4,0},{8,12},{12,8},{16,20},{20,16},{24,28},{28,24},{1,5},{5... | collective-permute-start | bytes 884744 | tf_op jit(solution)/shard_map/ppermute | solution.py:584
  65.2 21.0 %collective-permute-start.9 = (f32[432,128]{1,0:T(8,128)S(1)}, f32[432,128]{1,0:T(8,128)S(1)}, u32[]{:S(2)}, u32[]{:S(2)}) collective-permute-start(f32[432,128]{1,0:T(8,128)S(1)} %get-tuple-element.68), channel_id=1, source_target_pairs={{0,1},{1,0},{2,3},{3,2},{4,5},{5,4},{6,7},{7,6},{8,9},{9,8},{10,11... | collective-permute-start | bytes 663560 | tf_op jit(solution)/shard_map/ppermute | solution.py:438
  65.2 22.6 %collective-permute-start.10 = (f32[432,128]{1,0:T(8,128)S(1)}, f32[432,128]{1,0:T(8,128)S(1)}, u32[]{:S(2)}, u32[]{:S(2)}) collective-permute-start(f32[432,128]{1,0:T(8,128)S(1)} %get-tuple-element.69), channel_id=1, source_target_pairs={{0,2},{1,3},{2,0},{3,1},{4,6},{5,7},{6,4},{7,5},{8,10},{9,11},{10,... | collective-permute-start | bytes 663560 | tf_op jit(solution)/shard_map/ppermute | solution.py:438
  67.0 20.8 %collective-permute-start.11 = (f32[432,128]{1,0:T(8,128)S(1)}, f32[432,128]{1,0:T(8,128)S(1)}, u32[]{:S(2)}, u32[]{:S(2)}) collective-permute-start(f32[432,128]{1,0:T(8,128)S(1)} %get-tuple-element.70), channel_id=1, source_target_pairs={{0,3},{1,2},{2,1},{3,0},{4,7},{5,6},{6,5},{7,4},{8,11},{9,10},{10,... | collective-permute-start | bytes 663560 | tf_op jit(solution)/shard_map/ppermute | solution.py:438
  70.9 11.9 %collective-permute-start.33 = (f32[288,128]{1,0:T(8,128)S(1)}, f32[288,128]{1,0:T(8,128)S(1)}, u32[]{:S(2)}, u32[]{:S(2)}) collective-permute-start(f32[288,128]{1,0:T(8,128)S(1)} %get-tuple-element.101), channel_id=1, source_target_pairs={{0,3},{1,2},{2,1},{3,0},{4,7},{5,6},{6,5},{7,4},{8,11},{9,10},{10,... | collective-permute-start | bytes 442376 | tf_op jit(solution)/shard_map/ppermute | solution.py:438
  82.8 9.9 %collective-permute-start.35 = (f32[576,128]{1,0:T(8,128)S(1)}, f32[576,128]{1,0:T(8,128)S(1)}, u32[]{:S(2)}, u32[]{:S(2)}) collective-permute-start(f32[576,128]{1,0:T(8,128)S(1)} %get-tuple-element.104), channel_id=1, source_target_pairs={{0,24},{4,28},{8,0},{12,4},{16,8},{20,12},{24,16},{28,20},{1,25},{... | collective-permute-start | bytes 884744 | tf_op jit(solution)/shard_map/ppermute | solution.py:583
  86.2 9.9 %collective-permute-start.36 = (f32[576,128]{1,0:T(8,128)S(1)}, f32[576,128]{1,0:T(8,128)S(1)}, u32[]{:S(2)}, u32[]{:S(2)}) collective-permute-start(f32[576,128]{1,0:T(8,128)S(1)} %get-tuple-element.105), channel_id=1, source_target_pairs={{0,4},{4,0},{8,12},{12,8},{16,20},{20,16},{24,28},{28,24},{1,5},{5... | collective-permute-start | bytes 884744 | tf_op jit(solution)/shard_map/ppermute | solution.py:584
  87.8 11.2 %collective-permute-start.37 = (f32[576,128]{1,0:T(8,128)S(1)}, f32[576,128]{1,0:T(8,128)S(1)}, u32[]{:S(2)}, u32[]{:S(2)}) collective-permute-start(f32[576,128]{1,0:T(8,128)S(1)} %get-tuple-element.106), channel_id=1, source_target_pairs={{0,24},{4,28},{8,0},{12,4},{16,8},{20,12},{24,16},{28,20},{1,25},{... | collective-permute-start | bytes 884744 | tf_op jit(solution)/shard_map/ppermute | solution.py:583
  87.8 13.5 %collective-permute-start.38 = (f32[576,128]{1,0:T(8,128)S(1)}, f32[576,128]{1,0:T(8,128)S(1)}, u32[]{:S(2)}, u32[]{:S(2)}) collective-permute-start(f32[576,128]{1,0:T(8,128)S(1)} %get-tuple-element.108), channel_id=1, source_target_pairs={{0,4},{4,0},{8,12},{12,8},{16,20},{20,16},{24,28},{28,24},{1,5},{5... | collective-permute-start | bytes 884744 | tf_op jit(solution)/shard_map/ppermute | solution.py:584
  88.4 16.1 %collective-permute-start.39 = (f32[576,128]{1,0:T(8,128)S(1)}, f32[576,128]{1,0:T(8,128)S(1)}, u32[]{:S(2)}, u32[]{:S(2)}) collective-permute-start(f32[576,128]{1,0:T(8,128)S(1)} %get-tuple-element.109), channel_id=1, source_target_pairs={{0,24},{4,28},{8,0},{12,4},{16,8},{20,12},{24,16},{28,20},{1,25},{... | collective-permute-start | bytes 884744 | tf_op jit(solution)/shard_map/ppermute | solution.py:583
